TPU v7x, 128 devices: a whole 4x4x4 slice. The times are simulated.
128 devices in a mesh: gy: 16 (over z, x), gz: 8 (over y, core).
Axes of the slice: x: 4, y: 4, z: 4, core: 2. Of those that a mesh axis runs over, the one named last changes fastest.
Arguments:
- fraction: float32 [128, 128, 1024], P('gz', 'gy'), may hold values from 0 to 1
- velocity_x: float32 [128, 128, 1024], P('gz', 'gy'), may hold values from -9 to 9
- velocity_y: float32 [128, 128, 1024], P('gz', 'gy'), may hold values from -9 to 9
- velocity_z: float32 [128, 128, 1024], P('gz', 'gy'), may hold values from -9 to 9
Outputs:
- advected: float32 [128, 128, 1024], P('gz', 'gy')
- time_step: float32 [], replicated
All inputs are finite; a program needn't handle non-finite values. Where the computation divides by a largest or mean magnitude, that divisor is 1e-20 or more.
Results may differ from a plain program's by a relative error of at most 0.0003.
Values sent between devices are 32-bit elements; how exact they have to be, the bound alone decides.
A program may use at most 64 MiB of HBM per device.

v0:
```python
import jax
import jax.numpy as jnp
from jax import lax
from jax.sharding import Mesh
from jax.sharding import PartitionSpec as P

NEWTON = 5
GY_GZ = ("gy_0", "gy_1", "gz_0", "gz_1")
GY = ("gy_0", "gy_1")
GZ = ("gz_0", "gz_1")


tilt_floor = 0.1
courant = 0.45
epsilon = 1e-06


def extended(block, sides, width):
    for axis, dim in sides:
        count = lax.axis_size(axis)
        forward = [(i, i + 1) for i in range(count - 1)]
        forward.append((count - 1, 0))
        backward = [(target, source) for source, target in forward]
        low = lax.ppermute(
            lax.slice_in_dim(block, block.shape[dim] - width, None, axis=dim), axis, forward
        )
        high = lax.ppermute(lax.slice_in_dim(block, 0, width, axis=dim), axis, backward)
        block = jnp.concatenate([low, block, high], axis=dim)
    return block


def shifted(value, axis, steps):
    count = lax.axis_size(axis)
    pairs = [(source, (source + steps) % count) for source in range(count)]
    return lax.ppermute(value, axis, pairs)


def combined_by_axis(value, axes, combine):
    for axis in axes:
        pieces = jax.tree.map(lambda part: lax.all_gather(part, axis), value)
        value = jax.tree.map(lambda part: part[0], pieces)
        for k in range(1, lax.axis_size(axis)):
            value = combine(value, jax.tree.map(lambda part: part[k], pieces))
    return value


def cube_step(reach, height):
    safe = jnp.where(height > 0, height, 1.0)
    whole = 3.0 * reach * reach - 3.0 * reach * height + height * height
    partial_part = reach * reach * reach / safe
    return jnp.where(reach - height >= 0, whole, jnp.where(reach >= 0, partial_part, 0.0))


def cube_rate(reach, height):
    safe = jnp.where(height > 0, height, 1.0)
    whole = 6.0 * reach - 3.0 * height
    partial_part = 3.0 * reach * reach / safe
    return jnp.where(reach - height >= 0, whole, jnp.where(reach >= 0, partial_part, 0.0))


def region_volume(offset, tilt_a, tilt_b, height, extent):
    combo = (
        cube_step(offset, height)
        - cube_step(offset - tilt_a, height)
        - cube_step(offset - tilt_b, height)
        + cube_step(offset - tilt_a - tilt_b, height)
    )
    return extent * combo / (6.0 * tilt_a * tilt_b)


def section_area(offset, tilt_a, tilt_b, height):
    combo = (
        cube_rate(offset, height)
        - cube_rate(offset - tilt_a, height)
        - cube_rate(offset - tilt_b, height)
        + cube_rate(offset - tilt_a - tilt_b, height)
    )
    return combo / (6.0 * tilt_a * tilt_b)


def youngs_slope(padded):

    def smooth_zero(arr):
        return arr[:-2] + 2.0 * arr[1:-1] + arr[2:]

    def smooth_one(arr):
        return arr[:, :-2] + 2.0 * arr[:, 1:-1] + arr[:, 2:]

    def smooth_cells(arr):
        return jnp.roll(arr, 1, 2) + 2.0 * arr + jnp.roll(arr, -1, 2)

    diff_zero = padded[2:] - padded[:-2]
    diff_one = padded[:, 2:] - padded[:, :-2]
    diff_cells = jnp.roll(padded, -1, 2) - jnp.roll(padded, 1, 2)
    grad_zero = smooth_cells(smooth_one(diff_zero)) / 32.0
    grad_one = smooth_cells(smooth_zero(diff_one)) / 32.0
    grad_cells = smooth_one(smooth_zero(diff_cells)) / 32.0
    return (grad_zero, grad_one, grad_cells)


def plane_for(fraction, slopes, axis_dim):
    slope_d = slopes[axis_dim]
    across = [slopes[index] for index in range(3) if index != axis_dim]
    tilt_d = jnp.abs(slope_d)
    tilt_a = jnp.abs(across[0]) + tilt_floor
    tilt_b = jnp.abs(across[1]) + tilt_floor
    volume = jnp.clip(fraction, 0.0, 1.0)
    lesser = jnp.minimum(volume, 1.0 - volume)
    summed = tilt_a + tilt_b + tilt_d
    offset = 0.5 * summed
    for repeat in range(NEWTON):
        offset = offset - (
            region_volume(offset, tilt_a, tilt_b, tilt_d, 1.0) - lesser
        ) / section_area(offset, tilt_a, tilt_b, tilt_d)
    offset = jnp.where(volume > 0.5, summed - offset, offset)
    return (offset, tilt_a, tilt_b, tilt_d, slope_d > 0)


def outflow(planes, width, upward):
    offset, tilt_a, tilt_b, tilt_d, mirrored = planes
    if upward:
        start_at = jnp.where(mirrored, 0.0, 1.0 - width)
    else:
        start_at = jnp.where(mirrored, 1.0 - width, 0.0)
    return region_volume(offset - tilt_d * start_at, tilt_a, tilt_b, tilt_d * width, width)


def take_rows(arr, first_row, limit_row, axis_dim):
    return lax.slice_in_dim(arr, first_row, limit_row, axis=axis_dim)


def combine_stats(former, latter):
    return (jnp.maximum(former[0], latter[0]), former[1] + latter[1])


def sweep_cells(fraction, velocity, time_step):
    padded = extended(fraction, ((GY, 1), (GZ, 0)), 1)
    planes = plane_for(fraction, youngs_slope(padded), 2)
    velocity_low = jnp.roll(velocity, 1, 2)
    out_upper = outflow(planes, jnp.maximum(time_step * velocity, 0.0), True)
    out_lower = outflow(planes, jnp.maximum(-time_step * velocity_low, 0.0), False)
    from_below = jnp.roll(out_upper, 1, 2)
    from_above = jnp.roll(out_lower, -1, 2)
    divisor = 1.0 - time_step * velocity + time_step * velocity_low
    return (fraction - out_upper - out_lower + from_below + from_above) / divisor


def pass_rows(upper_row, lower_row, axis_dim):
    if axis_dim == 1:
        from_below = shifted(upper_row, GY, 1)
        from_above = shifted(lower_row, GY, -1)
    else:
        from_below = shifted(upper_row, GZ, 1)
        from_above = shifted(lower_row, GZ, -1)
    return (from_below, from_above)


def sweep_outflow(fraction, velocity, lower_row, axis_dim, time_step):
    padded = extended(fraction, ((GY, 1), (GZ, 0)), 1)
    planes = plane_for(fraction, youngs_slope(padded), axis_dim)
    cells_d = velocity.shape[axis_dim]
    velocity_low = jnp.concatenate(
        [lower_row, take_rows(velocity, 0, cells_d - 1, axis_dim)], axis=axis_dim
    )
    out_upper = outflow(planes, jnp.maximum(time_step * velocity, 0.0), True)
    out_lower = outflow(planes, jnp.maximum(-time_step * velocity_low, 0.0), False)
    edge_below, edge_above = pass_rows(
        take_rows(out_upper, cells_d - 1, cells_d, axis_dim),
        take_rows(out_lower, 0, 1, axis_dim),
        axis_dim,
    )
    from_below = jnp.concatenate(
        [edge_below, take_rows(out_upper, 0, cells_d - 1, axis_dim)], axis=axis_dim
    )
    from_above = jnp.concatenate(
        [take_rows(out_lower, 1, cells_d, axis_dim), edge_above], axis=axis_dim
    )
    divisor = 1.0 - time_step * velocity + time_step * velocity_low
    return (fraction - out_upper - out_lower + from_below + from_above) / divisor


def shards(fraction, velocity_x, velocity_y, velocity_z):
    cells_all = float(fraction.size * lax.axis_size(GY) * lax.axis_size(GZ))
    local_peak = jnp.maximum(
        jnp.maximum(jnp.max(jnp.abs(velocity_x)), jnp.max(jnp.abs(velocity_y))),
        jnp.max(jnp.abs(velocity_z)),
    )
    local_share = jnp.sum(4.0 * fraction * (1.0 - fraction))
    umax, share_sum = combined_by_axis((local_peak, local_share), GY_GZ, combine_stats)
    time_step = courant / ((umax + epsilon) * (1.0 + share_sum / cells_all))
    rows_y = velocity_y.shape[1]
    planes_z = velocity_z.shape[0]
    lower_y = shifted(take_rows(velocity_y, rows_y - 1, rows_y, 1), GY, 1)
    lower_z = shifted(take_rows(velocity_z, planes_z - 1, planes_z, 0), GZ, 1)
    field = sweep_cells(fraction, velocity_x, time_step)
    field = sweep_outflow(field, velocity_y, lower_y, 1, time_step)
    field = sweep_outflow(field, velocity_z, lower_z, 0, time_step)
    return (field, time_step)


def solution(mesh):
    split = Mesh(mesh.devices.reshape(4, 4, 4, 2), ("gy_0", "gy_1", "gz_0", "gz_1"))
    placed = (P(GZ, GY, None), P(GZ, GY, None), P(GZ, GY, None), P(GZ, GY, None))
    return jax.shard_map(
        shards, mesh=split, in_specs=placed, out_specs=(P(GZ, GY, None), P()), check_vma=False
    )
```

profile of v0, /device:TPU:1, one launch (start us, length us, event | category | flops | bytes accessed | tf_op | source)
XLA Modules:
  0.0 146.5 jit_solution(2994722266037057236)
XLA Ops:
  0.7 1.4 fusion.863
  2.1 2.1 %collective-permute-start = (f32[16,1,1024]{2,1,0:T(1,128)S(1)}, f32[16,1,1024]{2,1,0:T(1,128)S(1)}, u32[]{:S(2)}, u32[]{:S(2)}) collective-permute-start(f32[16,1,1024]{2,1,0:T(1,128)S(1)} %get-tuple-element.65), channel_id=1, source_target_pairs={{0,8},{8,16},{16,24},{24,32},{32,40},{40,48},{48,56},{56,64},{64,7... | collective-permute-start | bytes 196616 | tf_op jit(solution)/shard_map/ppermute | solution.py:24
  4.2 4.8 %collective-permute-start.1 = (f32[16,1,1024]{2,1,0:T(1,128)S(1)}, f32[16,1,1024]{2,1,0:T(1,128)S(1)}, u32[]{:S(2)}, u32[]{:S(2)}) collective-permute-start(f32[16,1,1024]{2,1,0:T(1,128)S(1)} %get-tuple-element.66), channel_id=1, source_target_pairs={{8,0},{16,8},{24,16},{32,24},{40,32},{48,40},{56,48},{64,56},{72,6... | collective-permute-start | bytes 196616 | tf_op jit(solution)/shard_map/ppermute | solution.py:27
  9.0 1.8 %multiply_reduce_fusion = f32[]{:T(128)} fusion(f32[16,8,1024]{2,1,0:T(8,128)} %param.4), kind=kLoop, calls=%fused_computation.1320 | loop fusion | flops 524287 | bytes 524292 | tf_op jit(solution)/shard_map/reduce_sum | solution.py:188
  10.9 1.7 %abs_reduce_fusion.1 = f32[]{:T(128)} fusion(f32[16,8,1024]{2,1,0:T(8,128)} %param.6), kind=kLoop, calls=%fused_computation.1322 | loop fusion | flops 262143 | bytes 524292 | tf_op jit(solution)/shard_map/reduce_max | solution.py:185
  12.5 0.6 abs_reduce_fusion.2
  13.2 0.7 abs_reduce_fusion
  13.9 0.6 dynamic-slice
  16.5 0.7 dynamic-update-slice
  17.2 1.4 dynamic-update-slice.4
  18.6 0.6 dynamic-slice.1
  19.2 7.3 %all-reduce.10 = (f32[4]{0:T(128)S(1)}, f32[4]{0:T(128)S(1)}) all-reduce(f32[4]{0:T(128)S(1)} %dynamic-update-slice, f32[4]{0:T(128)S(1)} %dynamic-update-slice.4), channel_id=1, replica_groups=mesh['gy_0'=4,'gy_1'=4,'gz_0'=4,'gz_1'=2] {'gy_0'}, use_global_device_ids=true, to_apply=%add | all-reduce | flops 8 | bytes 64
  26.4 0.8 add_dynamic-update-slice_fusion.2
  27.3 0.8 maximum_dynamic-update-slice_fusion.2
  28.1 0.6 dynamic-slice.2
  28.7 6.3 %all-reduce.9 = (f32[4]{0:T(128)S(1)}, f32[4]{0:T(128)S(1)}) all-reduce(f32[4]{0:T(128)S(1)} %maximum_dynamic-update-slice_fusion.2, f32[4]{0:T(128)S(1)} %add_dynamic-update-slice_fusion.2), channel_id=1, replica_groups=mesh['gy_0'=4,'gy_1'=4,'gz_0'=4,'gz_1'=2] {'gy_1'}, use_global_device_ids=true, to_apply=%add.1 | all-reduce | flops 8 | bytes 64
  35.0 0.8 add_dynamic-update-slice_fusion.1
  35.8 0.8 maximum_dynamic-update-slice_fusion.1
  36.6 0.6 dynamic-slice.3
  37.2 8.7 %all-reduce.8 = (f32[4]{0:T(128)S(1)}, f32[4]{0:T(128)S(1)}) all-reduce(f32[4]{0:T(128)S(1)} %maximum_dynamic-update-slice_fusion.1, f32[4]{0:T(128)S(1)} %add_dynamic-update-slice_fusion.1), channel_id=1, replica_groups=mesh['gy_0'=4,'gy_1'=4,'gz_0'=4,'gz_1'=2] {'gz_0'}, use_global_device_ids=true, to_apply=%add.2 | all-reduce | flops 8 | bytes 64
  45.9 0.8 add_dynamic-update-slice_fusion
  46.7 0.8 maximum_dynamic-update-slice_fusion
  47.5 9.4 %all-reduce.11 = (f32[2]{0:T(128)S(1)}, f32[2]{0:T(128)S(1)}) all-reduce(f32[2]{0:T(128)S(1)} %maximum_dynamic-update-slice_fusion, f32[2]{0:T(128)S(1)} %add_dynamic-update-slice_fusion), channel_id=1, replica_groups=mesh['gy_0'=4,'gy_1'=4,'gz_0'=4,'gz_1'=2] {'gz_1'}, use_global_device_ids=true, to_apply=%add.3 | all-reduce | flops 4 | bytes 32
  57.3 1.4 collective-permute-start.3
  58.7 0.6 fusion.864
  64.4 11.0 %fusion.133 = (f32[16,8,1024]{2,1,0:T(8,128)S(1)}, f32[16,8,1024]{2,1,0:T(8,128)S(1)}, f32[16,8,1024]{2,1,0:T(8,128)S(1)}, f32[16,8,1024]{2,1,0:T(8,128)S(1)}, f32[16,8,1024]{2,1,0:T(8,128)S(1)}) fusion(f32[16,8,1023]{2,1,0:T(8,128)S(1)} %bitcast.11, f32[16,8,1]{2,1,0:T(8,128)S(1)} %slice.500, f32[]{:T(128)S(6)} %neg.2, f32[16,8,1024]{2,1,0:T(8,128)S(1)} %copy-done, ...), kind=kLoop, calls=%fused_computation.450 | loop fusion | flops 71303168 | bytes 10485764 | tf_op jit(solution)/shard_map/div | solution.py:68
  75.6 1.3 fusion.118
  77.6 1.2 collective-permute-start.4
  78.7 3.7 %collective-permute-start.5 = (f32[16,1,1024]{2,1,0:T(1,128)S(1)}, f32[16,1,1024]{2,1,0:T(1,128)S(1)}, u32[]{:S(2)}, u32[]{:S(2)}) collective-permute-start(f32[16,1,1024]{2,1,0:T(1,128)S(1)} %get-tuple-element.56), channel_id=1, source_target_pairs={{8,0},{16,8},{24,16},{32,24},{40,32},{48,40},{56,48},{64,56},{72,6... | collective-permute-start | bytes 196616 | tf_op jit(solution)/shard_map/ppermute | solution.py:27
  82.4 2.0 %collective-permute-done.4 = f32[16,1,1024]{2,1,0:T(1,128)S(1)} collective-permute-done((f32[16,1,1024]{2,1,0:T(1,128)S(1)}, f32[16,1,1024]{2,1,0:T(1,128)S(1)}, u32[]{:S(2)}, u32[]{:S(2)}) %collective-permute-start.4) | collective-permute-done | bytes 65568 | tf_op jit(solution)/shard_map/ppermute | solution.py:24
  84.4 1.1 collective-permute-start.6
  85.5 0.7 collective-permute-start.7
  86.5 1.6 %collective-permute-done.6 = f32[1,10,1024]{2,1,0:T(8,128)S(1)} collective-permute-done((f32[1,10,1024]{2,1,0:T(8,128)S(1)}, f32[1,10,1024]{2,1,0:T(8,128)S(1)}, u32[]{:S(2)}, u32[]{:S(2)}) %collective-permute-start.6) | collective-permute-done | bytes 40992 | tf_op jit(solution)/shard_map/ppermute | solution.py:27
  90.6 3.1 %collective-permute-done.8 = f32[16,1,1024]{2,1,0:T(1,128)S(1)} collective-permute-done((f32[16,1,1024]{2,1,0:T(1,128)S(1)}, f32[16,1,1024]{2,1,0:T(1,128)S(1)}, u32[]{:S(2)}, u32[]{:S(2)}) %collective-permute-start.8) | collective-permute-done | bytes 65568 | tf_op jit(solution)/shard_map/ppermute | solution.py:35
  93.6 10.9 %fusion.259 = (f32[16,8,1024]{2,1,0:T(8,128)S(1)}, f32[16,8,1024]{2,1,0:T(8,128)S(1)}, f32[16,8,1024]{2,1,0:T(8,128)S(1)}, f32[16,8,1024]{2,1,0:T(8,128)S(1)}, f32[16,8,1024]{2,1,0:T(8,128)S(1)}) fusion(f32[16,7,1024]{2,1,0:T(8,128)S(1)} %bitcast.13, f32[16,1,1024]{2,1,0:T(1,128)S(1)} %collective-permute-done.8, f32[]{:T(128)S(6)} %neg.2, ...), kind=kLoop, calls=%fused_computation.580 | loop fusion | flops 71303168 | bytes 10485764 | tf_op jit(solution)/shard_map/div | solution.py:68
  104.5 1.3 fusion.244
  106.0 4.8 %collective-permute-start.10 = (f32[16,1,1024]{2,1,0:T(1,128)S(1)}, f32[16,1,1024]{2,1,0:T(1,128)S(1)}, u32[]{:S(2)}, u32[]{:S(2)}) collective-permute-start(f32[16,1,1024]{2,1,0:T(1,128)S(1)} %slice.639), channel_id=1, source_target_pairs={{0,120},{8,0},{16,8},{24,16},{32,24},{40,32},{48,40},{56,48},{64,5... | collective-permute-start | bytes 196616 | tf_op jit(solution)/shard_map/ppermute | solution.py:35
  110.9 1.5 %collective-permute-done.9 = f32[16,1,1024]{2,1,0:T(1,128)S(1)} collective-permute-done((f32[16,1,1024]{2,1,0:T(1,128)S(1)}, f32[16,1,1024]{2,1,0:T(1,128)S(1)}, u32[]{:S(2)}, u32[]{:S(2)}) %collective-permute-start.9) | collective-permute-done | bytes 65568 | tf_op jit(solution)/shard_map/ppermute | solution.py:35
  113.1 5.2 %collective-permute-start.12 = (f32[16,1,1024]{2,1,0:T(1,128)S(1)}, f32[16,1,1024]{2,1,0:T(1,128)S(1)}, u32[]{:S(2)}, u32[]{:S(2)}) collective-permute-start(f32[16,1,1024]{2,1,0:T(1,128)S(1)} %get-tuple-element.46), channel_id=1, source_target_pairs={{8,0},{16,8},{24,16},{32,24},{40,32},{48,40},{56,48},{64,56},{72,6... | collective-permute-start | bytes 196616 | tf_op jit(solution)/shard_map/ppermute | solution.py:27
  118.3 1.4 collective-permute-done.11
  119.6 2.8 %collective-permute-start.13 = (f32[1,10,1024]{2,1,0:T(8,128)S(1)}, f32[1,10,1024]{2,1,0:T(8,128)S(1)}, u32[]{:S(2)}, u32[]{:S(2)}) collective-permute-start(f32[1,10,1024]{2,1,0:T(8,128)S(1)} %get-tuple-element.31), channel_id=1, source_target_pairs={{0,1},{1,2},{2,3},{3,4},{4,5},{5,6},{6,7},{7,0},{8,9},{9,10},{10,1... | collective-permute-start | bytes 122888 | tf_op jit(solution)/shard_map/ppermute | solution.py:24
  122.7 1.5 %collective-permute-start.15 = (f32[1,8,1024]{2,1,0:T(8,128)S(1)}, f32[1,8,1024]{2,1,0:T(8,128)S(1)}, u32[]{:S(2)}, u32[]{:S(2)}) collective-permute-start(f32[1,8,1024]{2,1,0:T(8,128)S(1)} %slice.576), channel_id=1, source_target_pairs={{0,1},{1,2},{2,3},{3,4},{4,5},{5,6},{6,7},{7,0},{8,9},{9,10},{10,1... | collective-permute-start | bytes 98312 | tf_op jit(solution)/shard_map/ppermute | solution.py:35
  124.2 1.9 %collective-permute-done.14 = f32[1,10,1024]{2,1,0:T(8,128)S(1)} collective-permute-done((f32[1,10,1024]{2,1,0:T(8,128)S(1)}, f32[1,10,1024]{2,1,0:T(8,128)S(1)}, u32[]{:S(2)}, u32[]{:S(2)}) %collective-permute-start.14) | collective-permute-done | bytes 40992 | tf_op jit(solution)/shard_map/ppermute | solution.py:27
  128.6 10.9 %fusion.385 = (f32[16,8,1024]{2,1,0:T(8,128)S(1)}, f32[16,8,1024]{2,1,0:T(8,128)S(1)}, f32[16,8,1024]{2,1,0:T(8,128)S(1)}, f32[16,8,1024]{2,1,0:T(8,128)S(1)}, f32[16,8,1024]{2,1,0:T(8,128)S(1)}) fusion(f32[15,8,1024]{2,1,0:T(8,128)S(1)} %slice.577, f32[1,8,1024]{2,1,0:T(8,128)S(1)} %collective-permute-done.15, f32[]{:T(128)S(6)} %neg.2, ...), kind=kLoop, calls=%fused_computation.710 | loop fusion | flops 71303168 | bytes 10485764 | tf_op jit(solution)/shard_map/div | solution.py:68
  139.5 1.3 fusion.370
  140.8 1.6 %collective-permute-start.17 = (f32[1,8,1024]{2,1,0:T(8,128)S(1)}, f32[1,8,1024]{2,1,0:T(8,128)S(1)}, u32[]{:S(2)}, u32[]{:S(2)}) collective-permute-start(f32[1,8,1024]{2,1,0:T(8,128)S(1)} %slice.669), channel_id=1, source_target_pairs={{0,7},{1,0},{2,1},{3,2},{4,3},{5,4},{6,5},{7,6},{8,15},{9,8},{10,9... | collective-permute-start | bytes 98312 | tf_op jit(solution)/shard_map/ppermute | solution.py:35
  143.1 1.1 collective-permute-done.17
  144.2 1.2 fusion.608
  (96 shorter events, 10.7 us)
Async XLA Ops:
  0.6 13.3 %copy-start.7 = (u32[128]{0:T(128)S(1)}, u32[128]{0:T(128)}, u32[]{:S(2)}) copy-start(u32[128]{0:T(128)} %constant.57) | copy-start | bytes 1540
  0.6 17.9 %copy-start.6 = (u32[128]{0:T(128)S(1)}, u32[128]{0:T(128)}, u32[]{:S(2)}) copy-start(u32[128]{0:T(128)} %constant.62) | copy-start | bytes 1540
  0.7 27.4 %copy-start.5 = (u32[128]{0:T(128)S(1)}, u32[128]{0:T(128)}, u32[]{:S(2)}) copy-start(u32[128]{0:T(128)} %constant.67) | copy-start | bytes 1540
  0.7 36.0 %copy-start.4 = (u32[128]{0:T(128)S(1)}, u32[128]{0:T(128)}, u32[]{:S(2)}) copy-start(u32[128]{0:T(128)} %constant.72) | copy-start | bytes 1540
  0.7 56.3 %copy-start = (f32[16,8,1024]{2,1,0:T(8,128)S(1)}, f32[16,8,1024]{2,1,0:T(8,128)}, u32[]{:S(2)}) copy-start(f32[16,8,1024]{2,1,0:T(8,128)} %param.4) | copy-start | bytes 1572868
  0.7 11.8 %copy-start.1 = (f32[16,8,1024]{2,1,0:T(8,128)S(1)}, f32[16,8,1024]{2,1,0:T(8,128)}, u32[]{:S(2)}) copy-start(f32[16,8,1024]{2,1,0:T(8,128)} %param.5) | copy-start | bytes 1572868
  0.7 12.5 %copy-start.3 = (f32[16,8,1024]{2,1,0:T(8,128)S(1)}, f32[16,8,1024]{2,1,0:T(8,128)}, u32[]{:S(2)}) copy-start(f32[16,8,1024]{2,1,0:T(8,128)} %param.7) | copy-start | bytes 1572868
  2.1 54.8 %collective-permute-start = (f32[16,1,1024]{2,1,0:T(1,128)S(1)}, f32[16,1,1024]{2,1,0:T(1,128)S(1)}, u32[]{:S(2)}, u32[]{:S(2)}) collective-permute-start(f32[16,1,1024]{2,1,0:T(1,128)S(1)} %get-tuple-element.65), channel_id=1, source_target_pairs={{0,8},{8,16},{16,24},{24,32},{32,40},{40,48},{48,56},{56,64},{64,7... | collective-permute-start | bytes 196616 | tf_op jit(solution)/shard_map/ppermute | solution.py:24
  4.2 52.7 %collective-permute-start.1 = (f32[16,1,1024]{2,1,0:T(1,128)S(1)}, f32[16,1,1024]{2,1,0:T(1,128)S(1)}, u32[]{:S(2)}, u32[]{:S(2)}) collective-permute-start(f32[16,1,1024]{2,1,0:T(1,128)S(1)} %get-tuple-element.66), channel_id=1, source_target_pairs={{8,0},{16,8},{24,16},{32,24},{40,32},{48,40},{56,48},{64,56},{72,6... | collective-permute-start | bytes 196616 | tf_op jit(solution)/shard_map/ppermute | solution.py:27
  57.0 5.1 %collective-permute-start.2 = (f32[1,10,1024]{2,1,0:T(8,128)S(1)}, f32[1,10,1024]{2,1,0:T(8,128)S(1)}, u32[]{:S(2)}, u32[]{:S(2)}) collective-permute-start(f32[1,10,1024]{2,1,0:T(8,128)S(1)} %get-tuple-element.35), channel_id=1, source_target_pairs={{1,0},{2,1},{3,2},{4,3},{5,4},{6,5},{7,6},{0,7},{9,8},{10,9},{11,1... | collective-permute-start | bytes 122888 | tf_op jit(solution)/shard_map/ppermute | solution.py:27
  57.3 4.7 %collective-permute-start.3 = (f32[1,10,1024]{2,1,0:T(8,128)S(1)}, f32[1,10,1024]{2,1,0:T(8,128)S(1)}, u32[]{:S(2)}, u32[]{:S(2)}) collective-permute-start(f32[1,10,1024]{2,1,0:T(8,128)S(1)} %get-tuple-element.36), channel_id=1, source_target_pairs={{0,1},{1,2},{2,3},{3,4},{4,5},{5,6},{6,7},{7,0},{8,9},{9,10},{10,1... | collective-permute-start | bytes 122888 | tf_op jit(solution)/shard_map/ppermute | solution.py:24
  77.0 9.2 %copy-start.2 = (f32[16,8,1024]{2,1,0:T(8,128)S(1)}, f32[16,8,1024]{2,1,0:T(8,128)}, u32[]{:S(2)}) copy-start(f32[16,8,1024]{2,1,0:T(8,128)} %param.6) | copy-start | bytes 1572868
  77.6 6.8 %collective-permute-start.4 = (f32[16,1,1024]{2,1,0:T(1,128)S(1)}, f32[16,1,1024]{2,1,0:T(1,128)S(1)}, u32[]{:S(2)}, u32[]{:S(2)}) collective-permute-start(f32[16,1,1024]{2,1,0:T(1,128)S(1)} %get-tuple-element.55), channel_id=1, source_target_pairs={{0,8},{8,16},{16,24},{24,32},{32,40},{40,48},{48,56},{56,64},{64,7... | collective-permute-start | bytes 196616 | tf_op jit(solution)/shard_map/ppermute | solution.py:24
  78.7 5.7 %collective-permute-start.5 = (f32[16,1,1024]{2,1,0:T(1,128)S(1)}, f32[16,1,1024]{2,1,0:T(1,128)S(1)}, u32[]{:S(2)}, u32[]{:S(2)}) collective-permute-start(f32[16,1,1024]{2,1,0:T(1,128)S(1)} %get-tuple-element.56), channel_id=1, source_target_pairs={{8,0},{16,8},{24,16},{32,24},{40,32},{48,40},{56,48},{64,56},{72,6... | collective-permute-start | bytes 196616 | tf_op jit(solution)/shard_map/ppermute | solution.py:27
  84.4 3.7 %collective-permute-start.6 = (f32[1,10,1024]{2,1,0:T(8,128)S(1)}, f32[1,10,1024]{2,1,0:T(8,128)S(1)}, u32[]{:S(2)}, u32[]{:S(2)}) collective-permute-start(f32[1,10,1024]{2,1,0:T(8,128)S(1)} %get-tuple-element.33), channel_id=1, source_target_pairs={{1,0},{2,1},{3,2},{4,3},{5,4},{6,5},{7,6},{0,7},{9,8},{10,9},{11,1... | collective-permute-start | bytes 122888 | tf_op jit(solution)/shard_map/ppermute | solution.py:27
  85.5 2.6 %collective-permute-start.7 = (f32[1,10,1024]{2,1,0:T(8,128)S(1)}, f32[1,10,1024]{2,1,0:T(8,128)S(1)}, u32[]{:S(2)}, u32[]{:S(2)}) collective-permute-start(f32[1,10,1024]{2,1,0:T(8,128)S(1)} %get-tuple-element.34), channel_id=1, source_target_pairs={{0,1},{1,2},{2,3},{3,4},{4,5},{5,6},{6,7},{7,0},{8,9},{9,10},{10,1... | collective-permute-start | bytes 122888 | tf_op jit(solution)/shard_map/ppermute | solution.py:24
  86.3 7.4 %collective-permute-start.8 = (f32[16,1,1024]{2,1,0:T(1,128)S(1)}, f32[16,1,1024]{2,1,0:T(1,128)S(1)}, u32[]{:S(2)}, u32[]{:S(2)}) collective-permute-start(f32[16,1,1024]{2,1,0:T(1,128)S(1)} %slice.538), channel_id=1, source_target_pairs={{0,8},{8,16},{16,24},{24,32},{32,40},{40,48},{48,56},{56,64},{64,7... | collective-permute-start | bytes 196616 | tf_op jit(solution)/shard_map/ppermute | solution.py:35
  105.9 6.5 %collective-permute-start.9 = (f32[16,1,1024]{2,1,0:T(1,128)S(1)}, f32[16,1,1024]{2,1,0:T(1,128)S(1)}, u32[]{:S(2)}, u32[]{:S(2)}) collective-permute-start(f32[16,1,1024]{2,1,0:T(1,128)S(1)} %slice.636), channel_id=1, source_target_pairs={{0,8},{8,16},{16,24},{24,32},{32,40},{40,48},{48,56},{56,64},{64,7... | collective-permute-start | bytes 196616 | tf_op jit(solution)/shard_map/ppermute | solution.py:35
  106.0 6.4 %collective-permute-start.10 = (f32[16,1,1024]{2,1,0:T(1,128)S(1)}, f32[16,1,1024]{2,1,0:T(1,128)S(1)}, u32[]{:S(2)}, u32[]{:S(2)}) collective-permute-start(f32[16,1,1024]{2,1,0:T(1,128)S(1)} %slice.639), channel_id=1, source_target_pairs={{0,120},{8,0},{16,8},{24,16},{32,24},{40,32},{48,40},{56,48},{64,5... | collective-permute-start | bytes 196616 | tf_op jit(solution)/shard_map/ppermute | solution.py:35
  113.0 6.6 %collective-permute-start.11 = (f32[16,1,1024]{2,1,0:T(1,128)S(1)}, f32[16,1,1024]{2,1,0:T(1,128)S(1)}, u32[]{:S(2)}, u32[]{:S(2)}) collective-permute-start(f32[16,1,1024]{2,1,0:T(1,128)S(1)} %get-tuple-element.45), channel_id=1, source_target_pairs={{0,8},{8,16},{16,24},{24,32},{32,40},{40,48},{48,56},{56,64},{64,7... | collective-permute-start | bytes 196616 | tf_op jit(solution)/shard_map/ppermute | solution.py:24
  113.1 6.5 %collective-permute-start.12 = (f32[16,1,1024]{2,1,0:T(1,128)S(1)}, f32[16,1,1024]{2,1,0:T(1,128)S(1)}, u32[]{:S(2)}, u32[]{:S(2)}) collective-permute-start(f32[16,1,1024]{2,1,0:T(1,128)S(1)} %get-tuple-element.46), channel_id=1, source_target_pairs={{8,0},{16,8},{24,16},{32,24},{40,32},{48,40},{56,48},{64,56},{72,6... | collective-permute-start | bytes 196616 | tf_op jit(solution)/shard_map/ppermute | solution.py:27
  119.6 4.6 %collective-permute-start.13 = (f32[1,10,1024]{2,1,0:T(8,128)S(1)}, f32[1,10,1024]{2,1,0:T(8,128)S(1)}, u32[]{:S(2)}, u32[]{:S(2)}) collective-permute-start(f32[1,10,1024]{2,1,0:T(8,128)S(1)} %get-tuple-element.31), channel_id=1, source_target_pairs={{0,1},{1,2},{2,3},{3,4},{4,5},{5,6},{6,7},{7,0},{8,9},{9,10},{10,1... | collective-permute-start | bytes 122888 | tf_op jit(solution)/shard_map/ppermute | solution.py:24
  122.4 3.7 %collective-permute-start.14 = (f32[1,10,1024]{2,1,0:T(8,128)S(1)}, f32[1,10,1024]{2,1,0:T(8,128)S(1)}, u32[]{:S(2)}, u32[]{:S(2)}) collective-permute-start(f32[1,10,1024]{2,1,0:T(8,128)S(1)} %get-tuple-element.32), channel_id=1, source_target_pairs={{1,0},{2,1},{3,2},{4,3},{5,4},{6,5},{7,6},{0,7},{9,8},{10,9},{11,1... | collective-permute-start | bytes 122888 | tf_op jit(solution)/shard_map/ppermute | solution.py:27
  122.7 5.9 %collective-permute-start.15 = (f32[1,8,1024]{2,1,0:T(8,128)S(1)}, f32[1,8,1024]{2,1,0:T(8,128)S(1)}, u32[]{:S(2)}, u32[]{:S(2)}) collective-permute-start(f32[1,8,1024]{2,1,0:T(8,128)S(1)} %slice.576), channel_id=1, source_target_pairs={{0,1},{1,2},{2,3},{3,4},{4,5},{5,6},{6,7},{7,0},{8,9},{9,10},{10,1... | collective-permute-start | bytes 98312 | tf_op jit(solution)/shard_map/ppermute | solution.py:35
  140.8 2.3 %collective-permute-start.16 = (f32[1,8,1024]{2,1,0:T(8,128)S(1)}, f32[1,8,1024]{2,1,0:T(8,128)S(1)}, u32[]{:S(2)}, u32[]{:S(2)}) collective-permute-start(f32[1,8,1024]{2,1,0:T(8,128)S(1)} %slice.666), channel_id=1, source_target_pairs={{0,1},{1,2},{2,3},{3,4},{4,5},{5,6},{6,7},{7,0},{8,9},{9,10},{10,1... | collective-permute-start | bytes 98312 | tf_op jit(solution)/shard_map/ppermute | solution.py:35
  140.8 3.4 %collective-permute-start.17 = (f32[1,8,1024]{2,1,0:T(8,128)S(1)}, f32[1,8,1024]{2,1,0:T(8,128)S(1)}, u32[]{:S(2)}, u32[]{:S(2)}) collective-permute-start(f32[1,8,1024]{2,1,0:T(8,128)S(1)} %slice.669), channel_id=1, source_target_pairs={{0,7},{1,0},{2,1},{3,2},{4,3},{5,4},{6,5},{7,6},{8,15},{9,8},{10,9... | collective-permute-start | bytes 98312 | tf_op jit(solution)/shard_map/ppermute | solution.py:35
where the time goes:
time: 149 us; the launch traced here: 146 us
  other arithmetic  52.8 us (35%)
  starting transfers between devices  31.8 us (21%)
  blocking collectives  31.7 us (21%)
  waiting for transfers between devices  13.1 us (9%)
  local copies, waits for them, and re-layouts  10.3 us (7%)
  between operations  6.86 us (5%)
    div x6, other arithmetic, region_volume(): return extent * combo / (6.0 * tilt_a * tilt_b)  36.7 us
    unnamed x4, blocking collectives  31.7 us
    ppermute x6, starting transfers between devices, extended(): lax.ppermute(lax.slice_in_dim(block, 0, width, axis=dim), axis, backward)  15.4 us
    ppermute x6, starting transfers between devices, shifted(): return lax.ppermute(value, axis, pairs)  8.26 us
    ppermute x6, starting transfers between devices, extended(): lax.ppermute(lax.slice_in_dim(block, block.shape[dim] - width, None, axis...  8.17 us
    ppermute x6, waiting for transfers between devices, shifted(): return lax.ppermute(value, axis, pairs)  6.21 us
    unnamed x6, other arithmetic  4.88 us
    unnamed x30, local copies, waits for them, and re-layouts  4.5 us
  transfers between devices with their start and end apart: 18, of which 8 were waited for; matrix products, arithmetic and copies ran while one was open for 14% of the time, Pallas kernels for 0%

commit v1 on v0

v1 whole, which is shorter than its diff:
```python
import jax
import jax.numpy as jnp
from jax import lax
from jax.experimental import pallas as pl
from jax.experimental.pallas import tpu as pltpu
from jax.sharding import PartitionSpec as P

NEWTON = 5
TILT_FLOOR = 3.2
TINY = 1e-18
COURANT = 0.45
EPSILON = 1e-6
THIRD = 1.0 / 3.0

NZ, NY, J, LN = 16, 8, 8, 128
N_GY, N_GZ = 16, 8
RING = 4
F32 = jnp.float32

HALO = (0, 8, 16)
VEL = 24
FLUX_Y = 26
FLUX_Z = 28
STAT_A = 30
STAT_X = 37
STAT_Z = 40
N_SEMS = 43


def lanes(u):
    return lax.broadcasted_iota(jnp.int32, u.shape, u.ndim - 1)


def at_next(u):
    moved = pltpu.roll(u, LN - 1, u.ndim - 1)
    return jnp.where(lanes(u) == LN - 1, pltpu.roll(moved, J - 1, u.ndim - 2), moved)


def at_prev(u):
    moved = pltpu.roll(u, 1, u.ndim - 1)
    return jnp.where(lanes(u) == 0, pltpu.roll(moved, 1, u.ndim - 2), moved)


def plane(g, slope_d, slope_a, slope_b):
    tilt_a = jnp.abs(slope_a) + TILT_FLOOR
    tilt_b = jnp.abs(slope_b) + TILT_FLOOR
    lo, hi = jnp.minimum(tilt_a, tilt_b), jnp.maximum(tilt_a, tilt_b)
    slope_d = jnp.where(jnp.abs(slope_d) < TINY, TINY, slope_d)
    tilt_d = jnp.abs(slope_d)
    m1, rest = jnp.minimum(lo, tilt_d), jnp.maximum(lo, tilt_d)
    m2, m3 = jnp.minimum(rest, hi), jnp.maximum(rest, hi)
    volume = jnp.clip(g, 0.0, 1.0)
    lesser = jnp.minimum(volume, 1.0 - volume)
    m12 = m1 * m2
    product = m12 * m3
    target = lesser * product
    both = target + target
    summed = lo + hi + tilt_d
    w = 0.5 * jnp.maximum(m1 + m2 - m3, 0.0)
    a = 0.5 * summed - (0.5 * product - target) / (m12 - w * w)
    for _ in range(NEWTON - 1):
        q0 = jnp.minimum(a, m1)
        r0 = a - q0
        p2 = jnp.maximum(a - m2, 0.0)
        q2 = jnp.minimum(p2, m1)
        r2 = p2 - q2
        p3 = jnp.maximum(a - m3, 0.0)
        s3 = p3 * p3
        value = q0 * (q0 * q0 * THIRD + a * r0) - q2 * (q2 * q2 * THIRD + p2 * r2) - s3 * (p3 * THIRD) - both
        rate = q0 * (a + r0) - q2 * (p2 + r2) - s3
        a = a - value / rate
    return jnp.where(volume > 0.5, summed - a, a), lo, hi, slope_d, 0.5 / product


def cube_part(s, h):
    p = jnp.maximum(s, 0.0)
    q = jnp.minimum(p, h)
    r = p - q
    return q * (q * q * THIRD + p * r)


def flow(offset, lo, hi, slope_d, scale, c):
    signed = c * slope_d
    h = jnp.abs(signed)
    s = offset - jnp.where(signed < 0, jnp.abs(slope_d) - h, 0.0)
    t = s - hi
    return scale * ((cube_part(s, h) - cube_part(s - lo, h)) - (cube_part(t, h) - cube_part(t - lo, h)))


def rows(ref, where):
    parts = [ref[z, pl.ds(y, n)] for z, y, n in where]
    return parts[0] if len(parts) == 1 else jnp.concatenate(parts, axis=0)


def put(ref, where, value):
    start = 0
    for z, y, n in where:
        ref[z, pl.ds(y, n)] = value[start : start + n]
        start += n


def moved(where, dz, dy):
    return [(z + dz, y + dy, n) for z, y, n in where]


def loop(first, last, body):
    def step(i, carry):
        body(i)
        return carry

    lax.fori_loop(first, last, step, 0)


def kernel(
    f_hbm, vx_hbm, vy_hbm, vz_hbm, out_hbm, dt_out,
    f_ext, g1_ext, g2_ext, vx, vy, vz, smooth, diff, sum_y, dif_y, sum_d,
    off, lo, hi, slope, scale, face_y, face_z, edge_y, edge_z,
    stat_a, stat_x, stat_z, dt_vec, out_buf,
    load_sem, out_sem, send_sem, recv_sem,
):
    gy, gz = lax.axis_index("gy"), lax.axis_index("gz")
    chip_z, chip_x = gy // RING, lax.rem(gy, RING)

    def neighbour(dy, dz):
        return {"gy": lax.rem(gy + dy + N_GY, N_GY), "gz": lax.rem(gz + dz + N_GZ, N_GZ)}

    def along_x(k):
        return {"gy": chip_z * RING + lax.rem(chip_x + k, RING), "gz": gz}

    def along_z(k):
        return {"gy": lax.rem(chip_z + k, RING) * RING + chip_x, "gz": gz}

    corners = [(1, 1), (1, -1), (-1, 1), (-1, -1)]

    loads = []
    for source, target in (
        (f_hbm, lambda y: f_ext.at[pl.ds(1, NZ), 1 + y]),
        (vx_hbm, lambda y: vx.at[:, y]),
        (vy_hbm, lambda y: vy.at[:, 1 + y]),
        (vz_hbm, lambda y: vz.at[pl.ds(1, NZ), y]),
    ):
        loads.append([
            pltpu.make_async_copy(source.at[:, :, y, :], target(y), load_sem.at[len(loads), y])
            for y in range(NY)
        ])
    for group in loads:
        for copy in group:
            copy.start()
    barrier = pltpu.get_barrier_semaphore()
    greeted = [neighbour(0, k) for k in range(1, N_GZ)]
    greeted += [neighbour(1, 0), neighbour(-1, 0)] + [neighbour(*c) for c in corners]
    greeted += [along_x(k) for k in range(1, RING)] + [along_z(k) for k in range(1, RING)]
    for device in greeted:
        pl.semaphore_signal(barrier, inc=1, device_id=device, device_id_type=pl.DeviceIdType.MESH)

    def remote(source, target, k, device):
        return pltpu.make_async_remote_copy(
            src_ref=source, dst_ref=target, send_sem=send_sem.at[k], recv_sem=recv_sem.at[k],
            device_id=device, device_id_type=pl.DeviceIdType.MESH,
        )

    def halo(g, base):
        inner_z, inner_y = pl.ds(1, NZ), pl.ds(1, NY)
        copies = [
            remote(g.at[inner_z, NY], g.at[inner_z, 0], base, neighbour(1, 0)),
            remote(g.at[inner_z, 1], g.at[inner_z, NY + 1], base + 1, neighbour(-1, 0)),
            remote(g.at[NZ, inner_y], g.at[0, inner_y], base + 2, neighbour(0, 1)),
            remote(g.at[1, inner_y], g.at[NZ + 1, inner_y], base + 3, neighbour(0, -1)),
        ]
        for k, (dy, dz) in enumerate(corners):
            source = g.at[NZ if dz > 0 else 1, NY if dy > 0 else 1]
            target = g.at[0 if dz > 0 else NZ + 1, 0 if dy > 0 else NY + 1]
            copies.append(remote(source, target, base + 4 + k, neighbour(dy, dz)))
        return copies

    sent = []

    def send(copies):
        for copy in copies:
            copy.start()
        sent.extend(copies)

    def arrive(copies):
        for copy in copies:
            copy.wait_recv()

    def put_shifts(g, where):
        before, after = at_prev(g), at_next(g)
        put(smooth, where, before + 2.0 * g + after)
        put(diff, where, after - before)

    for copy in loads[0]:
        copy.wait()

    def scan_fraction(z, total):
        g = f_ext[z, pl.ds(1, NY)]
        put_shifts(g, [(z, 1, NY)])
        return total + g * (1.0 - g)

    total = lax.fori_loop(1, NZ + 1, scan_fraction, jnp.zeros((NY, J, LN), F32))
    for group in loads[1:]:
        for copy in group:
            copy.wait()

    def scan_velocity(z, peak):
        own = jnp.maximum(jnp.abs(vx[z]), jnp.abs(vy[z, pl.ds(1, NY)]))
        return jnp.maximum(peak, jnp.maximum(own, jnp.abs(vz[z + 1])))

    peak = lax.fori_loop(0, NZ, scan_velocity, jnp.zeros((NY, J, LN), F32))
    first_row = lax.broadcasted_iota(jnp.int32, (J, LN), 0) == 0

    def stat_tile(peak_rows, total_rows):
        return jnp.where(
            first_row,
            jnp.broadcast_to(jnp.max(peak_rows, axis=0, keepdims=True), (J, LN)),
            jnp.broadcast_to(jnp.sum(total_rows, axis=0, keepdims=True), (J, LN)),
        )

    def combined(ref, n):
        top, add = ref[0], ref[0]
        for k in range(1, n):
            top, add = jnp.maximum(top, ref[k]), add + ref[k]
        return jnp.where(first_row, top, add)

    stat_a[gz] = stat_tile(jnp.max(peak, axis=0), jnp.sum(total, axis=0))

    pl.semaphore_wait(barrier, len(greeted))
    halo_f = halo(f_ext, HALO[0])
    stats_a = [
        remote(stat_a.at[gz], stat_a.at[gz], STAT_A + k - 1, neighbour(0, k)) for k in range(1, N_GZ)
    ]
    stats_x = [
        remote(stat_x.at[chip_x], stat_x.at[chip_x], STAT_X + k - 1, along_x(k)) for k in range(1, RING)
    ]
    stats_z = [
        remote(stat_z.at[chip_z], stat_z.at[chip_z], STAT_Z + k - 1, along_z(k)) for k in range(1, RING)
    ]
    velocity = [
        remote(vy.at[:, NY], vy.at[:, 0], VEL, neighbour(1, 0)),
        remote(vz.at[NZ], vz.at[0], VEL + 1, neighbour(0, 1)),
    ]
    send(stats_a)
    send(halo_f)
    send(velocity)

    def put_sums(z, y, n):
        s = smooth[z, pl.ds(y - 1, n + 2)]
        d = diff[z, pl.ds(y - 1, n + 2)]
        where = [(z, y - 1, n)]
        put(sum_y, where, s[:-2] + 2.0 * s[1:-1] + s[2:])
        put(dif_y, where, s[2:] - s[:-2])
        put(sum_d, where, d[:-2] + 2.0 * d[1:-1] + d[2:])

    def put_planes(g_ext, where, dim):
        at = moved(where, 0, -1)
        below, above = moved(at, -1, 0), moved(at, 1, 0)
        along_z = rows(sum_y, above) - rows(sum_y, below)
        along_y = rows(dif_y, below) + 2.0 * rows(dif_y, at) + rows(dif_y, above)
        along_x = rows(sum_d, below) + 2.0 * rows(sum_d, at) + rows(sum_d, above)
        slopes = [along_z, along_y, along_x]
        across = [slopes[k] for k in range(3) if k != dim]
        found = plane(rows(g_ext, where), slopes[dim], *across)
        for ref, value in zip((off, lo, hi, slope, scale), found):
            put(ref, moved(where, -1, -1), value)

    inner = (2, NY - 2)

    def sums_inner():
        loop(1, NZ + 1, lambda z: put_sums(z, *inner))

    def planes_inner(g_ext, dim, first, last):
        loop(first, last, lambda z: put_planes(g_ext, [(z, *inner)], dim))

    def y_edge(i):
        z = 2 * i + 1
        return [(z, 1, 1), (z, NY, 1), (z + 1, 1, 1), (z + 1, NY, 1)]

    def z_edge(i):
        return [(1 + i * (NZ - 1), *inner)]

    def sums_outer(g_ext):
        def sides(i):
            z = 2 * i + 1
            where = [(z, 0, 1), (z, NY + 1, 1), (z + 1, 0, 1), (z + 1, NY + 1, 1)]
            put_shifts(rows(g_ext, where), where)

        def ends(i):
            where = [(i * (NZ + 1), 0, NY + 2)]
            put_shifts(rows(g_ext, where), where)

        loop(0, NZ // 2, sides)
        loop(0, 2, ends)

        def side_sums(z):
            put_sums(z, 1, 1)
            put_sums(z, NY, 1)

        loop(1, NZ + 1, side_sums)
        loop(0, 2, lambda i: put_sums(i * (NZ + 1), 1, NY))

    def donors(upward, here, there):
        picked = []
        for ref in (off, lo, hi, slope):
            picked.append(jnp.where(upward, rows(ref, here), rows(ref, there)))
        picked.append(jnp.where(upward, rows(scale, here), -rows(scale, there)))
        return picked

    sums_inner()
    planes_inner(f_ext, 2, 2, 6)
    arrive(stats_a)
    stat_x[chip_x] = combined(stat_a, N_GZ)
    planes_inner(f_ext, 2, 6, 7)
    send(stats_x)
    planes_inner(f_ext, 2, 7, 11)
    arrive(stats_x)
    stat_z[chip_z] = combined(stat_x, RING)
    planes_inner(f_ext, 2, 11, 12)
    send(stats_z)
    planes_inner(f_ext, 2, 12, NZ)
    arrive(halo_f)
    arrive(velocity)
    sums_outer(f_ext)
    loop(0, NZ // 2, lambda i: put_planes(f_ext, y_edge(i), 2))
    loop(0, 2, lambda i: put_planes(f_ext, z_edge(i), 2))
    arrive(stats_z)
    stats = combined(stat_z, RING)
    umax = jnp.max(stats[0:1], axis=1, keepdims=True)
    share = jnp.sum(stats[1:2], axis=1, keepdims=True) * (4.0 / (N_GZ * NZ * N_GY * NY * J * LN))
    step = COURANT / ((umax + EPSILON) * (1.0 + share))
    dt_vec[...] = jnp.broadcast_to(step, (J, LN))
    dt_out[0, 0] = jnp.max(step)

    def sweep_x(where):
        here = moved(where, -1, -1)
        c = dt_vec[...] * rows(vx, here)
        upward = c > 0
        picked = []
        for ref in (off, lo, hi, slope, scale):
            own = rows(ref, here)
            other = at_next(own)
            picked.append(jnp.where(upward, own, -other if ref is scale else other))
        out = flow(*picked, c)
        g = (rows(f_ext, where) - out + at_prev(out)) / (1.0 - c + at_prev(c))
        put(g1_ext, where, g)
        put_shifts(g, where)

    loop(0, NZ // 2, lambda i: sweep_x(y_edge(i)))
    loop(0, 2, lambda i: sweep_x(z_edge(i)))
    halo_1 = halo(g1_ext, HALO[1])
    send(halo_1)
    loop(2, NZ, lambda z: sweep_x([(z, *inner)]))

    half = NZ // 2 + 1
    sums_inner()
    planes_inner(g1_ext, 1, 2, half)
    arrive(halo_1)
    sums_outer(g1_ext)
    loop(0, NZ // 2, lambda i: put_planes(g1_ext, y_edge(i), 1))

    def half_faces_y(i):
        where = moved(y_edge(i), -1, -1)
        at_face = [(2 * i, 0, 1), (2 * i, NY, 1), (2 * i + 1, 0, 1), (2 * i + 1, NY, 1)]
        c = dt_vec[...] * rows(vy, at_face)
        out = flow(*[rows(ref, where) for ref in (off, lo, hi, slope, scale)], c)
        for k in range(2):
            edge_y[0, 2 * i + k] = jnp.where(c[2 * k + 1] > 0, out[2 * k + 1], 0.0)
            edge_y[1, 2 * i + k] = jnp.where(c[2 * k] < 0, out[2 * k], 0.0)

    loop(0, NZ // 2, half_faces_y)
    flux_y = [
        remote(edge_y.at[0], edge_y.at[2], FLUX_Y, neighbour(1, 0)),
        remote(edge_y.at[1], edge_y.at[3], FLUX_Y + 1, neighbour(-1, 0)),
    ]
    loop(0, 2, lambda i: put_planes(g1_ext, z_edge(i), 1))
    send(flux_y)
    planes_inner(g1_ext, 1, half, NZ)

    def faces_y(z):
        c = dt_vec[...] * vy[z, pl.ds(1, NY - 1)]
        face_y[z, pl.ds(1, NY - 1)] = flow(*donors(c > 0, [(z, 0, NY - 1)], [(z, 1, NY - 1)]), c)

    loop(0, NZ, faces_y)
    arrive(flux_y)

    def update_y(z):
        face_y[z, 0] = edge_y[2, z] - edge_y[1, z]
        face_y[z, NY] = edge_y[0, z] - edge_y[3, z]
        out, q = face_y[z], vy[z]
        g = (g1_ext[z + 1, pl.ds(1, NY)] - out[1:] + out[:-1]) / (1.0 - dt_vec[...] * (q[1:] - q[:-1]))
        where = [(z + 1, 1, NY)]
        put(g2_ext, where, g)
        put_shifts(g, where)

    loop(0, NZ, update_y)
    halo_2 = halo(g2_ext, HALO[2])

    sums_inner()
    send(halo_2)
    planes_inner(g2_ext, 0, 2, half)
    arrive(halo_2)
    sums_outer(g2_ext)
    loop(0, NZ // 2, lambda i: put_planes(g2_ext, y_edge(i), 0))
    loop(0, 2, lambda i: put_planes(g2_ext, z_edge(i), 0))

    def half_faces_z(i):
        c = dt_vec[...] * vz[i * NZ]
        where = [(i * (NZ - 1), 0, NY)]
        out = flow(*[rows(ref, where) for ref in (off, lo, hi, slope, scale)], c)
        toward = jnp.where(i == 0, -c, c)
        edge_z[1 - i] = jnp.where(toward > 0, out, 0.0)

    loop(0, 2, half_faces_z)
    flux_z = [
        remote(edge_z.at[0], edge_z.at[2], FLUX_Z, neighbour(0, 1)),
        remote(edge_z.at[1], edge_z.at[3], FLUX_Z + 1, neighbour(0, -1)),
    ]
    planes_inner(g2_ext, 0, half, half + 1)
    send(flux_z)
    planes_inner(g2_ext, 0, half + 1, NZ)

    def faces_z(z):
        c = dt_vec[...] * vz[z]
        face_z[z] = flow(*donors(c > 0, [(z - 1, 0, NY)], [(z, 0, NY)]), c)

    loop(1, NZ, faces_z)
    arrive(flux_z)
    face_z[0] = edge_z[2] - edge_z[1]
    face_z[NZ] = edge_z[0] - edge_z[3]

    def update_z(z):
        g = g2_ext[z + 1, pl.ds(1, NY)] - face_z[z + 1] + face_z[z]
        out_buf[z] = g / (1.0 - dt_vec[...] * (vz[z + 1] - vz[z]))

    loop(0, NZ, update_z)
    stores = [
        pltpu.make_async_copy(out_buf.at[:, y], out_hbm.at[:, :, y, :], out_sem.at[y]) for y in range(NY)
    ]
    for copy in stores:
        copy.start()
    for copy in sent:
        copy.wait_send()
    for copy in stores:
        copy.wait()


def shards(*blocks):
    tiled = [b.reshape(NZ, NY, J, LN).transpose(0, 2, 1, 3) for b in blocks]
    row = (J, LN)
    ext = pltpu.VMEM((NZ + 2, NY + 2, *row), F32)
    sums = pltpu.VMEM((NZ + 2, NY, *row), F32)
    own = pltpu.VMEM((NZ, NY, *row), F32)
    anywhere = pl.BlockSpec(memory_space=pl.ANY)
    field, step = pl.pallas_call(
        kernel,
        out_shape=(jax.ShapeDtypeStruct((NZ, J, NY, LN), F32), jax.ShapeDtypeStruct((1, 1), F32)),
        in_specs=[anywhere] * 4,
        out_specs=(anywhere, pl.BlockSpec(memory_space=pltpu.SMEM)),
        scratch_shapes=[
            ext, ext, ext,
            own, pltpu.VMEM((NZ, NY + 1, *row), F32), pltpu.VMEM((NZ + 1, NY, *row), F32),
            ext, ext, sums, sums, sums,
            own, own, own, own, own,
            pltpu.VMEM((NZ, NY + 1, *row), F32), pltpu.VMEM((NZ + 1, NY, *row), F32),
            pltpu.VMEM((4, NZ, *row), F32), pltpu.VMEM((4, NY, *row), F32),
            pltpu.VMEM((N_GZ, *row), F32), pltpu.VMEM((RING, *row), F32), pltpu.VMEM((RING, *row), F32),
            pltpu.VMEM(row, F32), own,
            pltpu.SemaphoreType.DMA((4, NY)), pltpu.SemaphoreType.DMA((NY,)),
            pltpu.SemaphoreType.DMA((N_SEMS,)), pltpu.SemaphoreType.DMA((N_SEMS,)),
        ],
        compiler_params=pltpu.CompilerParams(collective_id=0, has_side_effects=True),
        name="advect",
    )(*tiled)
    return field.transpose(0, 2, 1, 3).reshape(NZ, NY, J * LN), step.reshape(())


def solution(mesh):
    spec = P("gz", "gy", None)
    return jax.shard_map(shards, mesh=mesh, in_specs=(spec,) * 4, out_specs=(spec, P()), check_vma=False)
```

time: 149 us -> 54.5 us (0.37); the launches traced: 146 us -> 54.1 us
  other arithmetic: 52.8 us -> 0 us
  Pallas kernels: 0 us -> 49.9 us
  starting transfers between devices: 31.8 us -> 0 us
  blocking collectives: 31.7 us -> 0 us
  waiting for transfers between devices: 13.1 us -> 0 us
  local copies, waits for them, and re-layouts: 10.3 us -> 1.89 us
  between operations: 6.86 us -> 2.34 us
    pallas_call x0 -> x1, Pallas kernels: none -> 49.9 us  [shards(): pl.pallas_call(kernel, out_shape=(jax.ShapeDtypeStruct((NZ, J, NY, LN), F...]
    div x9 -> x0, other arithmetic: 38.8 us -> none  [the longest x6 36.7 us: region_volume(): return extent * combo / (6.0 * tilt_a * tilt_b)]
    ppermute x18 -> x0, starting transfers between devices: 31.8 us -> none  [the longest x6 15.4 us: extended(): lax.ppermute(lax.slice_in_dim(block, 0, width, axis=dim), axis, backward)]
    unnamed x4 -> x0, blocking collectives: 31.7 us -> none
    ppermute x18 -> x0, waiting for transfers between devices: 13.1 us -> none  [the longest x6 6.21 us: shifted(): return lax.ppermute(value, axis, pairs)]
    slice x31 -> x0, local copies, waits for them, and re-layouts: 5.8 us -> none  [the longest x10 1.62 us: smooth_cells(): return jnp.roll(arr, 1, 2) + 2.0 * arr + jnp.roll(arr, -1, 2)]
    unnamed x6 -> x0, other arithmetic: 4.88 us -> none
    reduce_max x3 -> x0, other arithmetic: 3.04 us -> none  [the longest x1 1.68 us: shards(): jnp.max(jnp.abs(velocity_y))]
  transfers between devices with their start and end apart: 18 -> 0, of which waited for: 8 -> 0; matrix products, arithmetic and copies ran while one was open for 14% -> 0% of each run, Pallas kernels for 0% -> 0%
where the time goes in v1:
time: 54.5 us; the launch traced here: 54.1 us
  Pallas kernels  49.9 us (92%)
  between operations  2.34 us (4%)
  local copies, waits for them, and re-layouts  1.89 us (3%)
    pallas_call x1, Pallas kernels, shards(): pl.pallas_call(kernel, out_shape=(jax.ShapeDtypeStruct((NZ, J, NY, LN), F...  49.9 us
    unnamed x1, local copies, waits for them, and re-layouts  1.89 us

profile of v1, /device:TPU:1, one launch (start us, length us, event | category | flops | bytes accessed | tf_op | source)
XLA Modules:
  0.0 54.1 jit_solution(16165205656496894407)
XLA Ops:
  0.6 49.9 %advect.1 = (f32[16,8,8,128]{3,2,1,0:T(8,128)}, f32[1,1]{1,0:T(1,128)}) custom-call(f32[16,8,8,128]{3,2,1,0:T(8,128)} %bitcast.17, f32[16,8,8,128]{3,2,1,0:T(8,128)} %bitcast.18, f32[16,8,8,128]{3,2,1,0:T(8,128)} %bitcast.19, f32[16,8,8,128]{3,2,1,0:T(8,128)} %bitcast.20), custom_call_target="tpu_custom_call" | custom-call | tf_op jit(solution)/shard_map/advect/pallas_call | solution.py:453
  50.5 1.9 %copy.8 = f32[16,8,1024]{2,1,0:T(8,128)} copy(f32[16,8,1024]{2,1,0:T(8,128)} %bitcast.16) | data formatting | bytes 1048576

commit v2 on v1

v2 whole, which is shorter than its diff:
```python
import jax
import jax.numpy as jnp
from jax import lax
from jax.experimental import pallas as pl
from jax.experimental.pallas import tpu as pltpu
from jax.sharding import PartitionSpec as P

NEWTON = 5
TILT_FLOOR = 3.2
TINY = 1e-18
COURANT = 0.45
EPSILON = 1e-6
THIRD = 1.0 / 3.0

NZ, NY, J, LN = 16, 8, 8, 128
N_GY, N_GZ = 16, 8
RING = 4
F32 = jnp.float32

EZ, EY = NZ + 4, NY + 4
Z0, Y0 = 2, 2
Z1, Y1 = Z0 + NZ, Y0 + NY

HALO_F, HALO_V, HALO_G = 0, 8, 16
VEL = 24
FLUX_Y = 26
STAT_A = 28
STAT_X = 35
STAT_Z = 38
N_SEMS = 41


def lanes(u):
    return lax.broadcasted_iota(jnp.int32, u.shape, u.ndim - 1)


def at_next(u):
    moved = pltpu.roll(u, LN - 1, u.ndim - 1)
    return jnp.where(lanes(u) == LN - 1, pltpu.roll(moved, J - 1, u.ndim - 2), moved)


def at_prev(u):
    moved = pltpu.roll(u, 1, u.ndim - 1)
    return jnp.where(lanes(u) == 0, pltpu.roll(moved, 1, u.ndim - 2), moved)


def plane(g, slope_d, slope_a, slope_b):
    tilt_a = jnp.abs(slope_a) + TILT_FLOOR
    tilt_b = jnp.abs(slope_b) + TILT_FLOOR
    lo, hi = jnp.minimum(tilt_a, tilt_b), jnp.maximum(tilt_a, tilt_b)
    slope_d = jnp.where(jnp.abs(slope_d) < TINY, TINY, slope_d)
    tilt_d = jnp.abs(slope_d)
    m1, rest = jnp.minimum(lo, tilt_d), jnp.maximum(lo, tilt_d)
    m2, m3 = jnp.minimum(rest, hi), jnp.maximum(rest, hi)
    volume = jnp.clip(g, 0.0, 1.0)
    lesser = jnp.minimum(volume, 1.0 - volume)
    m12 = m1 * m2
    product = m12 * m3
    target = lesser * product
    both = target + target
    summed = lo + hi + tilt_d
    w = 0.5 * jnp.maximum(m1 + m2 - m3, 0.0)
    a = 0.5 * summed - (0.5 * product - target) / (m12 - w * w)
    for _ in range(NEWTON - 1):
        q0 = jnp.minimum(a, m1)
        r0 = a - q0
        p2 = jnp.maximum(a - m2, 0.0)
        q2 = jnp.minimum(p2, m1)
        r2 = p2 - q2
        p3 = jnp.maximum(a - m3, 0.0)
        s3 = p3 * p3
        value = q0 * (q0 * q0 * THIRD + a * r0) - q2 * (q2 * q2 * THIRD + p2 * r2) - s3 * (p3 * THIRD) - both
        rate = q0 * (a + r0) - q2 * (p2 + r2) - s3
        a = a - value / rate
    return jnp.where(volume > 0.5, summed - a, a), lo, hi, slope_d, 0.5 / product


def cube_part(s, h):
    p = jnp.maximum(s, 0.0)
    q = jnp.minimum(p, h)
    r = p - q
    return q * (q * q * THIRD + p * r)


def flow(offset, lo, hi, slope_d, scale, c):
    signed = c * slope_d
    h = jnp.abs(signed)
    s = offset - jnp.where(signed < 0, jnp.abs(slope_d) - h, 0.0)
    t = s - hi
    return scale * ((cube_part(s, h) - cube_part(s - lo, h)) - (cube_part(t, h) - cube_part(t - lo, h)))


def rows(ref, where):
    parts = [ref[z, pl.ds(y, n)] for z, y, n in where]
    return parts[0] if len(parts) == 1 else jnp.concatenate(parts, axis=0)


def put(ref, where, value):
    start = 0
    for z, y, n in where:
        ref[z, pl.ds(y, n)] = value[start : start + n]
        start += n


def moved(where, dz, dy):
    return [(z + dz, y + dy, n) for z, y, n in where]


def loop(first, last, body):
    def step(i, carry):
        body(i)
        return carry

    lax.fori_loop(first, last, step, 0)


def pipelined(count, where_of, *stages):
    depth = len(stages)

    def run(i, live):
        for store in reversed([stages[k](where_of(i - k)) for k in live]):
            store()

    for i in range(depth - 1):
        run(i, range(i + 1))
    loop(depth - 1, count, lambda i: run(i, range(depth)))
    for i in range(count, count + depth - 1):
        run(i, range(i - count + 1, depth))


def kernel(
    f_hbm, vx_hbm, vy_hbm, vz_hbm, out_hbm, dt_out,
    f_ext, g1_ext, g2_ext, vx, vy, vz, vx_diff, smooth, diff, sum_y, dif_y, sum_d,
    off, lo, hi, slope, scale, face, edge_y, stat_a, stat_x, stat_z, dt_vec, out_buf,
    load_sem, out_sem, send_sem, recv_sem,
):
    gy, gz = lax.axis_index("gy"), lax.axis_index("gz")
    chip_z, chip_x = gy // RING, lax.rem(gy, RING)

    def neighbour(dy, dz):
        return {"gy": lax.rem(gy + dy + N_GY, N_GY), "gz": lax.rem(gz + dz + N_GZ, N_GZ)}

    def along_x(k):
        return {"gy": chip_z * RING + lax.rem(chip_x + k, RING), "gz": gz}

    def along_z(k):
        return {"gy": lax.rem(chip_z + k, RING) * RING + chip_x, "gz": gz}

    corners = [(1, 1), (1, -1), (-1, 1), (-1, -1)]
    own_z, own_y = pl.ds(Z0, NZ), pl.ds(Y0, NY)

    loads = []
    for source, target in ((f_hbm, f_ext), (vx_hbm, vx), (vy_hbm, vy), (vz_hbm, vz)):
        for y in range(NY):
            semaphore = load_sem.at[len(loads)]
            loads.append(pltpu.make_async_copy(source.at[:, :, y, :], target.at[own_z, Y0 + y], semaphore))
    for copy in loads:
        copy.start()
    barrier = pltpu.get_barrier_semaphore()
    greeted = [neighbour(0, k) for k in range(1, N_GZ)]
    greeted += [neighbour(1, 0), neighbour(-1, 0)] + [neighbour(*c) for c in corners]
    greeted += [along_x(k) for k in range(1, RING)] + [along_z(k) for k in range(1, RING)]
    for device in greeted:
        pl.semaphore_signal(barrier, inc=1, device_id=device, device_id_type=pl.DeviceIdType.MESH)

    def remote(source, target, k, device):
        return pltpu.make_async_remote_copy(
            src_ref=source, dst_ref=target, send_sem=send_sem.at[k], recv_sem=recv_sem.at[k],
            device_id=device, device_id_type=pl.DeviceIdType.MESH,
        )

    def halo(g, base, wide_z, wide_y):
        from_z = {1: pl.ds(Z1 - wide_z, wide_z), -1: pl.ds(Z0, wide_z), 0: own_z}
        from_y = {1: pl.ds(Y1 - wide_y, wide_y), -1: pl.ds(Y0, wide_y), 0: own_y}
        to_z = {1: pl.ds(Z0 - wide_z, wide_z), -1: pl.ds(Z1, wide_z), 0: own_z}
        to_y = {1: pl.ds(Y0 - wide_y, wide_y), -1: pl.ds(Y1, wide_y), 0: own_y}
        return [
            remote(g.at[from_z[dz], from_y[dy]], g.at[to_z[dz], to_y[dy]], base + k, neighbour(dy, dz))
            for k, (dy, dz) in enumerate([(1, 0), (-1, 0), (0, 1), (0, -1)] + corners)
        ]

    sent = []

    def send(copies):
        for copy in copies:
            copy.start()
        sent.extend(copies)

    def arrive(copies):
        for copy in copies:
            copy.wait_recv()

    for copy in loads:
        copy.wait()

    def scan(i, found):
        z = i + Z0
        peak, total = found
        g = f_ext[z, own_y]
        own = jnp.maximum(jnp.abs(vx[z, own_y]), jnp.abs(vy[z, own_y]))
        return jnp.maximum(peak, jnp.maximum(own, jnp.abs(vz[z, own_y]))), total + g * (1.0 - g)

    zeros = jnp.zeros((NY, J, LN), F32)
    peak, total = lax.fori_loop(0, NZ, scan, (zeros, zeros))
    first_row = lax.broadcasted_iota(jnp.int32, (J, LN), 0) == 0

    def stat_tile(peak_rows, total_rows):
        return jnp.where(
            first_row,
            jnp.broadcast_to(jnp.max(peak_rows, axis=0, keepdims=True), (J, LN)),
            jnp.broadcast_to(jnp.sum(total_rows, axis=0, keepdims=True), (J, LN)),
        )

    def combined(ref, n):
        top, add = ref[0], ref[0]
        for k in range(1, n):
            top, add = jnp.maximum(top, ref[k]), add + ref[k]
        return jnp.where(first_row, top, add)

    stat_a[gz] = stat_tile(jnp.max(peak, axis=0), jnp.sum(total, axis=0))

    pl.semaphore_wait(barrier, len(greeted))
    halo_f = halo(f_ext, HALO_F, 2, 2)
    halo_v = halo(vx, HALO_V, 1, 1)
    stats_a = [
        remote(stat_a.at[gz], stat_a.at[gz], STAT_A + k - 1, neighbour(0, k)) for k in range(1, N_GZ)
    ]
    stats_x = [
        remote(stat_x.at[chip_x], stat_x.at[chip_x], STAT_X + k - 1, along_x(k)) for k in range(1, RING)
    ]
    stats_z = [
        remote(stat_z.at[chip_z], stat_z.at[chip_z], STAT_Z + k - 1, along_z(k)) for k in range(1, RING)
    ]
    velocity = [
        remote(vy.at[own_z, Y1 - 1], vy.at[own_z, Y0 - 1], VEL, neighbour(1, 0)),
        remote(vz.at[Z1 - 1, own_y], vz.at[Z0 - 1, own_y], VEL + 1, neighbour(0, 1)),
    ]
    send(stats_a)
    send(halo_f)

    def put_shifts(g, where):
        before, after = at_prev(g), at_next(g)
        put(smooth, where, before + 2.0 * g + after)
        put(diff, where, after - before)

    def shift_rows(g_ext, where):
        put_shifts(rows(g_ext, where), where)

    def put_sums(z, y, n):
        s = smooth[z, pl.ds(y - 1, n + 2)]
        d = diff[z, pl.ds(y - 1, n + 2)]
        where = [(z, y, n)]
        put(sum_y, where, s[:-2] + 2.0 * s[1:-1] + s[2:])
        put(dif_y, where, s[2:] - s[:-2])
        put(sum_d, where, d[:-2] + 2.0 * d[1:-1] + d[2:])

    planes = (off, lo, hi, slope, scale)

    def planes_of(g_ext, dim):
        def stage(where):
            below, above = moved(where, -1, 0), moved(where, 1, 0)
            along_z = rows(sum_y, above) - rows(sum_y, below)
            along_y = rows(dif_y, below) + 2.0 * rows(dif_y, where) + rows(dif_y, above)
            along_x = rows(sum_d, below) + 2.0 * rows(sum_d, where) + rows(sum_d, above)
            slopes = [along_z, along_y, along_x]
            across = [slopes[k] for k in range(3) if k != dim]
            g = rows(g_ext, where)

            def store():
                for ref, value in zip(planes, plane(g, slopes[dim], *across)):
                    put(ref, where, value)

            return store

        return stage

    def put_planes(g_ext, dim, where):
        planes_of(g_ext, dim)(where)()

    def donors_x(where):
        found = [rows(ref, where) for ref in planes]
        q = rows(vx, where)
        others = [at_next(value) for value in found]
        before = at_prev(q)

        def store():
            upward = q > 0
            others[-1] = -others[-1]
            for ref, value, other in zip(planes, found, others):
                put(ref, where, jnp.where(upward, value, other))
            put(vx_diff, where, q - before)

        return store

    def donors(upward, here, there):
        picked = [jnp.where(upward, rows(ref, here), rows(ref, there)) for ref in planes[:-1]]
        return picked + [jnp.where(upward, rows(scale, here), -rows(scale, there))]

    inner = (Y0 + 1, NY - 2)

    loop(0, NZ // 2, lambda i: shift_rows(f_ext, [(Z0 + 2 * i, Y0, NY), (Z0 + 2 * i + 1, Y0, NY)]))
    loop(Z0, Z1, lambda z: put_sums(z, *inner))
    pipelined(NZ - 2, lambda i: [(Z0 + 1 + i, *inner)], planes_of(f_ext, 2), donors_x)
    arrive(stats_a)
    stat_x[chip_x] = combined(stat_a, N_GZ)
    arrive(halo_f[:2])
    send(stats_x)
    send(halo_v)
    send(velocity)

    def shift_sides(i):
        z = Z0 + 2 * i
        shift_rows(f_ext, [(z, 0, 2), (z, Y1, 2), (z + 1, 0, 2), (z + 1, Y1, 2)])

    def shift_ends(i):
        z = i + (i // 2) * (EZ - 4)
        shift_rows(f_ext, [(z, 0, EY)])

    def sums_side(z):
        put_sums(z, 1, 2)
        put_sums(z, Y1 - 1, 2)

    loop(0, NZ // 2, shift_sides)
    arrive(halo_f[2:])
    loop(0, 4, shift_ends)
    loop(Z0, Z1, sums_side)
    loop(0, 4, lambda i: put_sums(i + (i // 2) * (EZ - 4), 1, EY - 2))
    arrive(stats_x)
    stat_z[chip_z] = combined(stat_x, RING)

    def sides(i):
        z = 1 + 2 * i
        return [(z, 1, 2), (z, Y1 - 1, 2), (z + 1, 1, 2), (z + 1, Y1 - 1, 2)]

    def ends(i):
        return [(1 + i + (i // 2) * (NZ - 2), *inner)]

    loop(0, 4, lambda i: put_planes(f_ext, 2, ends(i)))
    send(stats_z)
    arrive(halo_v)
    loop(0, 4, lambda i: donors_x(ends(i))())
    pipelined(NZ // 2 + 1, sides, planes_of(f_ext, 2), donors_x)
    arrive(stats_z)
    arrive(velocity)
    stats = combined(stat_z, RING)
    umax = jnp.max(stats[0:1], axis=1, keepdims=True)
    share = jnp.sum(stats[1:2], axis=1, keepdims=True) * (4.0 / (N_GZ * NZ * N_GY * NY * J * LN))
    step = COURANT / ((umax + EPSILON) * (1.0 + share))
    dt_vec[...] = jnp.broadcast_to(step, (J, LN))
    dt_out[0, 0] = jnp.max(step)

    def flow_x(where):
        found = [rows(ref, where) for ref in planes]
        q = rows(vx, where)
        return lambda: put(face, where, flow(*found, dt_vec[...] * q))

    def update_x(where):
        out = rows(face, where)
        before = at_prev(out)
        g, change = rows(f_ext, where), rows(vx_diff, where)
        return lambda: put(g1_ext, where, (g - out + before) / (1.0 - dt_vec[...] * change))

    def shifts_of(g_ext):
        def stage(where):
            g = rows(g_ext, where)
            before, after = at_prev(g), at_next(g)

            def store():
                put(smooth, where, before + 2.0 * g + after)
                put(diff, where, after - before)

            return store

        return stage

    x_stages = (flow_x, update_x, shifts_of(g1_ext))
    pipelined(NZ + 2, lambda i: [(1 + i, 1, 3), (1 + i, Y1 - 2, 3)], *x_stages)

    def sums_edge(z):
        put_sums(z, Y0, 1)
        put_sums(z, Y1 - 1, 1)

    def y_edge(i):
        z = Z0 + 2 * i
        return [(z, Y0, 1), (z, Y1 - 1, 1), (z + 1, Y0, 1), (z + 1, Y1 - 1, 1)]

    def half_faces_y(i):
        z = Z0 + 2 * i
        at_face = [(z, Y0 - 1, 1), (z, Y1 - 1, 1), (z + 1, Y0 - 1, 1), (z + 1, Y1 - 1, 1)]
        c = dt_vec[...] * rows(vy, at_face)
        out = flow(*[rows(ref, y_edge(i)) for ref in planes], c)
        for k in range(2):
            edge_y[0, 2 * i + k] = jnp.where(c[2 * k + 1] > 0, out[2 * k + 1], 0.0)
            edge_y[1, 2 * i + k] = jnp.where(c[2 * k] < 0, out[2 * k], 0.0)

    flux_y = [
        remote(edge_y.at[0], edge_y.at[2], FLUX_Y, neighbour(1, 0)),
        remote(edge_y.at[1], edge_y.at[3], FLUX_Y + 1, neighbour(-1, 0)),
    ]
    loop(Z0 - 1, Z1 + 1, sums_edge)
    loop(0, NZ // 2, lambda i: put_planes(g1_ext, 1, y_edge(i)))
    loop(0, NZ // 2, half_faces_y)
    send(flux_y)

    def middle(i):
        return [(1 + 2 * i, Y0 + 2, NY - 4), (2 + 2 * i, Y0 + 2, NY - 4)]

    def faces_y(z):
        c = dt_vec[...] * vy[z, pl.ds(Y0, NY - 1)]
        picked = donors(c > 0, [(z, Y0, NY - 1)], [(z, Y0 + 1, NY - 1)])
        put(face, [(z, Y0, NY - 1)], flow(*picked, c))

    pipelined(NZ // 2 + 1, middle, *x_stages)
    loop(Z0 - 1, Z1 + 1, lambda z: put_sums(z, *inner))
    loop(Z0, Z1, lambda z: put_planes(g1_ext, 1, [(z, *inner)]))
    loop(Z0, Z1, faces_y)
    arrive(flux_y)

    def update_y(z):
        face[z, Y0 - 1] = edge_y[2, z - Z0] - edge_y[1, z - Z0]
        face[z, Y1 - 1] = edge_y[0, z - Z0] - edge_y[3, z - Z0]
        out, q = face[z, pl.ds(Y0 - 1, NY + 1)], vy[z, pl.ds(Y0 - 1, NY + 1)]
        g2_ext[z, own_y] = (g1_ext[z, own_y] - out[1:] + out[:-1]) / (1.0 - dt_vec[...] * (q[1:] - q[:-1]))

    loop(Z0, Z1, update_y)
    halo_g = halo(g2_ext, HALO_G, 2, 1)

    def faces_z(where):
        c = dt_vec[...] * rows(vz, where)
        put(face, where, flow(*donors(c > 0, where, moved(where, 1, 0)), c))

    loop(0, 1, lambda i: shift_rows(g2_ext, [(Z0 + 2 * i, Y0, NY), (Z0 + 2 * i + 1, Y0, NY)]))
    send(halo_g)
    loop(1, NZ // 2, lambda i: shift_rows(g2_ext, [(Z0 + 2 * i, Y0, NY), (Z0 + 2 * i + 1, Y0, NY)]))
    loop(Z0, Z1, lambda z: put_sums(z, *inner))
    loop(Z0 + 1, Z1 - 1, lambda z: put_planes(g2_ext, 0, [(z, *inner)]))
    loop(Z0 + 1, Z1 - 2, lambda z: faces_z([(z, *inner)]))
    arrive(halo_g)

    def shift_sides_g(i):
        z = Z0 + 4 * i
        shift_rows(g2_ext, [w for k in range(4) for w in ((z + k, Y0 - 1, 1), (z + k, Y1, 1))])

    def z_sides(i):
        z = 1 + 2 * i
        return [(z, Y0, 1), (z, Y1 - 1, 1), (z + 1, Y0, 1), (z + 1, Y1 - 1, 1)]

    loop(0, NZ // 4, shift_sides_g)
    loop(0, 4, lambda i: shift_rows(g2_ext, [(i + (i // 2) * (EZ - 4), 1, EY - 2)]))
    loop(Z0, Z1, sums_edge)
    loop(0, 4, lambda i: put_sums(i + (i // 2) * (EZ - 4), Y0, NY))
    loop(0, NZ // 2 + 1, lambda i: put_planes(g2_ext, 0, z_sides(i)))
    loop(0, 4, lambda i: put_planes(g2_ext, 0, ends(i)))
    loop(0, NZ // 2, lambda i: faces_z(z_sides(i)))
    faces_z([(Z1 - 1, Y0, 1), (Z1 - 1, Y1 - 1, 1)])
    loop(0, 4, lambda i: faces_z([(1 + i + (i // 2) * (NZ - 3), *inner)]))

    def update_z(z):
        g = g2_ext[z, own_y] - face[z, own_y] + face[z - 1, own_y]
        out_buf[z - Z0] = g / (1.0 - dt_vec[...] * (vz[z, own_y] - vz[z - 1, own_y]))

    loop(Z0, Z1, update_z)
    stores = [
        pltpu.make_async_copy(out_buf.at[:, y], out_hbm.at[:, :, y, :], out_sem.at[y]) for y in range(NY)
    ]
    for copy in stores:
        copy.start()
    for copy in sent:
        copy.wait_send()
    for copy in stores:
        copy.wait()


def shards(*blocks):
    tiled = [b.reshape(NZ, NY, J, LN).transpose(0, 2, 1, 3) for b in blocks]
    row = (J, LN)
    ext = pltpu.VMEM((EZ, EY, *row), F32)
    anywhere = pl.BlockSpec(memory_space=pl.ANY)
    field, step = pl.pallas_call(
        kernel,
        out_shape=(jax.ShapeDtypeStruct((NZ, J, NY, LN), F32), jax.ShapeDtypeStruct((1, 1), F32)),
        in_specs=[anywhere] * 4,
        out_specs=(anywhere, pl.BlockSpec(memory_space=pltpu.SMEM)),
        scratch_shapes=[ext] * 18 + [
            pltpu.VMEM((4, NZ, *row), F32),
            pltpu.VMEM((N_GZ, *row), F32), pltpu.VMEM((RING, *row), F32), pltpu.VMEM((RING, *row), F32),
            pltpu.VMEM(row, F32), pltpu.VMEM((NZ, NY, *row), F32),
            pltpu.SemaphoreType.DMA((4 * NY,)), pltpu.SemaphoreType.DMA((NY,)),
            pltpu.SemaphoreType.DMA((N_SEMS,)), pltpu.SemaphoreType.DMA((N_SEMS,)),
        ],
        compiler_params=pltpu.CompilerParams(collective_id=0, has_side_effects=True),
        name="advect",
    )(*tiled)
    return field.transpose(0, 2, 1, 3).reshape(NZ, NY, J * LN), step.reshape(())


def solution(mesh):
    spec = P("gz", "gy", None)
    return jax.shard_map(shards, mesh=mesh, in_specs=(spec,) * 4, out_specs=(spec, P()), check_vma=False)
```

time: 54.5 us -> 48.8 us (0.90)
  Pallas kernels: 49.9 us -> 44.3 us
    pallas_call x1, Pallas kernels: 49.9 us -> 44.3 us  [shards(): pl.pallas_call(kernel, out_shape=(jax.ShapeDtypeStruct((NZ, J, NY, LN), F...]
where the time goes in v2:
time: 48.8 us; the launch traced here: 48.5 us
  Pallas kernels  44.3 us (91%)
  between operations  2.34 us (5%)
  local copies, waits for them, and re-layouts  1.89 us (4%)
    pallas_call x1, Pallas kernels, shards(): pl.pallas_call(kernel, out_shape=(jax.ShapeDtypeStruct((NZ, J, NY, LN), F...  44.3 us
    unnamed x1, local copies, waits for them, and re-layouts  1.89 us

profile of v2, /device:TPU:1, one launch (start us, length us, event | category | flops | bytes accessed | tf_op | source)
XLA Modules:
  0.0 48.5 jit_solution(11419985179268098464)
XLA Ops:
  0.6 44.3 %advect.1 = (f32[16,8,8,128]{3,2,1,0:T(8,128)}, f32[1,1]{1,0:T(1,128)}) custom-call(f32[16,8,8,128]{3,2,1,0:T(8,128)} %bitcast.17, f32[16,8,8,128]{3,2,1,0:T(8,128)} %bitcast.18, f32[16,8,8,128]{3,2,1,0:T(8,128)} %bitcast.19, f32[16,8,8,128]{3,2,1,0:T(8,128)} %bitcast.20), custom_call_target="tpu_custom_call" | custom-call | tf_op jit(solution)/shard_map/advect/pallas_call | solution.py:479
  44.9 1.9 %copy.8 = f32[16,8,1024]{2,1,0:T(8,128)} copy(f32[16,8,1024]{2,1,0:T(8,128)} %bitcast.16) | data formatting | bytes 1048576

commit v3 on v2

--- a/solution.py
+++ b/solution.py
@@ -131,7 +131,7 @@
 def kernel(
     f_hbm, vx_hbm, vy_hbm, vz_hbm, out_hbm, dt_out,
     f_ext, g1_ext, g2_ext, vx, vy, vz, vx_diff, smooth, diff, sum_y, dif_y, sum_d,
-    off, lo, hi, slope, scale, face, edge_y, stat_a, stat_x, stat_z, dt_vec, out_buf,
+    off, lo, hi, slope, scale, face, edge_y, stat_a, stat_x, stat_z, dt_vec, dt_cell, out_buf,
     load_sem, out_sem, send_sem, recv_sem,
 ):
     gy, gz = lax.axis_index("gy"), lax.axis_index("gz")
@@ -217,7 +217,7 @@
             top, add = jnp.maximum(top, ref[k]), add + ref[k]
         return jnp.where(first_row, top, add)
 
-    stat_a[gz] = stat_tile(jnp.max(peak, axis=0), jnp.sum(total, axis=0))
+    stat_x[chip_x] = stat_tile(jnp.max(peak, axis=0), jnp.sum(total, axis=0))
 
     pl.semaphore_wait(barrier, len(greeted))
     halo_f = halo(f_ext, HALO_F, 2, 2)
@@ -235,8 +235,10 @@
         remote(vy.at[own_z, Y1 - 1], vy.at[own_z, Y0 - 1], VEL, neighbour(1, 0)),
         remote(vz.at[Z1 - 1, own_y], vz.at[Z0 - 1, own_y], VEL + 1, neighbour(0, 1)),
     ]
-    send(stats_a)
+    send(stats_x)
     send(halo_f)
+    send(halo_v)
+    send(velocity)
 
     def put_shifts(g, where):
         before, after = at_prev(g), at_next(g)
@@ -246,13 +248,20 @@
     def shift_rows(g_ext, where):
         put_shifts(rows(g_ext, where), where)
 
-    def put_sums(z, y, n):
+    def sums_of(z, y, n):
         s = smooth[z, pl.ds(y - 1, n + 2)]
         d = diff[z, pl.ds(y - 1, n + 2)]
-        where = [(z, y, n)]
-        put(sum_y, where, s[:-2] + 2.0 * s[1:-1] + s[2:])
-        put(dif_y, where, s[2:] - s[:-2])
-        put(sum_d, where, d[:-2] + 2.0 * d[1:-1] + d[2:])
+
+        def store():
+            where = [(z, y, n)]
+            put(sum_y, where, s[:-2] + 2.0 * s[1:-1] + s[2:])
+            put(dif_y, where, s[2:] - s[:-2])
+            put(sum_d, where, d[:-2] + 2.0 * d[1:-1] + d[2:])
+
+        return store
+
+    def put_sums(z, y, n):
+        sums_of(z, y, n)()
 
     planes = (off, lo, hi, slope, scale)
 
@@ -298,15 +307,18 @@
 
     inner = (Y0 + 1, NY - 2)
 
+    def x_inner(first, count):
+        pipelined(count, lambda i: [(first + i, *inner)], planes_of(f_ext, 2), donors_x)
+
     loop(0, NZ // 2, lambda i: shift_rows(f_ext, [(Z0 + 2 * i, Y0, NY), (Z0 + 2 * i + 1, Y0, NY)]))
     loop(Z0, Z1, lambda z: put_sums(z, *inner))
-    pipelined(NZ - 2, lambda i: [(Z0 + 1 + i, *inner)], planes_of(f_ext, 2), donors_x)
-    arrive(stats_a)
-    stat_x[chip_x] = combined(stat_a, N_GZ)
+    x_inner(Z0 + 1, 6)
+    arrive(stats_x)
+    stat_z[chip_z] = combined(stat_x, RING)
+    x_inner(Z0 + 7, 2)
+    send(stats_z)
+    x_inner(Z0 + 9, NZ - 10)
     arrive(halo_f[:2])
-    send(stats_x)
-    send(halo_v)
-    send(velocity)
 
     def shift_sides(i):
         z = Z0 + 2 * i
@@ -325,9 +337,6 @@
     loop(0, 4, shift_ends)
     loop(Z0, Z1, sums_side)
     loop(0, 4, lambda i: put_sums(i + (i // 2) * (EZ - 4), 1, EY - 2))
-    arrive(stats_x)
-    stat_z[chip_z] = combined(stat_x, RING)
-
     def sides(i):
         z = 1 + 2 * i
         return [(z, 1, 2), (z, Y1 - 1, 2), (z + 1, 1, 2), (z + 1, Y1 - 1, 2)]
@@ -335,19 +344,21 @@
     def ends(i):
         return [(1 + i + (i // 2) * (NZ - 2), *inner)]
 
+    arrive(stats_z)
+    stat_a[gz] = combined(stat_z, RING)
     loop(0, 4, lambda i: put_planes(f_ext, 2, ends(i)))
-    send(stats_z)
+    send(stats_a)
     arrive(halo_v)
     loop(0, 4, lambda i: donors_x(ends(i))())
     pipelined(NZ // 2 + 1, sides, planes_of(f_ext, 2), donors_x)
-    arrive(stats_z)
+    arrive(stats_a)
     arrive(velocity)
-    stats = combined(stat_z, RING)
+    stats = combined(stat_a, N_GZ)
     umax = jnp.max(stats[0:1], axis=1, keepdims=True)
     share = jnp.sum(stats[1:2], axis=1, keepdims=True) * (4.0 / (N_GZ * NZ * N_GY * NY * J * LN))
     step = COURANT / ((umax + EPSILON) * (1.0 + share))
     dt_vec[...] = jnp.broadcast_to(step, (J, LN))
-    dt_out[0, 0] = jnp.max(step)
+    dt_cell[...] = step
 
     def flow_x(where):
         found = [rows(ref, where) for ref in planes]
@@ -373,8 +384,11 @@
 
         return stage
 
+    dt_copy = pltpu.make_async_copy(dt_cell, dt_out, out_sem.at[NY])
     x_stages = (flow_x, update_x, shifts_of(g1_ext))
     pipelined(NZ + 2, lambda i: [(1 + i, 1, 3), (1 + i, Y1 - 2, 3)], *x_stages)
+
+    dt_copy.start()
 
     def sums_edge(z):
         put_sums(z, Y0, 1)
@@ -411,8 +425,15 @@
         put(face, [(z, Y0, NY - 1)], flow(*picked, c))
 
     pipelined(NZ // 2 + 1, middle, *x_stages)
-    loop(Z0 - 1, Z1 + 1, lambda z: put_sums(z, *inner))
-    loop(Z0, Z1, lambda z: put_planes(g1_ext, 1, [(z, *inner)]))
+    loop(Z0 - 1, Z0 + 2, lambda z: put_sums(z, *inner))
+
+    def y_inner(z):
+        stores = planes_of(g1_ext, 1)([(z, *inner)]), sums_of(z + 2, *inner)
+        for store in stores:
+            store()
+
+    loop(Z0, Z1 - 1, y_inner)
+    put_planes(g1_ext, 1, [(Z1 - 1, *inner)])
     loop(Z0, Z1, faces_y)
     arrive(flux_y)
 
@@ -429,11 +450,23 @@
         c = dt_vec[...] * rows(vz, where)
         put(face, where, flow(*donors(c > 0, where, moved(where, 1, 0)), c))
 
-    loop(0, 1, lambda i: shift_rows(g2_ext, [(Z0 + 2 * i, Y0, NY), (Z0 + 2 * i + 1, Y0, NY)]))
+    shift_rows(g2_ext, [(Z0, Y0, NY), (Z0 + 1, Y0, NY)])
     send(halo_g)
-    loop(1, NZ // 2, lambda i: shift_rows(g2_ext, [(Z0 + 2 * i, Y0, NY), (Z0 + 2 * i + 1, Y0, NY)]))
-    loop(Z0, Z1, lambda z: put_sums(z, *inner))
-    loop(Z0 + 1, Z1 - 1, lambda z: put_planes(g2_ext, 0, [(z, *inner)]))
+    shift_rows(g2_ext, [(Z0 + 2, Y0, NY), (Z0 + 3, Y0, NY)])
+    loop(Z0, Z0 + 3, lambda z: put_sums(z, *inner))
+
+    def z_inner(z):
+        stores = (
+            shifts_of(g2_ext)([(z + 3, Y0, NY)]),
+            planes_of(g2_ext, 0)([(z, *inner)]),
+            sums_of(z + 2, *inner),
+        )
+        for store in reversed(stores):
+            store()
+
+    loop(Z0 + 1, Z1 - 3, z_inner)
+    put_sums(Z1 - 1, *inner)
+    loop(Z1 - 3, Z1 - 1, lambda z: put_planes(g2_ext, 0, [(z, *inner)]))
     loop(Z0 + 1, Z1 - 2, lambda z: faces_z([(z, *inner)]))
     arrive(halo_g)
 
@@ -467,7 +500,7 @@
         copy.start()
     for copy in sent:
         copy.wait_send()
-    for copy in stores:
+    for copy in [*stores, dt_copy]:
         copy.wait()
 
 
@@ -480,12 +513,12 @@
         kernel,
         out_shape=(jax.ShapeDtypeStruct((NZ, J, NY, LN), F32), jax.ShapeDtypeStruct((1, 1), F32)),
         in_specs=[anywhere] * 4,
-        out_specs=(anywhere, pl.BlockSpec(memory_space=pltpu.SMEM)),
+        out_specs=(anywhere, anywhere),
         scratch_shapes=[ext] * 18 + [
             pltpu.VMEM((4, NZ, *row), F32),
             pltpu.VMEM((N_GZ, *row), F32), pltpu.VMEM((RING, *row), F32), pltpu.VMEM((RING, *row), F32),
-            pltpu.VMEM(row, F32), pltpu.VMEM((NZ, NY, *row), F32),
-            pltpu.SemaphoreType.DMA((4 * NY,)), pltpu.SemaphoreType.DMA((NY,)),
+            pltpu.VMEM(row, F32), pltpu.VMEM((1, 1), F32), pltpu.VMEM((NZ, NY, *row), F32),
+            pltpu.SemaphoreType.DMA((4 * NY,)), pltpu.SemaphoreType.DMA((NY + 1,)),
             pltpu.SemaphoreType.DMA((N_SEMS,)), pltpu.SemaphoreType.DMA((N_SEMS,)),
         ],
         compiler_params=pltpu.CompilerParams(collective_id=0, has_side_effects=True),

time: 48.8 us -> 46.5 us (0.953)
  Pallas kernels: 44.3 us -> 42 us
    pallas_call x1, Pallas kernels: 44.3 us -> 42 us  [shards(): pl.pallas_call(kernel, out_shape=(jax.ShapeDtypeStruct((NZ, J, NY, LN), F...]
where the time goes in v3:
time: 46.5 us; the launch traced here: 46.2 us
  Pallas kernels  42 us (90%)
  between operations  2.34 us (5%)
  local copies, waits for them, and re-layouts  1.89 us (4%)
    pallas_call x1, Pallas kernels, shards(): pl.pallas_call(kernel, out_shape=(jax.ShapeDtypeStruct((NZ, J, NY, LN), F...  42 us
    unnamed x1, local copies, waits for them, and re-layouts  1.89 us

profile of v3, /device:TPU:1, one launch (start us, length us, event | category | flops | bytes accessed | tf_op | source)
XLA Modules:
  0.0 46.2 jit_solution(675590726330321423)
XLA Ops:
  0.6 42.0 %advect.1 = (f32[16,8,8,128]{3,2,1,0:T(8,128)}, f32[1,1]{1,0:T(1,128)}) custom-call(f32[16,8,8,128]{3,2,1,0:T(8,128)} %bitcast.17, f32[16,8,8,128]{3,2,1,0:T(8,128)} %bitcast.18, f32[16,8,8,128]{3,2,1,0:T(8,128)} %bitcast.19, f32[16,8,8,128]{3,2,1,0:T(8,128)} %bitcast.20), custom_call_target="tpu_custom_call" | custom-call | tf_op jit(solution)/shard_map/advect/pallas_call | solution.py:512
  42.7 1.9 %copy.8 = f32[16,8,1024]{2,1,0:T(8,128)} copy(f32[16,8,1024]{2,1,0:T(8,128)} %bitcast.16) | data formatting | bytes 1048576

commit v4 on v3

--- a/solution.py
+++ b/solution.py
@@ -14,7 +14,6 @@
 
 NZ, NY, J, LN = 16, 8, 8, 128
 N_GY, N_GZ = 16, 8
-RING = 4
 F32 = jnp.float32
 
 EZ, EY = NZ + 4, NY + 4
@@ -24,10 +23,9 @@
 HALO_F, HALO_V, HALO_G = 0, 8, 16
 VEL = 24
 FLUX_Y = 26
-STAT_A = 28
-STAT_X = 35
-STAT_Z = 38
-N_SEMS = 41
+STAT_Y = 28
+STAT_Z = STAT_Y + N_GY - 1
+N_SEMS = STAT_Z + N_GZ - 1
 
 
 def lanes(u):
@@ -52,8 +50,7 @@
     tilt_d = jnp.abs(slope_d)
     m1, rest = jnp.minimum(lo, tilt_d), jnp.maximum(lo, tilt_d)
     m2, m3 = jnp.minimum(rest, hi), jnp.maximum(rest, hi)
-    volume = jnp.clip(g, 0.0, 1.0)
-    lesser = jnp.minimum(volume, 1.0 - volume)
+    lesser = jnp.maximum(jnp.minimum(g, 1.0 - g), 0.0)
     m12 = m1 * m2
     product = m12 * m3
     target = lesser * product
@@ -72,7 +69,7 @@
         value = q0 * (q0 * q0 * THIRD + a * r0) - q2 * (q2 * q2 * THIRD + p2 * r2) - s3 * (p3 * THIRD) - both
         rate = q0 * (a + r0) - q2 * (p2 + r2) - s3
         a = a - value / rate
-    return jnp.where(volume > 0.5, summed - a, a), lo, hi, slope_d, 0.5 / product
+    return jnp.where(g > 0.5, summed - a, a), lo, hi, slope_d, 0.5 / product
 
 
 def cube_part(s, h):
@@ -131,20 +128,13 @@
 def kernel(
     f_hbm, vx_hbm, vy_hbm, vz_hbm, out_hbm, dt_out,
     f_ext, g1_ext, g2_ext, vx, vy, vz, vx_diff, smooth, diff, sum_y, dif_y, sum_d,
-    off, lo, hi, slope, scale, face, edge_y, stat_a, stat_x, stat_z, dt_vec, dt_cell, out_buf,
+    off, lo, hi, slope, scale, face, edge_y, stat_y, stat_z, dt_vec, dt_cell, out_buf,
     load_sem, out_sem, send_sem, recv_sem,
 ):
     gy, gz = lax.axis_index("gy"), lax.axis_index("gz")
-    chip_z, chip_x = gy // RING, lax.rem(gy, RING)
 
     def neighbour(dy, dz):
         return {"gy": lax.rem(gy + dy + N_GY, N_GY), "gz": lax.rem(gz + dz + N_GZ, N_GZ)}
-
-    def along_x(k):
-        return {"gy": chip_z * RING + lax.rem(chip_x + k, RING), "gz": gz}
-
-    def along_z(k):
-        return {"gy": lax.rem(chip_z + k, RING) * RING + chip_x, "gz": gz}
 
     corners = [(1, 1), (1, -1), (-1, 1), (-1, -1)]
     own_z, own_y = pl.ds(Z0, NZ), pl.ds(Y0, NY)
@@ -158,8 +148,7 @@
         copy.start()
     barrier = pltpu.get_barrier_semaphore()
     greeted = [neighbour(0, k) for k in range(1, N_GZ)]
-    greeted += [neighbour(1, 0), neighbour(-1, 0)] + [neighbour(*c) for c in corners]
-    greeted += [along_x(k) for k in range(1, RING)] + [along_z(k) for k in range(1, RING)]
+    greeted += [neighbour(k, 0) for k in range(1, N_GY)] + [neighbour(*c) for c in corners]
     for device in greeted:
         pl.semaphore_signal(barrier, inc=1, device_id=device, device_id_type=pl.DeviceIdType.MESH)
 
@@ -202,40 +191,27 @@
 
     zeros = jnp.zeros((NY, J, LN), F32)
     peak, total = lax.fori_loop(0, NZ, scan, (zeros, zeros))
-    first_row = lax.broadcasted_iota(jnp.int32, (J, LN), 0) == 0
-
-    def stat_tile(peak_rows, total_rows):
-        return jnp.where(
-            first_row,
-            jnp.broadcast_to(jnp.max(peak_rows, axis=0, keepdims=True), (J, LN)),
-            jnp.broadcast_to(jnp.sum(total_rows, axis=0, keepdims=True), (J, LN)),
-        )
+    top_row = lax.broadcasted_iota(jnp.int32, (2, LN), 0) == 0
 
     def combined(ref, n):
         top, add = ref[0], ref[0]
         for k in range(1, n):
             top, add = jnp.maximum(top, ref[k]), add + ref[k]
-        return jnp.where(first_row, top, add)
-
-    stat_x[chip_x] = stat_tile(jnp.max(peak, axis=0), jnp.sum(total, axis=0))
+        return jnp.where(top_row, top, add)
+
+    top, add = jnp.max(peak, axis=0), jnp.sum(total, axis=0)
+    stat_y[gy] = jnp.concatenate([jnp.max(top, axis=0, keepdims=True), jnp.sum(add, axis=0, keepdims=True)], axis=0)
 
     pl.semaphore_wait(barrier, len(greeted))
     halo_f = halo(f_ext, HALO_F, 2, 2)
     halo_v = halo(vx, HALO_V, 1, 1)
-    stats_a = [
-        remote(stat_a.at[gz], stat_a.at[gz], STAT_A + k - 1, neighbour(0, k)) for k in range(1, N_GZ)
-    ]
-    stats_x = [
-        remote(stat_x.at[chip_x], stat_x.at[chip_x], STAT_X + k - 1, along_x(k)) for k in range(1, RING)
-    ]
-    stats_z = [
-        remote(stat_z.at[chip_z], stat_z.at[chip_z], STAT_Z + k - 1, along_z(k)) for k in range(1, RING)
-    ]
+    stats_y = [remote(stat_y.at[gy], stat_y.at[gy], STAT_Y + k - 1, neighbour(k, 0)) for k in range(1, N_GY)]
+    stats_z = [remote(stat_z.at[gz], stat_z.at[gz], STAT_Z + k - 1, neighbour(0, k)) for k in range(1, N_GZ)]
     velocity = [
         remote(vy.at[own_z, Y1 - 1], vy.at[own_z, Y0 - 1], VEL, neighbour(1, 0)),
         remote(vz.at[Z1 - 1, own_y], vz.at[Z0 - 1, own_y], VEL + 1, neighbour(0, 1)),
     ]
-    send(stats_x)
+    send(stats_y)
     send(halo_f)
     send(halo_v)
     send(velocity)
@@ -312,12 +288,11 @@
 
     loop(0, NZ // 2, lambda i: shift_rows(f_ext, [(Z0 + 2 * i, Y0, NY), (Z0 + 2 * i + 1, Y0, NY)]))
     loop(Z0, Z1, lambda z: put_sums(z, *inner))
-    x_inner(Z0 + 1, 6)
-    arrive(stats_x)
-    stat_z[chip_z] = combined(stat_x, RING)
-    x_inner(Z0 + 7, 2)
+    x_inner(Z0 + 1, 9)
+    arrive(stats_y)
+    stat_z[gz] = combined(stat_y, N_GY)
     send(stats_z)
-    x_inner(Z0 + 9, NZ - 10)
+    x_inner(Z0 + 10, NZ - 11)
     arrive(halo_f[:2])
 
     def shift_sides(i):
@@ -344,16 +319,13 @@
     def ends(i):
         return [(1 + i + (i // 2) * (NZ - 2), *inner)]
 
-    arrive(stats_z)
-    stat_a[gz] = combined(stat_z, RING)
     loop(0, 4, lambda i: put_planes(f_ext, 2, ends(i)))
-    send(stats_a)
     arrive(halo_v)
     loop(0, 4, lambda i: donors_x(ends(i))())
     pipelined(NZ // 2 + 1, sides, planes_of(f_ext, 2), donors_x)
-    arrive(stats_a)
+    arrive(stats_z)
     arrive(velocity)
-    stats = combined(stat_a, N_GZ)
+    stats = combined(stat_z, N_GZ)
     umax = jnp.max(stats[0:1], axis=1, keepdims=True)
     share = jnp.sum(stats[1:2], axis=1, keepdims=True) * (4.0 / (N_GZ * NZ * N_GY * NY * J * LN))
     step = COURANT / ((umax + EPSILON) * (1.0 + share))
@@ -386,45 +358,49 @@
 
     dt_copy = pltpu.make_async_copy(dt_cell, dt_out, out_sem.at[NY])
     x_stages = (flow_x, update_x, shifts_of(g1_ext))
-    pipelined(NZ + 2, lambda i: [(1 + i, 1, 3), (1 + i, Y1 - 2, 3)], *x_stages)
+    pipelined(
+        NZ // 2 + 1,
+        lambda i: [w for z in (1 + 2 * i, 2 + 2 * i) for w in ((z, 1, 3), (z, Y1 - 2, 3))],
+        *x_stages,
+    )
 
     dt_copy.start()
 
-    def sums_edge(z):
-        put_sums(z, Y0, 1)
-        put_sums(z, Y1 - 1, 1)
-
-    def y_edge(i):
-        z = Z0 + 2 * i
-        return [(z, Y0, 1), (z, Y1 - 1, 1), (z + 1, Y0, 1), (z + 1, Y1 - 1, 1)]
+    def sums_edge(first, n):
+        for z in range(n):
+            put_sums(first + z, Y0, 1)
+            put_sums(first + z, Y1 - 1, 1)
+
+    def edges(first, n):
+        return [w for k in range(n) for w in ((first + k, Y0, 1), (first + k, Y1 - 1, 1))]
 
     def half_faces_y(i):
-        z = Z0 + 2 * i
-        at_face = [(z, Y0 - 1, 1), (z, Y1 - 1, 1), (z + 1, Y0 - 1, 1), (z + 1, Y1 - 1, 1)]
+        z = Z0 + 4 * i
+        at_face = [w for k in range(4) for w in ((z + k, Y0 - 1, 1), (z + k, Y1 - 1, 1))]
         c = dt_vec[...] * rows(vy, at_face)
-        out = flow(*[rows(ref, y_edge(i)) for ref in planes], c)
-        for k in range(2):
-            edge_y[0, 2 * i + k] = jnp.where(c[2 * k + 1] > 0, out[2 * k + 1], 0.0)
-            edge_y[1, 2 * i + k] = jnp.where(c[2 * k] < 0, out[2 * k], 0.0)
+        out = flow(*[rows(ref, edges(z, 4)) for ref in planes], c)
+        for k in range(4):
+            edge_y[0, 4 * i + k] = jnp.where(c[2 * k + 1] > 0, out[2 * k + 1], 0.0)
+            edge_y[1, 4 * i + k] = jnp.where(c[2 * k] < 0, out[2 * k], 0.0)
 
     flux_y = [
         remote(edge_y.at[0], edge_y.at[2], FLUX_Y, neighbour(1, 0)),
         remote(edge_y.at[1], edge_y.at[3], FLUX_Y + 1, neighbour(-1, 0)),
     ]
-    loop(Z0 - 1, Z1 + 1, sums_edge)
-    loop(0, NZ // 2, lambda i: put_planes(g1_ext, 1, y_edge(i)))
-    loop(0, NZ // 2, half_faces_y)
+    loop(0, (NZ + 2) // 3, lambda i: sums_edge(Z0 - 1 + 3 * i, 3))
+    loop(0, NZ // 4, lambda i: put_planes(g1_ext, 1, edges(Z0 + 4 * i, 4)))
+    loop(0, NZ // 4, half_faces_y)
     send(flux_y)
 
     def middle(i):
-        return [(1 + 2 * i, Y0 + 2, NY - 4), (2 + 2 * i, Y0 + 2, NY - 4)]
+        return [(1 + 3 * i + k, Y0 + 2, NY - 4) for k in range(3)]
 
     def faces_y(z):
         c = dt_vec[...] * vy[z, pl.ds(Y0, NY - 1)]
         picked = donors(c > 0, [(z, Y0, NY - 1)], [(z, Y0 + 1, NY - 1)])
         put(face, [(z, Y0, NY - 1)], flow(*picked, c))
 
-    pipelined(NZ // 2 + 1, middle, *x_stages)
+    pipelined((NZ + 2) // 3, middle, *x_stages)
     loop(Z0 - 1, Z0 + 2, lambda z: put_sums(z, *inner))
 
     def y_inner(z):
@@ -468,25 +444,19 @@
     put_sums(Z1 - 1, *inner)
     loop(Z1 - 3, Z1 - 1, lambda z: put_planes(g2_ext, 0, [(z, *inner)]))
     loop(Z0 + 1, Z1 - 2, lambda z: faces_z([(z, *inner)]))
-    arrive(halo_g)
-
-    def shift_sides_g(i):
-        z = Z0 + 4 * i
-        shift_rows(g2_ext, [w for k in range(4) for w in ((z + k, Y0 - 1, 1), (z + k, Y1, 1))])
-
-    def z_sides(i):
-        z = 1 + 2 * i
-        return [(z, Y0, 1), (z, Y1 - 1, 1), (z + 1, Y0, 1), (z + 1, Y1 - 1, 1)]
-
-    loop(0, NZ // 4, shift_sides_g)
-    loop(0, 4, lambda i: shift_rows(g2_ext, [(i + (i // 2) * (EZ - 4), 1, EY - 2)]))
-    loop(Z0, Z1, sums_edge)
-    loop(0, 4, lambda i: put_sums(i + (i // 2) * (EZ - 4), Y0, NY))
-    loop(0, NZ // 2 + 1, lambda i: put_planes(g2_ext, 0, z_sides(i)))
+    arrive(halo_g[2:4])
+    loop(0, 2, lambda i: shift_rows(g2_ext, [(i * Z1, Y0, NY), (i * Z1 + 1, Y0, NY)]))
+    loop(0, 4, lambda i: put_sums(i + (i // 2) * (EZ - 4), *inner))
     loop(0, 4, lambda i: put_planes(g2_ext, 0, ends(i)))
-    loop(0, NZ // 2, lambda i: faces_z(z_sides(i)))
-    faces_z([(Z1 - 1, Y0, 1), (Z1 - 1, Y1 - 1, 1)])
     loop(0, 4, lambda i: faces_z([(1 + i + (i // 2) * (NZ - 3), *inner)]))
+    arrive(halo_g[:2] + halo_g[4:])
+    loop(0, 2, lambda i: shift_rows(
+        g2_ext, [w for k in range(EZ // 2) for w in ((i * (EZ // 2) + k, Y0 - 1, 1), (i * (EZ // 2) + k, Y1, 1))]
+    ))
+    loop(0, EZ // 4, lambda i: sums_edge(4 * i, 4))
+    loop(0, (NZ + 2) // 3, lambda i: put_planes(g2_ext, 0, edges(1 + 3 * i, 3)))
+    loop(0, NZ // 3, lambda i: faces_z(edges(1 + 3 * i, 3)))
+    faces_z(edges(Z1 - 2, 2))
 
     def update_z(z):
         g = g2_ext[z, own_y] - face[z, own_y] + face[z - 1, own_y]
@@ -516,7 +486,7 @@
         out_specs=(anywhere, anywhere),
         scratch_shapes=[ext] * 18 + [
             pltpu.VMEM((4, NZ, *row), F32),
-            pltpu.VMEM((N_GZ, *row), F32), pltpu.VMEM((RING, *row), F32), pltpu.VMEM((RING, *row), F32),
+            pltpu.VMEM((N_GY, 2, LN), F32), pltpu.VMEM((N_GZ, 2, LN), F32),
             pltpu.VMEM(row, F32), pltpu.VMEM((1, 1), F32), pltpu.VMEM((NZ, NY, *row), F32),
             pltpu.SemaphoreType.DMA((4 * NY,)), pltpu.SemaphoreType.DMA((NY + 1,)),
             pltpu.SemaphoreType.DMA((N_SEMS,)), pltpu.SemaphoreType.DMA((N_SEMS,)),

time: 46.5 us -> 43.2 us (0.929)
  Pallas kernels: 42 us -> 38.7 us
    pallas_call x1, Pallas kernels: 42 us -> 38.7 us  [shards(): pl.pallas_call(kernel, out_shape=(jax.ShapeDtypeStruct((NZ, J, NY, LN), F...]
where the time goes in v4:
time: 43.2 us; the launch traced here: 42.9 us
  Pallas kernels  38.7 us (90%)
  between operations  2.34 us (5%)
  local copies, waits for them, and re-layouts  1.89 us (4%)
    pallas_call x1, Pallas kernels, shards(): pl.pallas_call(kernel, out_shape=(jax.ShapeDtypeStruct((NZ, J, NY, LN), F...  38.7 us
    unnamed x1, local copies, waits for them, and re-layouts  1.89 us

profile of v4, /device:TPU:1, one launch (start us, length us, event | category | flops | bytes accessed | tf_op | source)
XLA Modules:
  0.0 42.9 jit_solution(2449011855425153587)
XLA Ops:
  0.6 38.7 %advect.1 = (f32[16,8,8,128]{3,2,1,0:T(8,128)}, f32[1,1]{1,0:T(1,128)}) custom-call(f32[16,8,8,128]{3,2,1,0:T(8,128)} %bitcast.17, f32[16,8,8,128]{3,2,1,0:T(8,128)} %bitcast.18, f32[16,8,8,128]{3,2,1,0:T(8,128)} %bitcast.19, f32[16,8,8,128]{3,2,1,0:T(8,128)} %bitcast.20), custom_call_target="tpu_custom_call" | custom-call | tf_op jit(solution)/shard_map/advect/pallas_call | solution.py:482
  39.3 1.9 %copy.8 = f32[16,8,1024]{2,1,0:T(8,128)} copy(f32[16,8,1024]{2,1,0:T(8,128)} %bitcast.16) | data formatting | bytes 1048576

commit v5 on v4

--- a/solution.py
+++ b/solution.py
@@ -23,7 +23,7 @@
 HALO_F, HALO_V, HALO_G = 0, 8, 16
 VEL = 24
 FLUX_Y = 26
-STAT_Y = 28
+STAT_Y = 30
 STAT_Z = STAT_Y + N_GY - 1
 N_SEMS = STAT_Z + N_GZ - 1
 
@@ -126,9 +126,9 @@
 
 
 def kernel(
-    f_hbm, vx_hbm, vy_hbm, vz_hbm, out_hbm, dt_out,
+    f_hbm, vx_hbm, vy_hbm, vz_hbm, out_ref, dt_out,
     f_ext, g1_ext, g2_ext, vx, vy, vz, vx_diff, smooth, diff, sum_y, dif_y, sum_d,
-    off, lo, hi, slope, scale, face, edge_y, stat_y, stat_z, dt_vec, dt_cell, out_buf,
+    off, lo, hi, slope, scale, face, edge_y, stat_y, stat_z, dt_vec, dt_cell,
     load_sem, out_sem, send_sem, recv_sem,
 ):
     gy, gz = lax.axis_index("gy"), lax.axis_index("gz")
@@ -283,38 +283,33 @@
 
     inner = (Y0 + 1, NY - 2)
 
-    def x_inner(first, count):
-        pipelined(count, lambda i: [(first + i, *inner)], planes_of(f_ext, 2), donors_x)
-
     loop(0, NZ // 2, lambda i: shift_rows(f_ext, [(Z0 + 2 * i, Y0, NY), (Z0 + 2 * i + 1, Y0, NY)]))
     loop(Z0, Z1, lambda z: put_sums(z, *inner))
-    x_inner(Z0 + 1, 9)
+    pipelined(NZ - 2, lambda i: [(Z0 + 1 + i, *inner)], planes_of(f_ext, 2), donors_x)
+    arrive(halo_f[:2])
+
+    def shift_sides(i):
+        z = Z0 + 4 * i
+        shift_rows(f_ext, [w for k in range(4) for w in ((z + k, 0, 2), (z + k, Y1, 2))])
+
+    def sums_side(z):
+        put_sums(z, 1, 2)
+        put_sums(z, Y1 - 1, 2)
+
+    loop(0, NZ // 4, shift_sides)
+    loop(Z0, Z1, sums_side)
     arrive(stats_y)
     stat_z[gz] = combined(stat_y, N_GY)
     send(stats_z)
-    x_inner(Z0 + 10, NZ - 11)
-    arrive(halo_f[:2])
-
-    def shift_sides(i):
-        z = Z0 + 2 * i
-        shift_rows(f_ext, [(z, 0, 2), (z, Y1, 2), (z + 1, 0, 2), (z + 1, Y1, 2)])
-
-    def shift_ends(i):
-        z = i + (i // 2) * (EZ - 4)
-        shift_rows(f_ext, [(z, 0, EY)])
-
-    def sums_side(z):
-        put_sums(z, 1, 2)
-        put_sums(z, Y1 - 1, 2)
-
-    loop(0, NZ // 2, shift_sides)
     arrive(halo_f[2:])
-    loop(0, 4, shift_ends)
-    loop(Z0, Z1, sums_side)
+
+    loop(0, 2, lambda i: shift_rows(f_ext, [(i * Z1, 0, EY), (i * Z1 + 1, 0, EY)]))
     loop(0, 4, lambda i: put_sums(i + (i // 2) * (EZ - 4), 1, EY - 2))
+
     def sides(i):
-        z = 1 + 2 * i
-        return [(z, 1, 2), (z, Y1 - 1, 2), (z + 1, 1, 2), (z + 1, Y1 - 1, 2)]
+        high = i // (NZ // 3 + 1)
+        z, y = 1 + 3 * (i - high * (NZ // 3 + 1)), 1 + high * (Y1 - 2)
+        return [(z + k, y, 2) for k in range(3)]
 
     def ends(i):
         return [(1 + i + (i // 2) * (NZ - 2), *inner)]
@@ -322,7 +317,7 @@
     loop(0, 4, lambda i: put_planes(f_ext, 2, ends(i)))
     arrive(halo_v)
     loop(0, 4, lambda i: donors_x(ends(i))())
-    pipelined(NZ // 2 + 1, sides, planes_of(f_ext, 2), donors_x)
+    pipelined(2 * (NZ // 3 + 1), sides, planes_of(f_ext, 2), donors_x)
     arrive(stats_z)
     arrive(velocity)
     stats = combined(stat_z, N_GZ)
@@ -356,7 +351,7 @@
 
         return stage
 
-    dt_copy = pltpu.make_async_copy(dt_cell, dt_out, out_sem.at[NY])
+    dt_copy = pltpu.make_async_copy(dt_cell, dt_out, out_sem)
     x_stages = (flow_x, update_x, shifts_of(g1_ext))
     pipelined(
         NZ // 2 + 1,
@@ -383,14 +378,18 @@
             edge_y[0, 4 * i + k] = jnp.where(c[2 * k + 1] > 0, out[2 * k + 1], 0.0)
             edge_y[1, 4 * i + k] = jnp.where(c[2 * k] < 0, out[2 * k], 0.0)
 
-    flux_y = [
-        remote(edge_y.at[0], edge_y.at[2], FLUX_Y, neighbour(1, 0)),
-        remote(edge_y.at[1], edge_y.at[3], FLUX_Y + 1, neighbour(-1, 0)),
-    ]
+    flux_y = []
+    for k in range(2):
+        part = pl.ds(k * (NZ // 2), NZ // 2)
+        flux_y += [
+            remote(edge_y.at[0, part], edge_y.at[2, part], FLUX_Y + 2 * k, neighbour(1, 0)),
+            remote(edge_y.at[1, part], edge_y.at[3, part], FLUX_Y + 2 * k + 1, neighbour(-1, 0)),
+        ]
     loop(0, (NZ + 2) // 3, lambda i: sums_edge(Z0 - 1 + 3 * i, 3))
-    loop(0, NZ // 4, lambda i: put_planes(g1_ext, 1, edges(Z0 + 4 * i, 4)))
-    loop(0, NZ // 4, half_faces_y)
-    send(flux_y)
+    for k in range(2):
+        loop(2 * k, 2 * k + 2, lambda i: put_planes(g1_ext, 1, edges(Z0 + 4 * i, 4)))
+        loop(2 * k, 2 * k + 2, half_faces_y)
+        send(flux_y[2 * k : 2 * k + 2])
 
     def middle(i):
         return [(1 + 3 * i + k, Y0 + 2, NY - 4) for k in range(3)]
@@ -411,15 +410,22 @@
     loop(Z0, Z1 - 1, y_inner)
     put_planes(g1_ext, 1, [(Z1 - 1, *inner)])
     loop(Z0, Z1, faces_y)
+    def update_y(where):
+        before, q = moved(where, 0, -1), dt_vec[...]
+        g = rows(g1_ext, where) - rows(face, where) + rows(face, before)
+        put(g2_ext, where, g / (1.0 - q * (rows(vy, where) - rows(vy, before))))
+
+    loop(Z0, Z1, lambda z: update_y([(z, *inner)]))
     arrive(flux_y)
 
-    def update_y(z):
-        face[z, Y0 - 1] = edge_y[2, z - Z0] - edge_y[1, z - Z0]
-        face[z, Y1 - 1] = edge_y[0, z - Z0] - edge_y[3, z - Z0]
-        out, q = face[z, pl.ds(Y0 - 1, NY + 1)], vy[z, pl.ds(Y0 - 1, NY + 1)]
-        g2_ext[z, own_y] = (g1_ext[z, own_y] - out[1:] + out[:-1]) / (1.0 - dt_vec[...] * (q[1:] - q[:-1]))
-
-    loop(Z0, Z1, update_y)
+    def update_y_edge(i):
+        for k in range(4):
+            z, at = Z0 + 4 * i + k, 4 * i + k
+            face[z, Y0 - 1] = edge_y[2, at] - edge_y[1, at]
+            face[z, Y1 - 1] = edge_y[0, at] - edge_y[3, at]
+        update_y(edges(Z0 + 4 * i, 4))
+
+    loop(0, NZ // 4, update_y_edge)
     halo_g = halo(g2_ext, HALO_G, 2, 1)
 
     def faces_z(where):
@@ -427,7 +433,7 @@
         put(face, where, flow(*donors(c > 0, where, moved(where, 1, 0)), c))
 
     shift_rows(g2_ext, [(Z0, Y0, NY), (Z0 + 1, Y0, NY)])
-    send(halo_g)
+    send(halo_g[:2] + halo_g[4:] + halo_g[2:4])
     shift_rows(g2_ext, [(Z0 + 2, Y0, NY), (Z0 + 3, Y0, NY)])
     loop(Z0, Z0 + 3, lambda z: put_sums(z, *inner))
 
@@ -460,18 +466,14 @@
 
     def update_z(z):
         g = g2_ext[z, own_y] - face[z, own_y] + face[z - 1, own_y]
-        out_buf[z - Z0] = g / (1.0 - dt_vec[...] * (vz[z, own_y] - vz[z - 1, own_y]))
+        g = g / (1.0 - dt_vec[...] * (vz[z, own_y] - vz[z - 1, own_y]))
+        for y in range(NY):
+            out_ref[z - Z0, :, y, :] = g[y]
 
     loop(Z0, Z1, update_z)
-    stores = [
-        pltpu.make_async_copy(out_buf.at[:, y], out_hbm.at[:, :, y, :], out_sem.at[y]) for y in range(NY)
-    ]
-    for copy in stores:
-        copy.start()
     for copy in sent:
         copy.wait_send()
-    for copy in [*stores, dt_copy]:
-        copy.wait()
+    dt_copy.wait()
 
 
 def shards(*blocks):
@@ -481,14 +483,14 @@
     anywhere = pl.BlockSpec(memory_space=pl.ANY)
     field, step = pl.pallas_call(
         kernel,
-        out_shape=(jax.ShapeDtypeStruct((NZ, J, NY, LN), F32), jax.ShapeDtypeStruct((1, 1), F32)),
+        out_shape=(pltpu.VMEM((NZ, J, NY, LN), F32), jax.ShapeDtypeStruct((1, 1), F32)),
         in_specs=[anywhere] * 4,
-        out_specs=(anywhere, anywhere),
+        out_specs=(pl.BlockSpec(memory_space=pltpu.VMEM), anywhere),
         scratch_shapes=[ext] * 18 + [
             pltpu.VMEM((4, NZ, *row), F32),
             pltpu.VMEM((N_GY, 2, LN), F32), pltpu.VMEM((N_GZ, 2, LN), F32),
-            pltpu.VMEM(row, F32), pltpu.VMEM((1, 1), F32), pltpu.VMEM((NZ, NY, *row), F32),
-            pltpu.SemaphoreType.DMA((4 * NY,)), pltpu.SemaphoreType.DMA((NY + 1,)),
+            pltpu.VMEM(row, F32), pltpu.VMEM((1, 1), F32),
+            pltpu.SemaphoreType.DMA((4 * NY,)), pltpu.SemaphoreType.DMA(()),
             pltpu.SemaphoreType.DMA((N_SEMS,)), pltpu.SemaphoreType.DMA((N_SEMS,)),
         ],
         compiler_params=pltpu.CompilerParams(collective_id=0, has_side_effects=True),

time: 43.2 us -> 42 us (0.972)
  local copies, waits for them, and re-layouts: 1.89 us -> 0.8 us
    unnamed x1, local copies, waits for them, and re-layouts: 1.89 us -> 0.8 us
where the time goes in v5:
time: 42 us; the launch traced here: 41.8 us
  Pallas kernels  38.6 us (92%)
  between operations  2.33 us (6%)
  local copies, waits for them, and re-layouts  0.8 us (2%)
    pallas_call x1, Pallas kernels, shards(): pl.pallas_call(kernel, out_shape=(pltpu.VMEM((NZ, J, NY, LN), F32), jax.S...  38.6 us

profile of v5, /device:TPU:1, one launch (start us, length us, event | category | flops | bytes accessed | tf_op | source)
XLA Modules:
  0.0 41.8 jit_solution(4443128353664144227)
XLA Ops:
  0.6 38.6 %advect.1 = (f32[16,8,8,128]{3,2,1,0:T(8,128)S(1)}, f32[1,1]{1,0:T(1,128)}) custom-call(f32[16,8,8,128]{3,2,1,0:T(8,128)} %bitcast.17, f32[16,8,8,128]{3,2,1,0:T(8,128)} %bitcast.18, f32[16,8,8,128]{3,2,1,0:T(8,128)} %bitcast.19, f32[16,8,8,128]{3,2,1,0:T(8,128)} %bitcast.20), custom_call_target="tpu_custom_call" | custom-call | tf_op jit(solution)/shard_map/advect/pallas_call | solution.py:484
  39.3 0.8 %copy.8 = f32[16,8,1024]{2,1,0:T(8,128)} copy(f32[16,8,1024]{2,1,0:T(8,128)S(1)} %bitcast.16) | data formatting | bytes 1048576

commit v6 on v5

--- a/solution.py
+++ b/solution.py
@@ -20,12 +20,9 @@
 Z0, Y0 = 2, 2
 Z1, Y1 = Z0 + NZ, Y0 + NY
 
-HALO_F, HALO_V, HALO_G = 0, 8, 16
-VEL = 24
-FLUX_Y = 26
-STAT_Y = 30
-STAT_Z = STAT_Y + N_GY - 1
-N_SEMS = STAT_Z + N_GZ - 1
+HALO_F, HALO_V, HALO_G, VEL, FLUX, STAT_Y, STAT_Z = range(7)
+HALO_F_FAR, HALO_G_NEAR = 7, 8
+N_SEND, N_RECV = 7, 9
 
 
 def lanes(u):
@@ -139,48 +136,47 @@
     corners = [(1, 1), (1, -1), (-1, 1), (-1, -1)]
     own_z, own_y = pl.ds(Z0, NZ), pl.ds(Y0, NY)
 
-    loads = []
-    for source, target in ((f_hbm, f_ext), (vx_hbm, vx), (vy_hbm, vy), (vz_hbm, vz)):
+    arrays = [(f_hbm, f_ext), (vx_hbm, vx), (vy_hbm, vy), (vz_hbm, vz)]
+    for k, (source, target) in enumerate(arrays):
         for y in range(NY):
-            semaphore = load_sem.at[len(loads)]
-            loads.append(pltpu.make_async_copy(source.at[:, :, y, :], target.at[own_z, Y0 + y], semaphore))
-    for copy in loads:
-        copy.start()
+            pltpu.make_async_copy(source.at[:, :, y, :], target.at[own_z, Y0 + y], load_sem.at[k]).start()
     barrier = pltpu.get_barrier_semaphore()
     greeted = [neighbour(0, k) for k in range(1, N_GZ)]
     greeted += [neighbour(k, 0) for k in range(1, N_GY)] + [neighbour(*c) for c in corners]
     for device in greeted:
         pl.semaphore_signal(barrier, inc=1, device_id=device, device_id_type=pl.DeviceIdType.MESH)
 
-    def remote(source, target, k, device):
+    def remote(source, target, sends, receives, device):
         return pltpu.make_async_remote_copy(
-            src_ref=source, dst_ref=target, send_sem=send_sem.at[k], recv_sem=recv_sem.at[k],
+            src_ref=source, dst_ref=target, send_sem=send_sem.at[sends], recv_sem=recv_sem.at[receives],
             device_id=device, device_id_type=pl.DeviceIdType.MESH,
         )
 
-    def halo(g, base, wide_z, wide_y):
+    def halo(g, sends, receives, wide_z, wide_y):
         from_z = {1: pl.ds(Z1 - wide_z, wide_z), -1: pl.ds(Z0, wide_z), 0: own_z}
         from_y = {1: pl.ds(Y1 - wide_y, wide_y), -1: pl.ds(Y0, wide_y), 0: own_y}
         to_z = {1: pl.ds(Z0 - wide_z, wide_z), -1: pl.ds(Z1, wide_z), 0: own_z}
         to_y = {1: pl.ds(Y0 - wide_y, wide_y), -1: pl.ds(Y1, wide_y), 0: own_y}
         return [
-            remote(g.at[from_z[dz], from_y[dy]], g.at[to_z[dz], to_y[dy]], base + k, neighbour(dy, dz))
+            remote(g.at[from_z[dz], from_y[dy]], g.at[to_z[dz], to_y[dy]], sends, receives[k], neighbour(dy, dz))
             for k, (dy, dz) in enumerate([(1, 0), (-1, 0), (0, 1), (0, -1)] + corners)
         ]
-
-    sent = []
 
     def send(copies):
         for copy in copies:
             copy.start()
-        sent.extend(copies)
-
-    def arrive(copies):
-        for copy in copies:
-            copy.wait_recv()
-
-    for copy in loads:
-        copy.wait()
+
+    def arrive(part, receives):
+        remote(part, part, 0, receives, neighbour(1, 0)).wait_recv()
+
+    def left(part, sends):
+        remote(part, part, sends, 0, neighbour(1, 0)).wait_send()
+
+    def some(ref, z, y):
+        return ref.at[pl.ds(0, z), pl.ds(0, y)]
+
+    for k, (source, target) in enumerate(arrays):
+        pltpu.make_async_copy(source, target.at[own_z, own_y], load_sem.at[k]).wait()
 
     def scan(i, found):
         z = i + Z0
@@ -203,18 +199,16 @@
     stat_y[gy] = jnp.concatenate([jnp.max(top, axis=0, keepdims=True), jnp.sum(add, axis=0, keepdims=True)], axis=0)
 
     pl.semaphore_wait(barrier, len(greeted))
-    halo_f = halo(f_ext, HALO_F, 2, 2)
-    halo_v = halo(vx, HALO_V, 1, 1)
-    stats_y = [remote(stat_y.at[gy], stat_y.at[gy], STAT_Y + k - 1, neighbour(k, 0)) for k in range(1, N_GY)]
-    stats_z = [remote(stat_z.at[gz], stat_z.at[gz], STAT_Z + k - 1, neighbour(0, k)) for k in range(1, N_GZ)]
+    halo_f = halo(f_ext, HALO_F, 2 * [HALO_F] + 6 * [HALO_F_FAR], 2, 2)
+    halo_v = halo(vx, HALO_V, 8 * [HALO_V], 1, 1)
+    stats_y = [remote(stat_y.at[gy], stat_y.at[gy], STAT_Y, STAT_Y, neighbour(k, 0)) for k in range(1, N_GY)]
+    stats_z = [remote(stat_z.at[gz], stat_z.at[gz], STAT_Z, STAT_Z, neighbour(0, k)) for k in range(1, N_GZ)]
     velocity = [
-        remote(vy.at[own_z, Y1 - 1], vy.at[own_z, Y0 - 1], VEL, neighbour(1, 0)),
-        remote(vz.at[Z1 - 1, own_y], vz.at[Z0 - 1, own_y], VEL + 1, neighbour(0, 1)),
+        remote(vy.at[own_z, Y1 - 1], vy.at[own_z, Y0 - 1], VEL, VEL, neighbour(1, 0)),
+        remote(vz.at[Z1 - 1, own_y], vz.at[Z0 - 1, own_y], VEL, VEL, neighbour(0, 1)),
     ]
     send(stats_y)
     send(halo_f)
-    send(halo_v)
-    send(velocity)
 
     def put_shifts(g, where):
         before, after = at_prev(g), at_next(g)
@@ -286,7 +280,8 @@
     loop(0, NZ // 2, lambda i: shift_rows(f_ext, [(Z0 + 2 * i, Y0, NY), (Z0 + 2 * i + 1, Y0, NY)]))
     loop(Z0, Z1, lambda z: put_sums(z, *inner))
     pipelined(NZ - 2, lambda i: [(Z0 + 1 + i, *inner)], planes_of(f_ext, 2), donors_x)
-    arrive(halo_f[:2])
+    send(halo_v)
+    arrive(some(f_ext, NZ, 4), HALO_F)
 
     def shift_sides(i):
         z = Z0 + 4 * i
@@ -298,10 +293,11 @@
 
     loop(0, NZ // 4, shift_sides)
     loop(Z0, Z1, sums_side)
-    arrive(stats_y)
+    arrive(stat_y.at[pl.ds(0, N_GY - 1)], STAT_Y)
     stat_z[gz] = combined(stat_y, N_GY)
     send(stats_z)
-    arrive(halo_f[2:])
+    send(velocity)
+    arrive(some(f_ext, 12, 4), HALO_F_FAR)
 
     loop(0, 2, lambda i: shift_rows(f_ext, [(i * Z1, 0, EY), (i * Z1 + 1, 0, EY)]))
     loop(0, 4, lambda i: put_sums(i + (i // 2) * (EZ - 4), 1, EY - 2))
@@ -315,11 +311,10 @@
         return [(1 + i + (i // 2) * (NZ - 2), *inner)]
 
     loop(0, 4, lambda i: put_planes(f_ext, 2, ends(i)))
-    arrive(halo_v)
-    loop(0, 4, lambda i: donors_x(ends(i))())
+    arrive(some(vx, 13, 4), HALO_V)
+    loop(0, 2, lambda i: donors_x([(1 + i * NZ + k, *inner) for k in range(2)])())
     pipelined(2 * (NZ // 3 + 1), sides, planes_of(f_ext, 2), donors_x)
-    arrive(stats_z)
-    arrive(velocity)
+    arrive(stat_z.at[pl.ds(0, N_GZ - 1)], STAT_Z)
     stats = combined(stat_z, N_GZ)
     umax = jnp.max(stats[0:1], axis=1, keepdims=True)
     share = jnp.sum(stats[1:2], axis=1, keepdims=True) * (4.0 / (N_GZ * NZ * N_GY * NY * J * LN))
@@ -382,9 +377,10 @@
     for k in range(2):
         part = pl.ds(k * (NZ // 2), NZ // 2)
         flux_y += [
-            remote(edge_y.at[0, part], edge_y.at[2, part], FLUX_Y + 2 * k, neighbour(1, 0)),
-            remote(edge_y.at[1, part], edge_y.at[3, part], FLUX_Y + 2 * k + 1, neighbour(-1, 0)),
+            remote(edge_y.at[0, part], edge_y.at[2, part], FLUX, FLUX, neighbour(1, 0)),
+            remote(edge_y.at[1, part], edge_y.at[3, part], FLUX, FLUX, neighbour(-1, 0)),
         ]
+    arrive(some(vy, 6, 4), VEL)
     loop(0, (NZ + 2) // 3, lambda i: sums_edge(Z0 - 1 + 3 * i, 3))
     for k in range(2):
         loop(2 * k, 2 * k + 2, lambda i: put_planes(g1_ext, 1, edges(Z0 + 4 * i, 4)))
@@ -416,7 +412,7 @@
         put(g2_ext, where, g / (1.0 - q * (rows(vy, where) - rows(vy, before))))
 
     loop(Z0, Z1, lambda z: update_y([(z, *inner)]))
-    arrive(flux_y)
+    arrive(edge_y.at[pl.ds(2, 2)], FLUX)
 
     def update_y_edge(i):
         for k in range(4):
@@ -426,7 +422,8 @@
         update_y(edges(Z0 + 4 * i, 4))
 
     loop(0, NZ // 4, update_y_edge)
-    halo_g = halo(g2_ext, HALO_G, 2, 1)
+    near = [HALO_G, HALO_G, HALO_G_NEAR, HALO_G_NEAR] + 4 * [HALO_G]
+    halo_g = halo(g2_ext, HALO_G, near, 2, 1)
 
     def faces_z(where):
         c = dt_vec[...] * rows(vz, where)
@@ -450,12 +447,12 @@
     put_sums(Z1 - 1, *inner)
     loop(Z1 - 3, Z1 - 1, lambda z: put_planes(g2_ext, 0, [(z, *inner)]))
     loop(Z0 + 1, Z1 - 2, lambda z: faces_z([(z, *inner)]))
-    arrive(halo_g[2:4])
+    arrive(some(g2_ext, 8, 4), HALO_G_NEAR)
     loop(0, 2, lambda i: shift_rows(g2_ext, [(i * Z1, Y0, NY), (i * Z1 + 1, Y0, NY)]))
     loop(0, 4, lambda i: put_sums(i + (i // 2) * (EZ - 4), *inner))
     loop(0, 4, lambda i: put_planes(g2_ext, 0, ends(i)))
     loop(0, 4, lambda i: faces_z([(1 + i + (i // 2) * (NZ - 3), *inner)]))
-    arrive(halo_g[:2] + halo_g[4:])
+    arrive(some(g2_ext, 10, 4), HALO_G)
     loop(0, 2, lambda i: shift_rows(
         g2_ext, [w for k in range(EZ // 2) for w in ((i * (EZ // 2) + k, Y0 - 1, 1), (i * (EZ // 2) + k, Y1, 1))]
     ))
@@ -471,8 +468,13 @@
             out_ref[z - Z0, :, y, :] = g[y]
 
     loop(Z0, Z1, update_z)
-    for copy in sent:
-        copy.wait_send()
+    left(some(f_ext, 14, 8), HALO_F)
+    left(some(vx, 13, 4), HALO_V)
+    left(some(g2_ext, 9, 8), HALO_G)
+    left(some(vy, 6, 4), VEL)
+    left(edge_y.at[pl.ds(0, 2)], FLUX)
+    left(stat_y.at[pl.ds(0, N_GY - 1)], STAT_Y)
+    left(stat_z.at[pl.ds(0, N_GZ - 1)], STAT_Z)
     dt_copy.wait()
 
 
@@ -490,8 +492,8 @@
             pltpu.VMEM((4, NZ, *row), F32),
             pltpu.VMEM((N_GY, 2, LN), F32), pltpu.VMEM((N_GZ, 2, LN), F32),
             pltpu.VMEM(row, F32), pltpu.VMEM((1, 1), F32),
-            pltpu.SemaphoreType.DMA((4 * NY,)), pltpu.SemaphoreType.DMA(()),
-            pltpu.SemaphoreType.DMA((N_SEMS,)), pltpu.SemaphoreType.DMA((N_SEMS,)),
+            pltpu.SemaphoreType.DMA((4,)), pltpu.SemaphoreType.DMA(()),
+            pltpu.SemaphoreType.DMA((N_SEND,)), pltpu.SemaphoreType.DMA((N_RECV,)),
         ],
         compiler_params=pltpu.CompilerParams(collective_id=0, has_side_effects=True),
         name="advect",

time: 42 us -> 40.7 us (0.969)
  Pallas kernels: 38.6 us -> 37.4 us
    pallas_call x1, Pallas kernels: 38.6 us -> 37.4 us  [shards(): pl.pallas_call(kernel, out_shape=(pltpu.VMEM((NZ, J, NY, LN), F32), jax.S...]
where the time goes in v6:
time: 40.7 us; the launch traced here: 40.5 us
  Pallas kernels  37.4 us (92%)
  between operations  2.33 us (6%)
  local copies, waits for them, and re-layouts  0.8 us (2%)
    pallas_call x1, Pallas kernels, shards(): pl.pallas_call(kernel, out_shape=(pltpu.VMEM((NZ, J, NY, LN), F32), jax.S...  37.4 us

profile of v6, /device:TPU:1, one launch (start us, length us, event | category | flops | bytes accessed | tf_op | source)
XLA Modules:
  0.0 40.5 jit_solution(7706967338319911738)
XLA Ops:
  0.6 37.4 %advect.1 = (f32[16,8,8,128]{3,2,1,0:T(8,128)S(1)}, f32[1,1]{1,0:T(1,128)}) custom-call(f32[16,8,8,128]{3,2,1,0:T(8,128)} %bitcast.17, f32[16,8,8,128]{3,2,1,0:T(8,128)} %bitcast.18, f32[16,8,8,128]{3,2,1,0:T(8,128)} %bitcast.19, f32[16,8,8,128]{3,2,1,0:T(8,128)} %bitcast.20), custom_call_target="tpu_custom_call" | custom-call | tf_op jit(solution)/shard_map/advect/pallas_call | solution.py:486
  38.0 0.8 %copy.8 = f32[16,8,1024]{2,1,0:T(8,128)} copy(f32[16,8,1024]{2,1,0:T(8,128)S(1)} %bitcast.16) | data formatting | bytes 1048576

commit v7 on v6

--- a/solution.py
+++ b/solution.py
@@ -137,14 +137,20 @@
     own_z, own_y = pl.ds(Z0, NZ), pl.ds(Y0, NY)
 
     arrays = [(f_hbm, f_ext), (vx_hbm, vx), (vy_hbm, vy), (vz_hbm, vz)]
-    for k, (source, target) in enumerate(arrays):
+
+    def load(k):
+        source, target = arrays[k]
         for y in range(NY):
             pltpu.make_async_copy(source.at[:, :, y, :], target.at[own_z, Y0 + y], load_sem.at[k]).start()
+
+    load(0)
     barrier = pltpu.get_barrier_semaphore()
-    greeted = [neighbour(0, k) for k in range(1, N_GZ)]
-    greeted += [neighbour(k, 0) for k in range(1, N_GY)] + [neighbour(*c) for c in corners]
+    greeted = [neighbour(k, 0) for k in range(1, N_GY)]
+    greeted += [neighbour(0, k) for k in range(1, N_GZ)] + [neighbour(*c) for c in corners]
     for device in greeted:
         pl.semaphore_signal(barrier, inc=1, device_id=device, device_id_type=pl.DeviceIdType.MESH)
+    for k in (1, 2, 3):
+        load(k)
 
     def remote(source, target, sends, receives, device):
         return pltpu.make_async_remote_copy(
@@ -175,18 +181,21 @@
     def some(ref, z, y):
         return ref.at[pl.ds(0, z), pl.ds(0, y)]
 
-    for k, (source, target) in enumerate(arrays):
+    def loaded(k):
+        source, target = arrays[k]
         pltpu.make_async_copy(source, target.at[own_z, own_y], load_sem.at[k]).wait()
 
-    def scan(i, found):
-        z = i + Z0
-        peak, total = found
-        g = f_ext[z, own_y]
-        own = jnp.maximum(jnp.abs(vx[z, own_y]), jnp.abs(vy[z, own_y]))
-        return jnp.maximum(peak, jnp.maximum(own, jnp.abs(vz[z, own_y]))), total + g * (1.0 - g)
-
-    zeros = jnp.zeros((NY, J, LN), F32)
-    peak, total = lax.fori_loop(0, NZ, scan, (zeros, zeros))
+    def scan_fraction(i, total):
+        g = f_ext[i + Z0, own_y]
+        return total + g * (1.0 - g)
+
+    loaded(0)
+    total = lax.fori_loop(0, NZ, scan_fraction, jnp.zeros((NY, J, LN), F32))
+    peak = jnp.zeros((NY, J, LN), F32)
+    for k in (1, 2, 3):
+        loaded(k)
+        speeds = arrays[k][1]
+        peak = lax.fori_loop(0, NZ, lambda i, peak: jnp.maximum(peak, jnp.abs(speeds[i + Z0, own_y])), peak)
     top_row = lax.broadcasted_iota(jnp.int32, (2, LN), 0) == 0
 
     def combined(ref, n):
@@ -390,10 +399,9 @@
     def middle(i):
         return [(1 + 3 * i + k, Y0 + 2, NY - 4) for k in range(3)]
 
-    def faces_y(z):
-        c = dt_vec[...] * vy[z, pl.ds(Y0, NY - 1)]
-        picked = donors(c > 0, [(z, Y0, NY - 1)], [(z, Y0 + 1, NY - 1)])
-        put(face, [(z, Y0, NY - 1)], flow(*picked, c))
+    def faces_y(where):
+        c = dt_vec[...] * rows(vy, where)
+        put(face, where, flow(*donors(c > 0, where, moved(where, 0, 1)), c))
 
     pipelined((NZ + 2) // 3, middle, *x_stages)
     loop(Z0 - 1, Z0 + 2, lambda z: put_sums(z, *inner))
@@ -405,14 +413,14 @@
 
     loop(Z0, Z1 - 1, y_inner)
     put_planes(g1_ext, 1, [(Z1 - 1, *inner)])
-    loop(Z0, Z1, faces_y)
+    def faces_y_near(i):
+        z = Z0 + 4 * i
+        faces_y([w for k in range(4) for w in ((z + k, Y0, 1), (z + k, Y1 - 2, 1))])
+
     def update_y(where):
         before, q = moved(where, 0, -1), dt_vec[...]
         g = rows(g1_ext, where) - rows(face, where) + rows(face, before)
         put(g2_ext, where, g / (1.0 - q * (rows(vy, where) - rows(vy, before))))
-
-    loop(Z0, Z1, lambda z: update_y([(z, *inner)]))
-    arrive(edge_y.at[pl.ds(2, 2)], FLUX)
 
     def update_y_edge(i):
         for k in range(4):
@@ -421,16 +429,26 @@
             face[z, Y1 - 1] = edge_y[0, at] - edge_y[3, at]
         update_y(edges(Z0 + 4 * i, 4))
 
-    loop(0, NZ // 4, update_y_edge)
+    def rest_y(i):
+        z = Z0 + 2 * lax.rem(7 * i, NZ // 2)
+        faces_y([(z, Y0 + 1, NY - 3), (z + 1, Y0 + 1, NY - 3)])
+        update_y([(z, *inner), (z + 1, *inner)])
+
     near = [HALO_G, HALO_G, HALO_G_NEAR, HALO_G_NEAR] + 4 * [HALO_G]
     halo_g = halo(g2_ext, HALO_G, near, 2, 1)
+    loop(0, NZ // 4, faces_y_near)
+    arrive(edge_y.at[pl.ds(2, 2)], FLUX)
+    loop(0, NZ // 4, update_y_edge)
+    send(halo_g[:2] + halo_g[4:])
+    loop(0, 2, rest_y)
+    send(halo_g[2:4])
+    loop(2, NZ // 2, rest_y)
 
     def faces_z(where):
         c = dt_vec[...] * rows(vz, where)
         put(face, where, flow(*donors(c > 0, where, moved(where, 1, 0)), c))
 
     shift_rows(g2_ext, [(Z0, Y0, NY), (Z0 + 1, Y0, NY)])
-    send(halo_g[:2] + halo_g[4:] + halo_g[2:4])
     shift_rows(g2_ext, [(Z0 + 2, Y0, NY), (Z0 + 3, Y0, NY)])
     loop(Z0, Z0 + 3, lambda z: put_sums(z, *inner))
 
@@ -452,6 +470,14 @@
     loop(0, 4, lambda i: put_sums(i + (i // 2) * (EZ - 4), *inner))
     loop(0, 4, lambda i: put_planes(g2_ext, 0, ends(i)))
     loop(0, 4, lambda i: faces_z([(1 + i + (i // 2) * (NZ - 3), *inner)]))
+    def update_z(where):
+        before, q = moved(where, -1, 0), dt_vec[...]
+        g = rows(g2_ext, where) - rows(face, where) + rows(face, before)
+        g = g / (1.0 - q * (rows(vz, where) - rows(vz, before)))
+        for k, (z, y) in enumerate([(z, y + k) for z, y, n in where for k in range(n)]):
+            out_ref[z - Z0, :, y - Y0, :] = g[k]
+
+    loop(Z0, Z1, lambda z: update_z([(z, *inner)]))
     arrive(some(g2_ext, 10, 4), HALO_G)
     loop(0, 2, lambda i: shift_rows(
         g2_ext, [w for k in range(EZ // 2) for w in ((i * (EZ // 2) + k, Y0 - 1, 1), (i * (EZ // 2) + k, Y1, 1))]
@@ -461,13 +487,7 @@
     loop(0, NZ // 3, lambda i: faces_z(edges(1 + 3 * i, 3)))
     faces_z(edges(Z1 - 2, 2))
 
-    def update_z(z):
-        g = g2_ext[z, own_y] - face[z, own_y] + face[z - 1, own_y]
-        g = g / (1.0 - dt_vec[...] * (vz[z, own_y] - vz[z - 1, own_y]))
-        for y in range(NY):
-            out_ref[z - Z0, :, y, :] = g[y]
-
-    loop(Z0, Z1, update_z)
+    loop(0, NZ // 4, lambda i: update_z(edges(Z0 + 4 * i, 4)))
     left(some(f_ext, 14, 8), HALO_F)
     left(some(vx, 13, 4), HALO_V)
     left(some(g2_ext, 9, 8), HALO_G)

time: 40.7 us -> 39 us (0.958)
  Pallas kernels: 37.4 us -> 35.7 us
    pallas_call x1, Pallas kernels: 37.4 us -> 35.7 us  [shards(): pl.pallas_call(kernel, out_shape=(pltpu.VMEM((NZ, J, NY, LN), F32), jax.S...]
where the time goes in v7:
time: 39 us; the launch traced here: 38.8 us
  Pallas kernels  35.7 us (92%)
  between operations  2.33 us (6%)
  local copies, waits for them, and re-layouts  0.8 us (2%)
    pallas_call x1, Pallas kernels, shards(): pl.pallas_call(kernel, out_shape=(pltpu.VMEM((NZ, J, NY, LN), F32), jax.S...  35.7 us
    unnamed x1, local copies, waits for them, and re-layouts  0.8 us

profile of v7, /device:TPU:1, one launch (start us, length us, event | category | flops | bytes accessed | tf_op | source)
XLA Modules:
  0.0 38.8 jit_solution(5944650507174291195)
XLA Ops:
  0.6 35.7 %advect.1 = (f32[16,8,8,128]{3,2,1,0:T(8,128)S(1)}, f32[1,1]{1,0:T(1,128)}) custom-call(f32[16,8,8,128]{3,2,1,0:T(8,128)} %bitcast.17, f32[16,8,8,128]{3,2,1,0:T(8,128)} %bitcast.18, f32[16,8,8,128]{3,2,1,0:T(8,128)} %bitcast.19, f32[16,8,8,128]{3,2,1,0:T(8,128)} %bitcast.20), custom_call_target="tpu_custom_call" | custom-call | tf_op jit(solution)/shard_map/advect/pallas_call | solution.py:506
  36.3 0.8 %copy.8 = f32[16,8,1024]{2,1,0:T(8,128)} copy(f32[16,8,1024]{2,1,0:T(8,128)S(1)} %bitcast.16) | data formatting | bytes 1048576

commit v8 on v7

--- a/solution.py
+++ b/solution.py
@@ -21,8 +21,8 @@
 Z1, Y1 = Z0 + NZ, Y0 + NY
 
 HALO_F, HALO_V, HALO_G, VEL, FLUX, STAT_Y, STAT_Z = range(7)
-HALO_F_FAR, HALO_G_NEAR = 7, 8
-N_SEND, N_RECV = 7, 9
+HALO_F_NEAR, HALO_F_FAR, HALO_G_NEAR = 7, 8, 9
+N_SEND, N_RECV = 7, 10
 
 
 def lanes(u):
@@ -208,7 +208,7 @@
     stat_y[gy] = jnp.concatenate([jnp.max(top, axis=0, keepdims=True), jnp.sum(add, axis=0, keepdims=True)], axis=0)
 
     pl.semaphore_wait(barrier, len(greeted))
-    halo_f = halo(f_ext, HALO_F, 2 * [HALO_F] + 6 * [HALO_F_FAR], 2, 2)
+    halo_f = halo(f_ext, HALO_F, 2 * [HALO_F] + 2 * [HALO_F_NEAR] + 4 * [HALO_F_FAR], 2, 2)
     halo_v = halo(vx, HALO_V, 8 * [HALO_V], 1, 1)
     stats_y = [remote(stat_y.at[gy], stat_y.at[gy], STAT_Y, STAT_Y, neighbour(k, 0)) for k in range(1, N_GY)]
     stats_z = [remote(stat_z.at[gz], stat_z.at[gz], STAT_Z, STAT_Z, neighbour(0, k)) for k in range(1, N_GZ)]
@@ -217,7 +217,7 @@
         remote(vz.at[Z1 - 1, own_y], vz.at[Z0 - 1, own_y], VEL, VEL, neighbour(0, 1)),
     ]
     send(stats_y)
-    send(halo_f)
+    send(halo_f[2:4] + halo_f[:2] + halo_f[4:])
 
     def put_shifts(g, where):
         before, after = at_prev(g), at_next(g)
@@ -286,10 +286,20 @@
 
     inner = (Y0 + 1, NY - 2)
 
+    def pair(z):
+        return [(z, *inner), (z + 1, *inner)]
+
+    def shift_ends(g_ext):
+        loop(0, 2, lambda i: shift_rows(g_ext, [(i * Z1, Y0, NY), (i * Z1 + 1, Y0, NY)]))
+        loop(0, 4, lambda i: put_sums(i + (i // 2) * (EZ - 4), *inner))
+
     loop(0, NZ // 2, lambda i: shift_rows(f_ext, [(Z0 + 2 * i, Y0, NY), (Z0 + 2 * i + 1, Y0, NY)]))
     loop(Z0, Z1, lambda z: put_sums(z, *inner))
-    pipelined(NZ - 2, lambda i: [(Z0 + 1 + i, *inner)], planes_of(f_ext, 2), donors_x)
+    pipelined(NZ // 2 - 1, lambda i: pair(Z0 + 1 + 2 * i), planes_of(f_ext, 2), donors_x)
     send(halo_v)
+    arrive(some(f_ext, 8, 4), HALO_F_NEAR)
+    shift_ends(f_ext)
+    loop(0, 2, lambda i: put_planes(f_ext, 2, pair(1 + i * NZ)))
     arrive(some(f_ext, NZ, 4), HALO_F)
 
     def shift_sides(i):
@@ -306,23 +316,22 @@
     stat_z[gz] = combined(stat_y, N_GY)
     send(stats_z)
     send(velocity)
-    arrive(some(f_ext, 12, 4), HALO_F_FAR)
-
-    loop(0, 2, lambda i: shift_rows(f_ext, [(i * Z1, 0, EY), (i * Z1 + 1, 0, EY)]))
-    loop(0, 4, lambda i: put_sums(i + (i // 2) * (EZ - 4), 1, EY - 2))
+    arrive(some(f_ext, 4, 4), HALO_F_FAR)
+
+    def shift_corners(i):
+        z = i * Z1
+        shift_rows(f_ext, [(z, 0, 2), (z, Y1, 2), (z + 1, 0, 2), (z + 1, Y1, 2)])
 
     def sides(i):
-        high = i // (NZ // 3 + 1)
-        z, y = 1 + 3 * (i - high * (NZ // 3 + 1)), 1 + high * (Y1 - 2)
-        return [(z + k, y, 2) for k in range(3)]
-
-    def ends(i):
-        return [(1 + i + (i // 2) * (NZ - 2), *inner)]
-
-    loop(0, 4, lambda i: put_planes(f_ext, 2, ends(i)))
+        high = i // 3
+        z, y = 1 + 6 * (i - 3 * high), 1 + high * (Y1 - 2)
+        return [(z + k, y, 2) for k in range(6)]
+
+    loop(0, 2, shift_corners)
+    loop(0, 4, lambda i: sums_side(i + (i // 2) * (EZ - 4)))
     arrive(some(vx, 13, 4), HALO_V)
-    loop(0, 2, lambda i: donors_x([(1 + i * NZ + k, *inner) for k in range(2)])())
-    pipelined(2 * (NZ // 3 + 1), sides, planes_of(f_ext, 2), donors_x)
+    loop(0, 2, lambda i: donors_x(pair(1 + i * NZ))())
+    pipelined(6, sides, planes_of(f_ext, 2), donors_x)
     arrive(stat_z.at[pl.ds(0, N_GZ - 1)], STAT_Z)
     stats = combined(stat_z, N_GZ)
     umax = jnp.max(stats[0:1], axis=1, keepdims=True)
@@ -392,7 +401,7 @@
     arrive(some(vy, 6, 4), VEL)
     loop(0, (NZ + 2) // 3, lambda i: sums_edge(Z0 - 1 + 3 * i, 3))
     for k in range(2):
-        loop(2 * k, 2 * k + 2, lambda i: put_planes(g1_ext, 1, edges(Z0 + 4 * i, 4)))
+        put_planes(g1_ext, 1, edges(Z0 + k * (NZ // 2), NZ // 2))
         loop(2 * k, 2 * k + 2, half_faces_y)
         send(flux_y[2 * k : 2 * k + 2])
 
@@ -404,15 +413,16 @@
         put(face, where, flow(*donors(c > 0, where, moved(where, 0, 1)), c))
 
     pipelined((NZ + 2) // 3, middle, *x_stages)
-    loop(Z0 - 1, Z0 + 2, lambda z: put_sums(z, *inner))
-
-    def y_inner(z):
-        stores = planes_of(g1_ext, 1)([(z, *inner)]), sums_of(z + 2, *inner)
+    loop(Z0 - 1, Z0 + 3, lambda z: put_sums(z, *inner))
+
+    def y_inner(i):
+        z = Z0 + 2 * i
+        stores = planes_of(g1_ext, 1)(pair(z)), sums_of(z + 3, *inner), sums_of(z + 4, *inner)
         for store in stores:
             store()
 
-    loop(Z0, Z1 - 1, y_inner)
-    put_planes(g1_ext, 1, [(Z1 - 1, *inner)])
+    loop(0, NZ // 2 - 1, y_inner)
+    put_planes(g1_ext, 1, pair(Z1 - 2))
     def faces_y_near(i):
         z = Z0 + 4 * i
         faces_y([w for k in range(4) for w in ((z + k, Y0, 1), (z + k, Y1 - 2, 1))])
@@ -448,28 +458,31 @@
         c = dt_vec[...] * rows(vz, where)
         put(face, where, flow(*donors(c > 0, where, moved(where, 1, 0)), c))
 
-    shift_rows(g2_ext, [(Z0, Y0, NY), (Z0 + 1, Y0, NY)])
-    shift_rows(g2_ext, [(Z0 + 2, Y0, NY), (Z0 + 3, Y0, NY)])
-    loop(Z0, Z0 + 3, lambda z: put_sums(z, *inner))
-
-    def z_inner(z):
+    loop(0, 2, lambda i: shift_rows(g2_ext, [(Z0 + 3 * i + k, Y0, NY) for k in range(3)]))
+    loop(Z0, Z0 + 4, lambda z: put_sums(z, *inner))
+
+    def z_inner(i):
+        z = Z0 + 1 + 2 * i
         stores = (
-            shifts_of(g2_ext)([(z + 3, Y0, NY)]),
-            planes_of(g2_ext, 0)([(z, *inner)]),
-            sums_of(z + 2, *inner),
+            shifts_of(g2_ext)([(z + 5, Y0, NY), (z + 6, Y0, NY)]),
+            planes_of(g2_ext, 0)(pair(z)),
+            sums_of(z + 3, *inner),
+            sums_of(z + 4, *inner),
         )
         for store in reversed(stores):
             store()
 
-    loop(Z0 + 1, Z1 - 3, z_inner)
+    loop(0, NZ // 2 - 3, z_inner)
+    put_sums(Z1 - 2, *inner)
     put_sums(Z1 - 1, *inner)
-    loop(Z1 - 3, Z1 - 1, lambda z: put_planes(g2_ext, 0, [(z, *inner)]))
-    loop(Z0 + 1, Z1 - 2, lambda z: faces_z([(z, *inner)]))
+    loop(0, 2, lambda i: put_planes(g2_ext, 0, pair(Z1 - 5 + 2 * i)))
+    loop(0, NZ // 2 - 2, lambda i: faces_z(pair(Z0 + 1 + 2 * i)))
+    faces_z([(Z1 - 3, *inner)])
     arrive(some(g2_ext, 8, 4), HALO_G_NEAR)
-    loop(0, 2, lambda i: shift_rows(g2_ext, [(i * Z1, Y0, NY), (i * Z1 + 1, Y0, NY)]))
-    loop(0, 4, lambda i: put_sums(i + (i // 2) * (EZ - 4), *inner))
-    loop(0, 4, lambda i: put_planes(g2_ext, 0, ends(i)))
-    loop(0, 4, lambda i: faces_z([(1 + i + (i // 2) * (NZ - 3), *inner)]))
+    shift_ends(g2_ext)
+    loop(0, 2, lambda i: put_planes(g2_ext, 0, pair(1 + i * NZ)))
+    loop(0, 2, lambda i: faces_z(pair(1 + i * (NZ - 1))))
+
     def update_z(where):
         before, q = moved(where, -1, 0), dt_vec[...]
         g = rows(g2_ext, where) - rows(face, where) + rows(face, before)
@@ -483,9 +496,9 @@
         g2_ext, [w for k in range(EZ // 2) for w in ((i * (EZ // 2) + k, Y0 - 1, 1), (i * (EZ // 2) + k, Y1, 1))]
     ))
     loop(0, EZ // 4, lambda i: sums_edge(4 * i, 4))
-    loop(0, (NZ + 2) // 3, lambda i: put_planes(g2_ext, 0, edges(1 + 3 * i, 3)))
-    loop(0, NZ // 3, lambda i: faces_z(edges(1 + 3 * i, 3)))
-    faces_z(edges(Z1 - 2, 2))
+    loop(0, (NZ + 2) // 6, lambda i: put_planes(g2_ext, 0, edges(1 + 6 * i, 6)))
+    loop(0, 2, lambda i: faces_z(edges(1 + 6 * i, 6)))
+    faces_z(edges(Z1 - 5, 5))
 
     loop(0, NZ // 4, lambda i: update_z(edges(Z0 + 4 * i, 4)))
     left(some(f_ext, 14, 8), HALO_F)

time: 39 us -> 39.3 us (level)
  no operation moved by 1% of the time
where the time goes in v8:
time: 39.3 us; the launch traced here: 39.1 us
  Pallas kernels  35.9 us (91%)
  between operations  2.33 us (6%)
  local copies, waits for them, and re-layouts  0.8 us (2%)
    pallas_call x1, Pallas kernels, shards(): pl.pallas_call(kernel, out_shape=(pltpu.VMEM((NZ, J, NY, LN), F32), jax.S...  35.9 us
    unnamed x1, local copies, waits for them, and re-layouts  0.8 us

profile of v8, /device:TPU:1, one launch (start us, length us, event | category | flops | bytes accessed | tf_op | source)
XLA Modules:
  0.0 39.1 jit_solution(10536246398590993795)
XLA Ops:
  0.6 35.9 %advect.1 = (f32[16,8,8,128]{3,2,1,0:T(8,128)S(1)}, f32[1,1]{1,0:T(1,128)}) custom-call(f32[16,8,8,128]{3,2,1,0:T(8,128)} %bitcast.17, f32[16,8,8,128]{3,2,1,0:T(8,128)} %bitcast.18, f32[16,8,8,128]{3,2,1,0:T(8,128)} %bitcast.19, f32[16,8,8,128]{3,2,1,0:T(8,128)} %bitcast.20), custom_call_target="tpu_custom_call" | custom-call | tf_op jit(solution)/shard_map/advect/pallas_call | solution.py:519
  36.6 0.8 %copy.8 = f32[16,8,1024]{2,1,0:T(8,128)} copy(f32[16,8,1024]{2,1,0:T(8,128)S(1)} %bitcast.16) | data formatting | bytes 1048576

commit v9 on v8

--- a/solution.py
+++ b/solution.py
@@ -295,8 +295,9 @@
 
     loop(0, NZ // 2, lambda i: shift_rows(f_ext, [(Z0 + 2 * i, Y0, NY), (Z0 + 2 * i + 1, Y0, NY)]))
     loop(Z0, Z1, lambda z: put_sums(z, *inner))
-    pipelined(NZ // 2 - 1, lambda i: pair(Z0 + 1 + 2 * i), planes_of(f_ext, 2), donors_x)
+    pipelined(5, lambda i: [(Z0 + 1 + i, *inner)], planes_of(f_ext, 2), donors_x)
     send(halo_v)
+    pipelined(NZ - 7, lambda i: [(Z0 + 6 + i, *inner)], planes_of(f_ext, 2), donors_x)
     arrive(some(f_ext, 8, 4), HALO_F_NEAR)
     shift_ends(f_ext)
     loop(0, 2, lambda i: put_planes(f_ext, 2, pair(1 + i * NZ)))
@@ -329,9 +330,10 @@
 
     loop(0, 2, shift_corners)
     loop(0, 4, lambda i: sums_side(i + (i // 2) * (EZ - 4)))
+    loop(0, 6, lambda i: put_planes(f_ext, 2, sides(i)))
     arrive(some(vx, 13, 4), HALO_V)
     loop(0, 2, lambda i: donors_x(pair(1 + i * NZ))())
-    pipelined(6, sides, planes_of(f_ext, 2), donors_x)
+    loop(0, 6, lambda i: donors_x(sides(i))())
     arrive(stat_z.at[pl.ds(0, N_GZ - 1)], STAT_Z)
     stats = combined(stat_z, N_GZ)
     umax = jnp.max(stats[0:1], axis=1, keepdims=True)
@@ -458,24 +460,22 @@
         c = dt_vec[...] * rows(vz, where)
         put(face, where, flow(*donors(c > 0, where, moved(where, 1, 0)), c))
 
-    loop(0, 2, lambda i: shift_rows(g2_ext, [(Z0 + 3 * i + k, Y0, NY) for k in range(3)]))
-    loop(Z0, Z0 + 4, lambda z: put_sums(z, *inner))
-
-    def z_inner(i):
-        z = Z0 + 1 + 2 * i
+    shift_rows(g2_ext, [(Z0, Y0, NY), (Z0 + 1, Y0, NY)])
+    shift_rows(g2_ext, [(Z0 + 2, Y0, NY), (Z0 + 3, Y0, NY)])
+    loop(Z0, Z0 + 3, lambda z: put_sums(z, *inner))
+
+    def z_inner(z):
         stores = (
-            shifts_of(g2_ext)([(z + 5, Y0, NY), (z + 6, Y0, NY)]),
-            planes_of(g2_ext, 0)(pair(z)),
-            sums_of(z + 3, *inner),
-            sums_of(z + 4, *inner),
+            shifts_of(g2_ext)([(z + 3, Y0, NY)]),
+            planes_of(g2_ext, 0)([(z, *inner)]),
+            sums_of(z + 2, *inner),
         )
         for store in reversed(stores):
             store()
 
-    loop(0, NZ // 2 - 3, z_inner)
-    put_sums(Z1 - 2, *inner)
+    loop(Z0 + 1, Z1 - 3, z_inner)
     put_sums(Z1 - 1, *inner)
-    loop(0, 2, lambda i: put_planes(g2_ext, 0, pair(Z1 - 5 + 2 * i)))
+    put_planes(g2_ext, 0, pair(Z1 - 3))
     loop(0, NZ // 2 - 2, lambda i: faces_z(pair(Z0 + 1 + 2 * i)))
     faces_z([(Z1 - 3, *inner)])
     arrive(some(g2_ext, 8, 4), HALO_G_NEAR)

time: 39.3 us -> 38.1 us (0.969)
  Pallas kernels: 35.9 us -> 34.8 us
    pallas_call x1, Pallas kernels: 35.9 us -> 34.8 us  [shards(): pl.pallas_call(kernel, out_shape=(pltpu.VMEM((NZ, J, NY, LN), F32), jax.S...]
where the time goes in v9:
time: 38.1 us; the launch traced here: 37.9 us
  Pallas kernels  34.8 us (91%)
  between operations  2.33 us (6%)
  local copies, waits for them, and re-layouts  0.8 us (2%)
    pallas_call x1, Pallas kernels, shards(): pl.pallas_call(kernel, out_shape=(pltpu.VMEM((NZ, J, NY, LN), F32), jax.S...  34.8 us
    unnamed x1, local copies, waits for them, and re-layouts  0.8 us

profile of v9, /device:TPU:1, one launch (start us, length us, event | category | flops | bytes accessed | tf_op | source)
XLA Modules:
  0.0 37.9 jit_solution(3553062214832720476)
XLA Ops:
  0.6 34.8 %advect.1 = (f32[16,8,8,128]{3,2,1,0:T(8,128)S(1)}, f32[1,1]{1,0:T(1,128)}) custom-call(f32[16,8,8,128]{3,2,1,0:T(8,128)} %bitcast.17, f32[16,8,8,128]{3,2,1,0:T(8,128)} %bitcast.18, f32[16,8,8,128]{3,2,1,0:T(8,128)} %bitcast.19, f32[16,8,8,128]{3,2,1,0:T(8,128)} %bitcast.20), custom_call_target="tpu_custom_call" | custom-call | tf_op jit(solution)/shard_map/advect/pallas_call | solution.py:519
  35.4 0.8 %copy.8 = f32[16,8,1024]{2,1,0:T(8,128)} copy(f32[16,8,1024]{2,1,0:T(8,128)S(1)} %bitcast.16) | data formatting | bytes 1048576

commit v10 on v9

--- a/solution.py
+++ b/solution.py
@@ -302,6 +302,9 @@
     shift_ends(f_ext)
     loop(0, 2, lambda i: put_planes(f_ext, 2, pair(1 + i * NZ)))
     arrive(some(f_ext, NZ, 4), HALO_F)
+    arrive(stat_y.at[pl.ds(0, N_GY - 1)], STAT_Y)
+    stat_z[gz] = combined(stat_y, N_GY)
+    send(stats_z)
 
     def shift_sides(i):
         z = Z0 + 4 * i
@@ -313,27 +316,31 @@
 
     loop(0, NZ // 4, shift_sides)
     loop(Z0, Z1, sums_side)
-    arrive(stat_y.at[pl.ds(0, N_GY - 1)], STAT_Y)
-    stat_z[gz] = combined(stat_y, N_GY)
-    send(stats_z)
-    send(velocity)
-    arrive(some(f_ext, 4, 4), HALO_F_FAR)
-
     def shift_corners(i):
         z = i * Z1
         shift_rows(f_ext, [(z, 0, 2), (z, Y1, 2), (z + 1, 0, 2), (z + 1, Y1, 2)])
 
+    def side(zs, high):
+        return [(z, 1 + high * (Y1 - 2), 2) for z in zs]
+
     def sides(i):
-        high = i // 3
-        z, y = 1 + 6 * (i - 3 * high), 1 + high * (Y1 - 2)
-        return [(z + k, y, 2) for k in range(6)]
-
+        high = i // 2
+        first = 3 + 6 * (i - 2 * high)
+        return side([first + k for k in range(6)], high)
+
+    def side_ends(high):
+        return side([1, 2, NZ - 1, NZ, NZ + 1, NZ + 2], high)
+
+    send(velocity)
+    loop(0, 4, lambda i: put_planes(f_ext, 2, sides(i)))
+    arrive(some(f_ext, 4, 4), HALO_F_FAR)
     loop(0, 2, shift_corners)
     loop(0, 4, lambda i: sums_side(i + (i // 2) * (EZ - 4)))
-    loop(0, 6, lambda i: put_planes(f_ext, 2, sides(i)))
+    loop(0, 2, lambda i: put_planes(f_ext, 2, side_ends(i)))
     arrive(some(vx, 13, 4), HALO_V)
     loop(0, 2, lambda i: donors_x(pair(1 + i * NZ))())
-    loop(0, 6, lambda i: donors_x(sides(i))())
+    loop(0, 2, lambda i: donors_x(side_ends(i))())
+    loop(0, 4, lambda i: donors_x(sides(i))())
     arrive(stat_z.at[pl.ds(0, N_GZ - 1)], STAT_Z)
     stats = combined(stat_z, N_GZ)
     umax = jnp.max(stats[0:1], axis=1, keepdims=True)
@@ -488,7 +495,7 @@
         g = rows(g2_ext, where) - rows(face, where) + rows(face, before)
         g = g / (1.0 - q * (rows(vz, where) - rows(vz, before)))
         for k, (z, y) in enumerate([(z, y + k) for z, y, n in where for k in range(n)]):
-            out_ref[z - Z0, :, y - Y0, :] = g[k]
+            out_ref[z - Z0, pl.ds(y - Y0, J, stride=NY), :] = g[k]
 
     loop(Z0, Z1, lambda z: update_z([(z, *inner)]))
     arrive(some(g2_ext, 10, 4), HALO_G)
@@ -518,7 +525,7 @@
     anywhere = pl.BlockSpec(memory_space=pl.ANY)
     field, step = pl.pallas_call(
         kernel,
-        out_shape=(pltpu.VMEM((NZ, J, NY, LN), F32), jax.ShapeDtypeStruct((1, 1), F32)),
+        out_shape=(pltpu.VMEM((NZ, J * NY, LN), F32), jax.ShapeDtypeStruct((1, 1), F32)),
         in_specs=[anywhere] * 4,
         out_specs=(pl.BlockSpec(memory_space=pltpu.VMEM), anywhere),
         scratch_shapes=[ext] * 18 + [
@@ -531,7 +538,7 @@
         compiler_params=pltpu.CompilerParams(collective_id=0, has_side_effects=True),
         name="advect",
     )(*tiled)
-    return field.transpose(0, 2, 1, 3).reshape(NZ, NY, J * LN), step.reshape(())
+    return field.reshape(NZ, J, NY, LN).transpose(0, 2, 1, 3).reshape(NZ, NY, J * LN), step.reshape(())
 
 
 def solution(mesh):

time: 38.1 us -> 38.1 us (level)
  no operation moved by 1% of the time
where the time goes in v10:
time: 38.1 us; the launch traced here: 37.9 us
  Pallas kernels  34.7 us (91%)
  between operations  2.33 us (6%)
  local copies, waits for them, and re-layouts  0.8 us (2%)
    pallas_call x1, Pallas kernels, shards(): pl.pallas_call(kernel, out_shape=(pltpu.VMEM((NZ, J * NY, LN), F32), jax....  34.7 us
    unnamed x1, local copies, waits for them, and re-layouts  0.8 us

profile of v10, /device:TPU:1, one launch (start us, length us, event | category | flops | bytes accessed | tf_op | source)
XLA Modules:
  0.0 37.9 jit_solution(8021738838509967144)
XLA Ops:
  0.6 34.7 %advect.1 = (f32[16,64,128]{2,1,0:T(8,128)S(1)}, f32[1,1]{1,0:T(1,128)}) custom-call(f32[16,8,8,128]{3,2,1,0:T(8,128)} %bitcast.19, f32[16,8,8,128]{3,2,1,0:T(8,128)} %bitcast.20, f32[16,8,8,128]{3,2,1,0:T(8,128)} %bitcast.21, f32[16,8,8,128]{3,2,1,0:T(8,128)} %bitcast.22), custom_call_target="tpu_custom_call" | custom-call | tf_op jit(solution)/shard_map/advect/pallas_call | solution.py:526
  35.4 0.8 %copy.8 = f32[16,8,1024]{2,1,0:T(8,128)} copy(f32[16,8,1024]{2,1,0:T(8,128)S(1)} %bitcast.18) | data formatting | bytes 1048576

commit v11 on v10

--- a/solution.py
+++ b/solution.py
@@ -125,7 +125,7 @@
 def kernel(
     f_hbm, vx_hbm, vy_hbm, vz_hbm, out_ref, dt_out,
     f_ext, g1_ext, g2_ext, vx, vy, vz, vx_diff, smooth, diff, sum_y, dif_y, sum_d,
-    off, lo, hi, slope, scale, face, edge_y, stat_y, stat_z, dt_vec, dt_cell,
+    off, lo, hi, slope, scale, face, edge_y, stat_y, stat_z, speeds, dt_vec, dt_cell,
     load_sem, out_sem, send_sem, recv_sem,
 ):
     gy, gz = lax.axis_index("gy"), lax.axis_index("gz")
@@ -144,13 +144,16 @@
             pltpu.make_async_copy(source.at[:, :, y, :], target.at[own_z, Y0 + y], load_sem.at[k]).start()
 
     load(0)
+    whole = [
+        pltpu.make_async_copy(arrays[k + 1][0], speeds.at[k], load_sem.at[4 + k]) for k in range(3)
+    ]
+    for copy in whole:
+        copy.start()
     barrier = pltpu.get_barrier_semaphore()
     greeted = [neighbour(k, 0) for k in range(1, N_GY)]
     greeted += [neighbour(0, k) for k in range(1, N_GZ)] + [neighbour(*c) for c in corners]
     for device in greeted:
         pl.semaphore_signal(barrier, inc=1, device_id=device, device_id_type=pl.DeviceIdType.MESH)
-    for k in (1, 2, 3):
-        load(k)
 
     def remote(source, target, sends, receives, device):
         return pltpu.make_async_remote_copy(
@@ -192,10 +195,9 @@
     loaded(0)
     total = lax.fori_loop(0, NZ, scan_fraction, jnp.zeros((NY, J, LN), F32))
     peak = jnp.zeros((NY, J, LN), F32)
-    for k in (1, 2, 3):
-        loaded(k)
-        speeds = arrays[k][1]
-        peak = lax.fori_loop(0, NZ, lambda i, peak: jnp.maximum(peak, jnp.abs(speeds[i + Z0, own_y])), peak)
+    for k in range(3):
+        whole[k].wait()
+        peak = lax.fori_loop(0, NZ, lambda z, peak: jnp.maximum(peak, jnp.abs(speeds[k, z])), peak)
     top_row = lax.broadcasted_iota(jnp.int32, (2, LN), 0) == 0
 
     def combined(ref, n):
@@ -218,6 +220,8 @@
     ]
     send(stats_y)
     send(halo_f[2:4] + halo_f[:2] + halo_f[4:])
+    for k in (1, 2, 3):
+        load(k)
 
     def put_shifts(g, where):
         before, after = at_prev(g), at_next(g)
@@ -295,6 +299,7 @@
 
     loop(0, NZ // 2, lambda i: shift_rows(f_ext, [(Z0 + 2 * i, Y0, NY), (Z0 + 2 * i + 1, Y0, NY)]))
     loop(Z0, Z1, lambda z: put_sums(z, *inner))
+    loaded(1)
     pipelined(5, lambda i: [(Z0 + 1 + i, *inner)], planes_of(f_ext, 2), donors_x)
     send(halo_v)
     pipelined(NZ - 7, lambda i: [(Z0 + 6 + i, *inner)], planes_of(f_ext, 2), donors_x)
@@ -331,6 +336,8 @@
     def side_ends(high):
         return side([1, 2, NZ - 1, NZ, NZ + 1, NZ + 2], high)
 
+    loaded(2)
+    loaded(3)
     send(velocity)
     loop(0, 4, lambda i: put_planes(f_ext, 2, sides(i)))
     arrive(some(f_ext, 4, 4), HALO_F_FAR)
@@ -422,16 +429,20 @@
         put(face, where, flow(*donors(c > 0, where, moved(where, 0, 1)), c))
 
     pipelined((NZ + 2) // 3, middle, *x_stages)
-    loop(Z0 - 1, Z0 + 3, lambda z: put_sums(z, *inner))
-
-    def y_inner(i):
-        z = Z0 + 2 * i
-        stores = planes_of(g1_ext, 1)(pair(z)), sums_of(z + 3, *inner), sums_of(z + 4, *inner)
-        for store in stores:
+    def y_sums(i):
+        for store in [sums_of(Z0 - 1 + 3 * i + k, *inner) for k in range(3)]:
             store()
 
-    loop(0, NZ // 2 - 1, y_inner)
-    put_planes(g1_ext, 1, pair(Z1 - 2))
+    def y_near(i):
+        z = Z0 + 8 * i
+        put_planes(g1_ext, 1, [w for k in range(8) for w in ((z + k, Y0 + 1, 1), (z + k, Y1 - 2, 1))])
+
+    def y_middle(i):
+        put_planes(g1_ext, 1, [(Z0 + 4 * i + k, Y0 + 2, NY - 4) for k in range(4)])
+
+    loop(0, (NZ + 2) // 3, y_sums)
+    loop(0, 2, y_near)
+    loop(0, 2, lambda i: y_middle(3 * i))
     def faces_y_near(i):
         z = Z0 + 4 * i
         faces_y([w for k in range(4) for w in ((z + k, Y0, 1), (z + k, Y1 - 2, 1))])
@@ -461,6 +472,7 @@
     send(halo_g[:2] + halo_g[4:])
     loop(0, 2, rest_y)
     send(halo_g[2:4])
+    loop(1, 3, y_middle)
     loop(2, NZ // 2, rest_y)
 
     def faces_z(where):
@@ -531,8 +543,9 @@
         scratch_shapes=[ext] * 18 + [
             pltpu.VMEM((4, NZ, *row), F32),
             pltpu.VMEM((N_GY, 2, LN), F32), pltpu.VMEM((N_GZ, 2, LN), F32),
+            pltpu.VMEM((3, NZ, J, NY, LN), F32),
             pltpu.VMEM(row, F32), pltpu.VMEM((1, 1), F32),
-            pltpu.SemaphoreType.DMA((4,)), pltpu.SemaphoreType.DMA(()),
+            pltpu.SemaphoreType.DMA((7,)), pltpu.SemaphoreType.DMA(()),
             pltpu.SemaphoreType.DMA((N_SEND,)), pltpu.SemaphoreType.DMA((N_RECV,)),
         ],
         compiler_params=pltpu.CompilerParams(collective_id=0, has_side_effects=True),

time: 38.1 us -> 38.2 us (level)
  no operation moved by 1% of the time
where the time goes in v11:
time: 38.2 us; the launch traced here: 37.9 us
  Pallas kernels  34.8 us (91%)
  between operations  2.33 us (6%)
  local copies, waits for them, and re-layouts  0.8 us (2%)
    pallas_call x1, Pallas kernels, shards(): pl.pallas_call(kernel, out_shape=(pltpu.VMEM((NZ, J * NY, LN), F32), jax....  34.8 us
    unnamed x1, local copies, waits for them, and re-layouts  0.8 us

profile of v11, /device:TPU:1, one launch (start us, length us, event | category | flops | bytes accessed | tf_op | source)
XLA Modules:
  0.0 37.9 jit_solution(8759730101828248654)
XLA Ops:
  0.6 34.8 %advect.1 = (f32[16,64,128]{2,1,0:T(8,128)S(1)}, f32[1,1]{1,0:T(1,128)}) custom-call(f32[16,8,8,128]{3,2,1,0:T(8,128)} %bitcast.19, f32[16,8,8,128]{3,2,1,0:T(8,128)} %bitcast.20, f32[16,8,8,128]{3,2,1,0:T(8,128)} %bitcast.21, f32[16,8,8,128]{3,2,1,0:T(8,128)} %bitcast.22), custom_call_target="tpu_custom_call" | custom-call | tf_op jit(solution)/shard_map/advect/pallas_call | solution.py:538
  35.4 0.8 %copy.8 = f32[16,8,1024]{2,1,0:T(8,128)} copy(f32[16,8,1024]{2,1,0:T(8,128)S(1)} %bitcast.18) | data formatting | bytes 1048576

commit v12 on v10

--- a/solution.py
+++ b/solution.py
@@ -301,6 +301,7 @@
     arrive(some(f_ext, 8, 4), HALO_F_NEAR)
     shift_ends(f_ext)
     loop(0, 2, lambda i: put_planes(f_ext, 2, pair(1 + i * NZ)))
+    donors_x([(Z0, *inner), (Z1 - 1, *inner)])()
     arrive(some(f_ext, NZ, 4), HALO_F)
     arrive(stat_y.at[pl.ds(0, N_GY - 1)], STAT_Y)
     stat_z[gz] = combined(stat_y, N_GY)
@@ -320,27 +321,30 @@
         z = i * Z1
         shift_rows(f_ext, [(z, 0, 2), (z, Y1, 2), (z + 1, 0, 2), (z + 1, Y1, 2)])
 
-    def side(zs, high):
-        return [(z, 1 + high * (Y1 - 2), 2) for z in zs]
-
-    def sides(i):
-        high = i // 2
-        first = 3 + 6 * (i - 2 * high)
-        return side([first + k for k in range(6)], high)
-
-    def side_ends(high):
-        return side([1, 2, NZ - 1, NZ, NZ + 1, NZ + 2], high)
-
+    def column(zs, y):
+        return [(z, y, 1) for z in zs]
+
+    def own_columns(i):
+        first, high = 3 + 6 * (i - 2 * (i // 2)), i // 2
+        return column([first + k for k in range(6)], Y0 + high * (NY - 1))
+
+    def next_columns(i):
+        first, high = 3 + 6 * (i - 2 * (i // 2)), i // 2
+        return column([first + k for k in range(6)], Y0 - 1 + high * (NY + 1))
+
+    def end_columns(i):
+        return column([1, 2, NZ - 1, NZ, NZ + 1, NZ + 2], 1 + i + (i // 2) * (NY - 2))
+
+    planes_x = planes_of(f_ext, 2)
     send(velocity)
-    loop(0, 4, lambda i: put_planes(f_ext, 2, sides(i)))
+    pipelined(4, own_columns, planes_x, donors_x)
+    arrive(some(vx, 13, 4), HALO_V)
+    pipelined(4, next_columns, planes_x, donors_x)
     arrive(some(f_ext, 4, 4), HALO_F_FAR)
     loop(0, 2, shift_corners)
     loop(0, 4, lambda i: sums_side(i + (i // 2) * (EZ - 4)))
-    loop(0, 2, lambda i: put_planes(f_ext, 2, side_ends(i)))
-    arrive(some(vx, 13, 4), HALO_V)
-    loop(0, 2, lambda i: donors_x(pair(1 + i * NZ))())
-    loop(0, 2, lambda i: donors_x(side_ends(i))())
-    loop(0, 4, lambda i: donors_x(sides(i))())
+    pipelined(4, end_columns, planes_x, donors_x)
+    donors_x([(1, *inner), (NZ + 2, *inner)])()
     arrive(stat_z.at[pl.ds(0, N_GZ - 1)], STAT_Z)
     stats = combined(stat_z, N_GZ)
     umax = jnp.max(stats[0:1], axis=1, keepdims=True)

time: 38.1 us -> 38.1 us (level)
  no operation moved by 1% of the time
where the time goes in v12:
time: 38.1 us; the launch traced here: 37.9 us
  Pallas kernels  34.7 us (91%)
  between operations  2.33 us (6%)
  local copies, waits for them, and re-layouts  0.8 us (2%)
    pallas_call x1, Pallas kernels, shards(): pl.pallas_call(kernel, out_shape=(pltpu.VMEM((NZ, J * NY, LN), F32), jax....  34.7 us
    unnamed x1, local copies, waits for them, and re-layouts  0.8 us

profile of v12, /device:TPU:1, one launch (start us, length us, event | category | flops | bytes accessed | tf_op | source)
XLA Modules:
  0.0 37.9 jit_solution(8701636868142914132)
XLA Ops:
  0.6 34.7 %advect.1 = (f32[16,64,128]{2,1,0:T(8,128)S(1)}, f32[1,1]{1,0:T(1,128)}) custom-call(f32[16,8,8,128]{3,2,1,0:T(8,128)} %bitcast.19, f32[16,8,8,128]{3,2,1,0:T(8,128)} %bitcast.20, f32[16,8,8,128]{3,2,1,0:T(8,128)} %bitcast.21, f32[16,8,8,128]{3,2,1,0:T(8,128)} %bitcast.22), custom_call_target="tpu_custom_call" | custom-call | tf_op jit(solution)/shard_map/advect/pallas_call | solution.py:530
  35.4 0.8 %copy.8 = f32[16,8,1024]{2,1,0:T(8,128)} copy(f32[16,8,1024]{2,1,0:T(8,128)S(1)} %bitcast.18) | data formatting | bytes 1048576

commit v13 on v12

--- a/solution.py
+++ b/solution.py
@@ -328,22 +328,23 @@
         first, high = 3 + 6 * (i - 2 * (i // 2)), i // 2
         return column([first + k for k in range(6)], Y0 + high * (NY - 1))
 
-    def next_columns(i):
-        first, high = 3 + 6 * (i - 2 * (i // 2)), i // 2
-        return column([first + k for k in range(6)], Y0 - 1 + high * (NY + 1))
-
-    def end_columns(i):
-        return column([1, 2, NZ - 1, NZ, NZ + 1, NZ + 2], 1 + i + (i // 2) * (NY - 2))
+    def next_column(high):
+        return column([Z0 + 1 + k for k in range(12)], Y0 - 1 + high * (NY + 1))
+
+    def end_columns(high):
+        return [(z, 1 + high * (Y1 - 2), 2) for z in (1, 2, NZ - 1, NZ, NZ + 1, NZ + 2)]
 
     planes_x = planes_of(f_ext, 2)
     send(velocity)
     pipelined(4, own_columns, planes_x, donors_x)
-    arrive(some(vx, 13, 4), HALO_V)
-    pipelined(4, next_columns, planes_x, donors_x)
+    loop(0, 2, lambda i: put_planes(f_ext, 2, next_column(i)))
     arrive(some(f_ext, 4, 4), HALO_F_FAR)
     loop(0, 2, shift_corners)
     loop(0, 4, lambda i: sums_side(i + (i // 2) * (EZ - 4)))
-    pipelined(4, end_columns, planes_x, donors_x)
+    loop(0, 2, lambda i: put_planes(f_ext, 2, end_columns(i)))
+    arrive(some(vx, 13, 4), HALO_V)
+    loop(0, 2, lambda i: donors_x(next_column(i))())
+    loop(0, 2, lambda i: donors_x(end_columns(i))())
     donors_x([(1, *inner), (NZ + 2, *inner)])()
     arrive(stat_z.at[pl.ds(0, N_GZ - 1)], STAT_Z)
     stats = combined(stat_z, N_GZ)

time: 38.1 us -> 38.1 us (level)
  no operation moved by 1% of the time
where the time goes in v13:
time: 38.1 us; the launch traced here: 37.9 us
  Pallas kernels  34.7 us (91%)
  between operations  2.33 us (6%)
  local copies, waits for them, and re-layouts  0.8 us (2%)
    pallas_call x1, Pallas kernels, shards(): pl.pallas_call(kernel, out_shape=(pltpu.VMEM((NZ, J * NY, LN), F32), jax....  34.7 us
    unnamed x1, local copies, waits for them, and re-layouts  0.8 us

profile of v13, /device:TPU:1, one launch (start us, length us, event | category | flops | bytes accessed | tf_op | source)
XLA Modules:
  0.0 37.9 jit_solution(9835647648049468690)
XLA Ops:
  0.6 34.7 %advect.1 = (f32[16,64,128]{2,1,0:T(8,128)S(1)}, f32[1,1]{1,0:T(1,128)}) custom-call(f32[16,8,8,128]{3,2,1,0:T(8,128)} %bitcast.19, f32[16,8,8,128]{3,2,1,0:T(8,128)} %bitcast.20, f32[16,8,8,128]{3,2,1,0:T(8,128)} %bitcast.21, f32[16,8,8,128]{3,2,1,0:T(8,128)} %bitcast.22), custom_call_target="tpu_custom_call" | custom-call | tf_op jit(solution)/shard_map/advect/pallas_call | solution.py:531
  35.4 0.8 %copy.8 = f32[16,8,1024]{2,1,0:T(8,128)} copy(f32[16,8,1024]{2,1,0:T(8,128)S(1)} %bitcast.18) | data formatting | bytes 1048576

commit v14 on v13

--- a/solution.py
+++ b/solution.py
@@ -298,6 +298,7 @@
     pipelined(5, lambda i: [(Z0 + 1 + i, *inner)], planes_of(f_ext, 2), donors_x)
     send(halo_v)
     pipelined(NZ - 7, lambda i: [(Z0 + 6 + i, *inner)], planes_of(f_ext, 2), donors_x)
+    send(velocity)
     arrive(some(f_ext, 8, 4), HALO_F_NEAR)
     shift_ends(f_ext)
     loop(0, 2, lambda i: put_planes(f_ext, 2, pair(1 + i * NZ)))
@@ -335,7 +336,6 @@
         return [(z, 1 + high * (Y1 - 2), 2) for z in (1, 2, NZ - 1, NZ, NZ + 1, NZ + 2)]
 
     planes_x = planes_of(f_ext, 2)
-    send(velocity)
     pipelined(4, own_columns, planes_x, donors_x)
     loop(0, 2, lambda i: put_planes(f_ext, 2, next_column(i)))
     arrive(some(f_ext, 4, 4), HALO_F_FAR)
@@ -412,10 +412,11 @@
             remote(edge_y.at[0, part], edge_y.at[2, part], FLUX, FLUX, neighbour(1, 0)),
             remote(edge_y.at[1, part], edge_y.at[3, part], FLUX, FLUX, neighbour(-1, 0)),
         ]
-    arrive(some(vy, 6, 4), VEL)
     loop(0, (NZ + 2) // 3, lambda i: sums_edge(Z0 - 1 + 3 * i, 3))
     for k in range(2):
         put_planes(g1_ext, 1, edges(Z0 + k * (NZ // 2), NZ // 2))
+    arrive(some(vy, 6, 4), VEL)
+    for k in range(2):
         loop(2 * k, 2 * k + 2, half_faces_y)
         send(flux_y[2 * k : 2 * k + 2])
 

time: 38.1 us -> 37.3 us (0.979); the launches traced: 37.9 us -> 36.7 us
  Pallas kernels: 34.7 us -> 33.5 us
    pallas_call x1, Pallas kernels: 34.7 us -> 33.5 us  [shards(): pl.pallas_call(kernel, out_shape=(pltpu.VMEM((NZ, J * NY, LN), F32), jax....]
where the time goes in v14:
time: 37.3 us; the launch traced here: 36.7 us
  Pallas kernels  33.5 us (90%)
  between operations  2.33 us (6%)
  local copies, waits for them, and re-layouts  0.8 us (2%)
    pallas_call x1, Pallas kernels, shards(): pl.pallas_call(kernel, out_shape=(pltpu.VMEM((NZ, J * NY, LN), F32), jax....  33.5 us
    unnamed x1, local copies, waits for them, and re-layouts  0.8 us

profile of v14, /device:TPU:1, one launch (start us, length us, event | category | flops | bytes accessed | tf_op | source)
XLA Modules:
  0.0 36.7 jit_solution(10927414822872548177)
XLA Ops:
  0.6 33.5 %advect.1 = (f32[16,64,128]{2,1,0:T(8,128)S(1)}, f32[1,1]{1,0:T(1,128)}) custom-call(f32[16,8,8,128]{3,2,1,0:T(8,128)} %bitcast.19, f32[16,8,8,128]{3,2,1,0:T(8,128)} %bitcast.20, f32[16,8,8,128]{3,2,1,0:T(8,128)} %bitcast.21, f32[16,8,8,128]{3,2,1,0:T(8,128)} %bitcast.22), custom_call_target="tpu_custom_call" | custom-call | tf_op jit(solution)/shard_map/advect/pallas_call | solution.py:532
  34.2 0.8 %copy.8 = f32[16,8,1024]{2,1,0:T(8,128)} copy(f32[16,8,1024]{2,1,0:T(8,128)S(1)} %bitcast.18) | data formatting | bytes 1048576

commit v15 on v14

--- a/solution.py
+++ b/solution.py
@@ -415,8 +415,8 @@
     loop(0, (NZ + 2) // 3, lambda i: sums_edge(Z0 - 1 + 3 * i, 3))
     for k in range(2):
         put_planes(g1_ext, 1, edges(Z0 + k * (NZ // 2), NZ // 2))
-    arrive(some(vy, 6, 4), VEL)
-    for k in range(2):
+        if k == 0:
+            arrive(some(vy, 6, 4), VEL)
         loop(2 * k, 2 * k + 2, half_faces_y)
         send(flux_y[2 * k : 2 * k + 2])
 
@@ -462,12 +462,13 @@
     near = [HALO_G, HALO_G, HALO_G_NEAR, HALO_G_NEAR] + 4 * [HALO_G]
     halo_g = halo(g2_ext, HALO_G, near, 2, 1)
     loop(0, NZ // 4, faces_y_near)
+    loop(NZ // 2 - 3, NZ // 2, rest_y)
     arrive(edge_y.at[pl.ds(2, 2)], FLUX)
     loop(0, NZ // 4, update_y_edge)
     send(halo_g[:2] + halo_g[4:])
     loop(0, 2, rest_y)
     send(halo_g[2:4])
-    loop(2, NZ // 2, rest_y)
+    loop(2, NZ // 2 - 3, rest_y)
 
     def faces_z(where):
         c = dt_vec[...] * rows(vz, where)

time: 37.3 us -> 37.2 us (level); the launches traced: 36.7 us -> 37 us
  no operation moved by 1% of the time
where the time goes in v15:
time: 37.2 us; the launch traced here: 37 us
  Pallas kernels  33.8 us (91%)
  between operations  2.33 us (6%)
  local copies, waits for them, and re-layouts  0.8 us (2%)
    pallas_call x1, Pallas kernels, shards(): pl.pallas_call(kernel, out_shape=(pltpu.VMEM((NZ, J * NY, LN), F32), jax....  33.8 us
    unnamed x1, local copies, waits for them, and re-layouts  0.8 us

profile of v15, /device:TPU:1, one launch (start us, length us, event | category | flops | bytes accessed | tf_op | source)
XLA Modules:
  0.0 37.0 jit_solution(15891754259193655911)
XLA Ops:
  0.6 33.8 %advect.1 = (f32[16,64,128]{2,1,0:T(8,128)S(1)}, f32[1,1]{1,0:T(1,128)}) custom-call(f32[16,8,8,128]{3,2,1,0:T(8,128)} %bitcast.19, f32[16,8,8,128]{3,2,1,0:T(8,128)} %bitcast.20, f32[16,8,8,128]{3,2,1,0:T(8,128)} %bitcast.21, f32[16,8,8,128]{3,2,1,0:T(8,128)} %bitcast.22), custom_call_target="tpu_custom_call" | custom-call | tf_op jit(solution)/shard_map/advect/pallas_call | solution.py:533
  34.5 0.8 %copy.8 = f32[16,8,1024]{2,1,0:T(8,128)} copy(f32[16,8,1024]{2,1,0:T(8,128)S(1)} %bitcast.18) | data formatting | bytes 1048576

commit v16 on v14

--- a/solution.py
+++ b/solution.py
@@ -303,10 +303,10 @@
     shift_ends(f_ext)
     loop(0, 2, lambda i: put_planes(f_ext, 2, pair(1 + i * NZ)))
     donors_x([(Z0, *inner), (Z1 - 1, *inner)])()
-    arrive(some(f_ext, NZ, 4), HALO_F)
     arrive(stat_y.at[pl.ds(0, N_GY - 1)], STAT_Y)
     stat_z[gz] = combined(stat_y, N_GY)
     send(stats_z)
+    arrive(some(f_ext, NZ, 4), HALO_F)
 
     def shift_sides(i):
         z = Z0 + 4 * i

time: 37.3 us -> 37.2 us (level)
  no operation moved by 1% of the time
where the time goes in v16:
time: 37.2 us; the launch traced here: 36.6 us
  Pallas kernels  33.4 us (90%)
  between operations  2.33 us (6%)
  local copies, waits for them, and re-layouts  0.8 us (2%)
    pallas_call x1, Pallas kernels, shards(): pl.pallas_call(kernel, out_shape=(pltpu.VMEM((NZ, J * NY, LN), F32), jax....  33.4 us
    unnamed x1, local copies, waits for them, and re-layouts  0.8 us

profile of v16, /device:TPU:1, one launch (start us, length us, event | category | flops | bytes accessed | tf_op | source)
XLA Modules:
  0.0 36.6 jit_solution(18420685095645018910)
XLA Ops:
  0.6 33.4 %advect.1 = (f32[16,64,128]{2,1,0:T(8,128)S(1)}, f32[1,1]{1,0:T(1,128)}) custom-call(f32[16,8,8,128]{3,2,1,0:T(8,128)} %bitcast.19, f32[16,8,8,128]{3,2,1,0:T(8,128)} %bitcast.20, f32[16,8,8,128]{3,2,1,0:T(8,128)} %bitcast.21, f32[16,8,8,128]{3,2,1,0:T(8,128)} %bitcast.22), custom_call_target="tpu_custom_call" | custom-call | tf_op jit(solution)/shard_map/advect/pallas_call | solution.py:532
  34.1 0.8 %copy.8 = f32[16,8,1024]{2,1,0:T(8,128)} copy(f32[16,8,1024]{2,1,0:T(8,128)S(1)} %bitcast.18) | data formatting | bytes 1048576

commit v17 on v15

--- a/solution.py
+++ b/solution.py
@@ -462,13 +462,12 @@
     near = [HALO_G, HALO_G, HALO_G_NEAR, HALO_G_NEAR] + 4 * [HALO_G]
     halo_g = halo(g2_ext, HALO_G, near, 2, 1)
     loop(0, NZ // 4, faces_y_near)
-    loop(NZ // 2 - 3, NZ // 2, rest_y)
     arrive(edge_y.at[pl.ds(2, 2)], FLUX)
     loop(0, NZ // 4, update_y_edge)
     send(halo_g[:2] + halo_g[4:])
     loop(0, 2, rest_y)
     send(halo_g[2:4])
-    loop(2, NZ // 2 - 3, rest_y)
+    loop(2, NZ // 2, rest_y)
 
     def faces_z(where):
         c = dt_vec[...] * rows(vz, where)

time: 37.2 us -> 37.1 us (level)
  no operation moved by 1% of the time
where the time goes in v17:
time: 37.1 us; the launch traced here: 36.7 us
  Pallas kernels  33.5 us (90%)
  between operations  2.33 us (6%)
  local copies, waits for them, and re-layouts  0.8 us (2%)
    pallas_call x1, Pallas kernels, shards(): pl.pallas_call(kernel, out_shape=(pltpu.VMEM((NZ, J * NY, LN), F32), jax....  33.5 us
    unnamed x1, local copies, waits for them, and re-layouts  0.8 us

profile of v17, /device:TPU:1, one launch (start us, length us, event | category | flops | bytes accessed | tf_op | source)
XLA Modules:
  0.0 36.7 jit_solution(12875212246554115496)
XLA Ops:
  0.6 33.5 %advect.1 = (f32[16,64,128]{2,1,0:T(8,128)S(1)}, f32[1,1]{1,0:T(1,128)}) custom-call(f32[16,8,8,128]{3,2,1,0:T(8,128)} %bitcast.19, f32[16,8,8,128]{3,2,1,0:T(8,128)} %bitcast.20, f32[16,8,8,128]{3,2,1,0:T(8,128)} %bitcast.21, f32[16,8,8,128]{3,2,1,0:T(8,128)} %bitcast.22), custom_call_target="tpu_custom_call" | custom-call | tf_op jit(solution)/shard_map/advect/pallas_call | solution.py:532
  34.2 0.8 %copy.8 = f32[16,8,1024]{2,1,0:T(8,128)} copy(f32[16,8,1024]{2,1,0:T(8,128)S(1)} %bitcast.18) | data formatting | bytes 1048576
